TPU v7x, 512 devices: a whole 4x8x8 slice. The times are simulated.
512 devices in a mesh: pair: 64 (over z, y), split: 8 (over x, core).
Axes of the slice: x: 4, y: 8, z: 8, core: 2. Of those that a mesh axis runs over, the one named last changes fastest.
Arguments:
- descriptors: bfloat16 [64, 1024, 256], P('pair', 'split'), as said below
- points: bfloat16 [64, 3, 1024], P('pair', None, 'split'), may hold values from -6 to 6
- normals: bfloat16 [64, 3, 1024], P('pair', None, 'split'), may hold values from -6 to 6
- pair_list: int32 [1536, 2], replicated, may hold values from 0 to 63, as said below
- intersection: int32 [1536], P('pair'), may hold values from 256 to 1024
- pose_index: int32 [64], replicated, may hold values from 0 to 63, each once
Outputs:
- pair_cross: float32 [1536, 6, 6], P('pair')
- pose_hessian: float32 [64, 6, 6], P('pair')
- pose_gradient: float32 [64, 6], P('pair')
Inputs may be any that keep to these rules, and one draw needn't show every extreme that they name: `descriptors`: values stay within -24 to 24. `pair_list`: task k's source scan is scan k // 24. The owner of a scan s is s; a task's target has another owner than its source. Among the 24 tasks of one aligned block (tasks k // 24 alike), no owner holds the targets of more than 1 of them, and some owner holds exactly 1.
All inputs are finite; a program needn't handle non-finite values.
Results may differ from a plain program's by a relative error of at most 0.0003.
Values may be sent and summed in bfloat16 or wider, within the bound.
No kernel may reach another device: no remote copies, remote signals or barrier semaphores. Data moves between devices by JAX's collectives and lax.ppermute only.
A program may use at most 64 MiB of HBM per device.

v0:
```python
import jax
import jax.numpy as jnp
from jax import lax
from jax.sharding import PartitionSpec as P

task_group = 4


def rows_first(arrays, axis, dims):
    turned = [jnp.moveaxis(a, dim, 0) for a, dim in zip(arrays, dims)]
    both = jnp.concatenate([t.reshape(len(t), -1) for t in turned], axis=1)
    out, at, gathered = (lax.all_gather(both, axis, axis=0, tiled=True), 0, [])
    for t, dim in zip(turned, dims):
        share = out[:, at : at + t[0].size].reshape(-1, *t.shape[1:])
        gathered.append(jnp.moveaxis(share, 0, dim))
        at += t[0].size
    return tuple(gathered)


def sent_together(arrays, axis, split_dim, concat_dim, along):
    ends, at = ([], 0)
    for a in arrays[:-1]:
        at += a.shape[along]
        ends.append(at)
    both = jnp.concatenate(arrays, axis=along)
    return tuple(
        jnp.split(
            lax.all_to_all(both, axis, split_axis=split_dim, concat_axis=concat_dim, tiled=True),
            ends,
            axis=along,
        )
    )


def copy_for_each(shard, axis):
    copies = jnp.broadcast_to(shard, (lax.axis_size(axis), *shard.shape))
    return lax.all_to_all(copies, axis, split_axis=0, concat_axis=0, tiled=True)


def of_everyone(shard, axis):
    everything = copy_for_each(shard, axis)
    return jnp.sum(everything, axis=0)


def in_one(arrays, axis):
    ends = [0]
    for a in arrays:
        ends.append(ends[-1] + a.size)
    total = of_everyone(jnp.concatenate([a.ravel() for a in arrays]), axis)
    return tuple((total[b:e].reshape(a.shape) for a, b, e in zip(arrays, ends, ends[1:])))


def in_blocks(shard, dim, size):
    before, after = (shard.shape[:dim], shard.shape[dim + 1 :])
    return jnp.moveaxis(shard.reshape(*before, size, -1, *after), dim, 0)


def sent_and_summed(shard, axis, dim):
    pieces = in_blocks(shard, dim, lax.axis_size(axis))
    arrived = lax.all_to_all(pieces, axis, split_axis=0, concat_axis=0, tiled=True)
    return arrived.sum(axis=0)


def side_by_side(arrays, axis, dim, along):
    both = jnp.concatenate(arrays, axis=along)
    out, at, gathered = (sent_and_summed(both, axis, dim), 0, [])
    for a in arrays:
        gathered.append(lax.slice_in_dim(out, at, at + a.shape[along], axis=along))
        at += a.shape[along]
    return tuple(gathered)


def cross_second(left_vec, right_vec):
    return jnp.stack(
        [
            left_vec[:, 1] * right_vec[:, 2] - left_vec[:, 2] * right_vec[:, 1],
            left_vec[:, 2] * right_vec[:, 0] - left_vec[:, 0] * right_vec[:, 2],
            left_vec[:, 0] * right_vec[:, 1] - left_vec[:, 1] * right_vec[:, 0],
        ],
        axis=1,
    )


def assemble(softened, source, row_seen, counts, all_rows):
    highest = lax.Precision.HIGHEST
    matched = softened[:, :3]
    normal = softened[:, 3:]
    weight = (row_seen[None, :] < counts[:, None]).astype(jnp.float32)
    jacobian = jnp.concatenate(
        [cross_second(source, normal), normal, -cross_second(matched, normal), -normal], axis=1
    )
    residual = jnp.sum(normal * (source - matched), axis=1)
    weighted = jacobian * weight[:, None, :]
    hessian = jnp.einsum("tan,tbn->tab", weighted, jacobian, precision=highest) / all_rows
    gradient = jnp.einsum("tan,tn->ta", weighted, residual, precision=highest) / all_rows
    return (hessian, gradient)


def per_device(descriptors, points, normals, pair_list, intersection, pose_index):
    highest = lax.Precision.HIGHEST
    scan_dev, block_rows, feature_width = descriptors.shape
    split_count = lax.axis_size("split")
    own_index = lax.axis_index("pair")
    all_rows = block_rows * split_count
    task_count = intersection.shape[0]
    my_pairs = lax.dynamic_slice_in_dim(pair_list, own_index * task_count, task_count, 0)
    sources = my_pairs[:, 0] - own_index * scan_dev
    targets = my_pairs[:, 1]
    geometry = jnp.concatenate([points, normals], axis=1)
    source_desc, source_points = rows_first((descriptors, points), "split", (1, 2))
    target_desc, target_geometry = (
        lax.all_gather(descriptors, "pair", axis=0, tiled=True),
        lax.all_gather(geometry, "pair", axis=0, tiled=True),
    )
    score_scale = feature_width ** (-0.5)
    group_count = task_count // task_group

    def attend(indices):
        source_ids, tile_ids = indices
        queries = source_desc[source_ids]
        key_rows = target_desc[tile_ids]
        tile_geometry = target_geometry[tile_ids].astype(jnp.float32)
        scores = (
            jnp.einsum("gic,gjc->gij", queries, key_rows, preferred_element_type=jnp.float32)
            * score_scale
        )
        maxima = jnp.max(scores, axis=2)
        exponent = jnp.exp(scores - maxima[:, :, None])
        totals = jnp.sum(exponent, axis=2)
        moment = jnp.einsum("gij,gdj->gdi", exponent, tile_geometry, precision=highest)
        return (maxima, totals, moment)

    maxima, totals, moment = lax.map(
        attend, (sources.reshape(group_count, task_group), targets.reshape(group_count, task_group))
    )
    maxima = maxima.reshape(task_count, all_rows)
    totals = totals.reshape(task_count, all_rows)
    moment = moment.reshape(task_count, 6, all_rows)
    maxima_parts = maxima.reshape(task_count, 1, split_count, block_rows)
    totals_parts = totals.reshape(task_count, 1, split_count, block_rows)
    moment_parts = moment.reshape(task_count, 6, split_count, block_rows)
    maxima_parts, totals_parts, moment_parts = sent_together(
        (maxima_parts, totals_parts, moment_parts), "split", 2, 2, 1
    )
    highest_score = jnp.max(maxima_parts, axis=2)
    factor = jnp.exp(maxima_parts - highest_score[:, :, None, :])
    totals_row = jnp.sum(totals_parts * factor, axis=2)
    moment_row = jnp.sum(moment_parts * factor, axis=2)
    softened = moment_row / totals_row
    row_seen = lax.axis_index("split") * block_rows + jnp.arange(block_rows, dtype=jnp.int32)
    hessian, gradient = assemble(
        softened, points[sources].astype(jnp.float32), row_seen, intersection, all_rows
    )
    hessian, gradient = in_one((hessian, gradient), "split")
    pair_cross = hessian[:, :6, 6:]
    all_poses = pose_index.shape[0]
    source_pose = pose_index[my_pairs[:, 0]]
    target_pose = pose_index[targets]
    source_part = jnp.concatenate(
        [hessian[:, :6, :6].reshape(task_count, 36), gradient[:, :6]], axis=1
    )
    target_part = jnp.concatenate(
        [hessian[:, 6:, 6:].reshape(task_count, 36), gradient[:, 6:]], axis=1
    )
    pose_slots = jnp.arange(all_poses, dtype=jnp.int32)[:, None]
    onehot_source = (pose_slots == source_pose[None, :]).astype(jnp.float32)
    onehot_target = (pose_slots == target_pose[None, :]).astype(jnp.float32)
    pose_terms = (
        jnp.dot(onehot_source, source_part, precision=highest)
        + jnp.dot(onehot_target, target_part, precision=highest)
    ) / task_count
    hessian_rows, gradient_rows = side_by_side(
        (pose_terms[:, :36], pose_terms[:, 36:]), "pair", 0, 1
    )
    return (pair_cross, hessian_rows.reshape(-1, 6, 6), gradient_rows)


def solution(mesh):
    in_specs = (
        P("pair", "split", None),
        P("pair", None, "split"),
        P("pair", None, "split"),
        P(),
        P("pair"),
        P(),
    )
    out_specs = (P("pair", None, None), P("pair", None, None), P("pair", None))
    return jax.shard_map(
        per_device, mesh=mesh, in_specs=in_specs, out_specs=out_specs, check_vma=False
    )
```

profile of v0, /device:TPU:1, one launch (start us, length us, event | category | flops | bytes accessed | tf_op | source)
XLA Modules:
  0.0 201.5 jit_solution(15148078323751725928)
XLA Ops:
  9.7 46.9 %all_gather.11 = bf16[64,6,128]{2,1,0:T(8,128)(2,1)S(1)} all-gather(bf16[1,6,128]{2,1,0:T(8,128)(2,1)S(1)} %pad_maximum_fusion.3), channel_id=1, replica_groups=mesh['pair'=64,'split'=8] {'pair'}, dimensions={0}, use_global_device_ids=true | all-gather | bytes 99840 | tf_op jit(solution)/shard_map/all_gather | solution.py:113
  57.4 24.7 %all_gather.9 = bf16[1024,259]{1,0:T(8,128)(2,1)S(1)} all-gather(bf16[128,259]{1,0:T(8,128)(2,1)S(1)} %pad_maximum_fusion.1), channel_id=1, replica_groups=mesh['pair'=64,'split'=8] {'split'}, dimensions={0}, use_global_device_ids=true | all-gather | bytes 596736 | tf_op jit(solution)/shard_map/all_gather | solution.py:12
  82.1 17.0 %all-gather.2.cloned.1.call-done = bf16[64,128,256]{2,1,0:T(8,128)(2,1)} async-done(((bf16[1,128,256]{2,1,0:T(8,128)(2,1)}), bf16[64,128,256]{2,1,0:T(8,128)(2,1)}) %all-gather.2.cloned.1.call-update) | async-done | bytes 4194320 | tf_op jit(solution)/shard_map/all_gather | solution.py:112
  99.1 37.8 %while.15 = (s32[]{:T(128)}, f32[6,4,1024]{2,1,0:T(4,128)S(1)}, f32[6,4,1024]{2,1,0:T(4,128)S(1)}, f32[6,4,6,1024]{3,2,1,0:T(8,128)}, bf16[1,1024,256]{2,1,0:T(8...) while((s32[]{:T(128)}, f32[6,4,1024]{2,1,0:T(4,128)S(1)}, ...), condition=%wide.region_3.4_spmd.clone, body=%wide.region_0.3_spmd.clone.sunk | while | flops 309847040 | bytes 7887541 | solution.py:133
  99.2 2.7 %gather_fusion = bf16[4,128,256]{2,1,0:T(8,128)(2,1)S(1)} fusion(bf16[64,128,256]{2,1,0:T(8,128)(2,1)} %get-tuple-element.215, s32[1024]{0:T(1024)S(1)} %pad_clamp_fusion.4), kind=kCustom, calls=%fused_computation.clone.1 | custom fusion | bytes 524304 | tf_op jit(solution)/shard_map/while/body/eval_jaxpr/gather | solution.py:121
  103.3 1.7 fusion.60
  105.5 2.8 %gather_fusion = bf16[4,128,256]{2,1,0:T(8,128)(2,1)S(1)} fusion(bf16[64,128,256]{2,1,0:T(8,128)(2,1)} %get-tuple-element.215, s32[1024]{0:T(1024)S(1)} %pad_clamp_fusion.4), kind=kCustom, calls=%fused_computation.clone.1 | custom fusion | bytes 524304 | tf_op jit(solution)/shard_map/while/body/eval_jaxpr/gather | solution.py:121
  109.6 1.7 fusion.60
  111.8 2.8 %gather_fusion = bf16[4,128,256]{2,1,0:T(8,128)(2,1)S(1)} fusion(bf16[64,128,256]{2,1,0:T(8,128)(2,1)} %get-tuple-element.215, s32[1024]{0:T(1024)S(1)} %pad_clamp_fusion.4), kind=kCustom, calls=%fused_computation.clone.1 | custom fusion | bytes 524304 | tf_op jit(solution)/shard_map/while/body/eval_jaxpr/gather | solution.py:121
  115.9 1.7 fusion.60
  118.1 2.8 %gather_fusion = bf16[4,128,256]{2,1,0:T(8,128)(2,1)S(1)} fusion(bf16[64,128,256]{2,1,0:T(8,128)(2,1)} %get-tuple-element.215, s32[1024]{0:T(1024)S(1)} %pad_clamp_fusion.4), kind=kCustom, calls=%fused_computation.clone.1 | custom fusion | bytes 524304 | tf_op jit(solution)/shard_map/while/body/eval_jaxpr/gather | solution.py:121
  122.2 1.7 fusion.60
  124.4 2.8 %gather_fusion = bf16[4,128,256]{2,1,0:T(8,128)(2,1)S(1)} fusion(bf16[64,128,256]{2,1,0:T(8,128)(2,1)} %get-tuple-element.215, s32[1024]{0:T(1024)S(1)} %pad_clamp_fusion.4), kind=kCustom, calls=%fused_computation.clone.1 | custom fusion | bytes 524304 | tf_op jit(solution)/shard_map/while/body/eval_jaxpr/gather | solution.py:121
  128.5 1.7 fusion.60
  130.7 2.8 %gather_fusion = bf16[4,128,256]{2,1,0:T(8,128)(2,1)S(1)} fusion(bf16[64,128,256]{2,1,0:T(8,128)(2,1)} %get-tuple-element.215, s32[1024]{0:T(1024)S(1)} %pad_clamp_fusion.4), kind=kCustom, calls=%fused_computation.clone.1 | custom fusion | bytes 524304 | tf_op jit(solution)/shard_map/while/body/eval_jaxpr/gather | solution.py:121
  134.9 1.7 fusion.60
  137.0 1.3 reshape.208
  138.4 1.0 copy.66
  139.4 9.2 %all-to-all-start = ((f32[24,8,8,128]{3,0,1,2:T(8,128)}), f32[24,8,8,128]{3,0,1,2:T(8,128)S(1)}, u32[]{:S(2)}, u32[]{:S(2)}) async-start(f32[24,8,8,128]{3,0,1,2:T(8,128)} %copy.66), calls=%async_computation | async-start | bytes 1572864 | tf_op jit(solution)/shard_map/all_to_all | solution.py:28
  148.8 12.0 %all-to-all-done = f32[24,8,8,128]{3,0,1,2:T(8,128)S(1)} async-done(((f32[24,8,8,128]{3,0,1,2:T(8,128)}), f32[24,8,8,128]{3,0,1,2:T(8,128)S(1)}, u32[]{:S(2)}, u32[]{:S(2)}) %all-to-all-start) | async-done | bytes 786464 | tf_op jit(solution)/shard_map/all_to_all | solution.py:28
  162.9 4.2 %all-to-all-start.1 = ((f32[8,1,3744]{2,1,0:T(1,128)}), f32[8,1,3744]{2,1,0:T(1,128)S(1)}, u32[]{:S(2)}, u32[]{:S(2)}) async-start(f32[8,1,3744]{2,1,0:T(1,128)} %broadcast_in_dim.20), calls=%async_computation.1 | async-start | bytes 245760 | tf_op jit(solution)/shard_map/all_to_all | solution.py:37
  168.6 3.8 %all-to-all-done.1 = f32[8,1,3744]{2,1,0:T(1,128)S(1)} async-done(((f32[8,1,3744]{2,1,0:T(1,128)}), f32[8,1,3744]{2,1,0:T(1,128)S(1)}, u32[]{:S(2)}, u32[]{:S(2)}) %all-to-all-start.1) | async-done | bytes 119840 | tf_op jit(solution)/shard_map/all_to_all | solution.py:37
  174.4 8.0 %all-to-all-start.2 = ((f32[64,1,42]{2,1,0:T(1,128)}), f32[64,1,42]{2,1,0:T(1,128)S(1)}, u32[]{:S(2)}, u32[]{:S(2)}) async-start(f32[64,1,42]{2,1,0:T(1,128)} %copy.75), calls=%async_computation.2 | async-start | bytes 65536 | tf_op jit(solution)/shard_map/all_to_all | solution.py:60
  183.2 10.1 %all-to-all-done.2 = f32[64,1,42]{2,1,0:T(1,128)S(1)} async-done(((f32[64,1,42]{2,1,0:T(1,128)}), f32[64,1,42]{2,1,0:T(1,128)S(1)}, u32[]{:S(2)}, u32[]{:S(2)}) %all-to-all-start.2) | async-done | bytes 10784 | tf_op jit(solution)/shard_map/all_to_all | solution.py:60
  (104 shorter events, 21.9 us)
Async XLA Ops:
  7.2 0.8 copy-start
  7.2 92.0 %all-gather.2.cloned.1.call-start = ((), (), s32[]{:S(2)}) async-start(), calls=%async_computation.3 | async-start | bytes 4259840 | tf_op jit(solution)/shard_map/all_gather | solution.py:112
  138.3 10.3 %copy-start.2 = (bf16[1,3,128]{2,1,0:T(4,128)(2,1)S(1)}, bf16[1,3,128]{2,1,0:T(4,128)(2,1)}, u32[]{:S(2)}) copy-start(bf16[1,3,128]{2,1,0:T(4,128)(2,1)} %param.9) | copy-start | bytes 2308
  138.4 10.4 %copy-start.3 = (s32[24]{0:T(128)S(1)}, s32[24]{0:T(128)}, u32[]{:S(2)}) copy-start(s32[24]{0:T(128)} %param.12) | copy-start | bytes 292
  139.4 21.4 %all-to-all-start = ((f32[24,8,8,128]{3,0,1,2:T(8,128)}), f32[24,8,8,128]{3,0,1,2:T(8,128)S(1)}, u32[]{:S(2)}, u32[]{:S(2)}) async-start(f32[24,8,8,128]{3,0,1,2:T(8,128)} %copy.66), calls=%async_computation | async-start | bytes 1572864 | tf_op jit(solution)/shard_map/all_to_all | solution.py:28
  148.7 18.5 %copy-start.1 = (s32[64]{0:T(128)S(1)}, s32[64]{0:T(128)}, u32[]{:S(2)}) copy-start(s32[64]{0:T(128)} %param.13) | copy-start | bytes 772
  162.9 9.4 %all-to-all-start.1 = ((f32[8,1,3744]{2,1,0:T(1,128)}), f32[8,1,3744]{2,1,0:T(1,128)S(1)}, u32[]{:S(2)}, u32[]{:S(2)}) async-start(f32[8,1,3744]{2,1,0:T(1,128)} %broadcast_in_dim.20), calls=%async_computation.1 | async-start | bytes 245760 | tf_op jit(solution)/shard_map/all_to_all | solution.py:37
  174.4 18.9 %all-to-all-start.2 = ((f32[64,1,42]{2,1,0:T(1,128)}), f32[64,1,42]{2,1,0:T(1,128)S(1)}, u32[]{:S(2)}, u32[]{:S(2)}) async-start(f32[64,1,42]{2,1,0:T(1,128)} %copy.75), calls=%async_computation.2 | async-start | bytes 65536 | tf_op jit(solution)/shard_map/all_to_all | solution.py:60
Sparse Core Ops, SparseCore 0:
  11.1 88.0 all-gather.1
where the time goes:
time: 202 us
  blocking collectives  71.6 us (35%)
  waiting for transfers between devices  43.6 us (22%)
  local copies, waits for them, and re-layouts  29.3 us (15%)
  starting transfers between devices  21.5 us (11%)
  matrix products  16.4 us (8%)
  between operations  14.4 us (7%)
  other arithmetic  4.44 us (2%)
    all_gather x1, blocking collectives, per_device(): lax.all_gather(geometry, 'pair', axis=0, tiled=True)  46.9 us
    all_gather x1, blocking collectives, rows_first(): out, at, gathered = (lax.all_gather(both, axis, axis=0, tiled=True), 0, [])  24.7 us
    all_gather x1, waiting for transfers between devices, per_device(): lax.all_gather(descriptors, 'pair', axis=0, tiled=True)  17 us
    gather x6, local copies, waits for them, and re-layouts, attend(): key_rows = target_desc[tile_ids]  16.5 us
    all_to_all x1, waiting for transfers between devices, sent_together(): lax.all_to_all(both, axis, split_axis=split_dim, concat_axis=concat_dim,...  12 us
    dot_general x6, matrix products, attend(): jnp.einsum('gij,gdj->gdi', exponent, tile_geometry, precision=highest)  10.2 us
    all_to_all x1, waiting for transfers between devices, sent_and_summed(): lax.all_to_all(pieces, axis, split_axis=0, concat_axis=0, tiled=True)  10.1 us
    all_to_all x1, starting transfers between devices, sent_together(): lax.all_to_all(both, axis, split_axis=split_dim, concat_axis=concat_dim,...  9.23 us
  transfers between devices with their start and end apart: 4, of which 4 were waited for; matrix products, arithmetic and copies ran while one was open for 2% of the time, Pallas kernels for 0%

commit v1 on v0

v1 whole, which is shorter than its diff:
```python
import math

import jax
import jax.numpy as jnp
from jax import lax
from jax.experimental import pallas as pl
from jax.experimental.pallas import tpu as pltpu
from jax.sharding import PartitionSpec as P

SIDE = 8
PAIRS_PER = 24
QUADS = SIDE // 2
SOURCES = 2 * SIDE
SLOTS = SOURCES * QUADS
ROWS = 128
WIDTH = 256
EXTRA = 8
PACKED = ROWS + EXTRA
LANES = 128
POSE = 42
HIGHEST = lax.Precision.HIGHEST

y_groups = [[z * SIDE + y for y in range(SIDE)] for z in range(SIDE)]
z_groups = [[(par + 2 * q) * SIDE + y for q in range(QUADS)] for par in range(2) for y in range(SIDE)]
x_groups = [[2 * x + core for x in range(4)] for core in range(2)]
z_swap = [(z * SIDE + y, (z ^ 1) * SIDE + y) for z in range(SIDE) for y in range(SIDE)]
core_swap = [(s, s ^ 1) for s in range(8)]


def to_each(block, axis, groups):
    copies = jnp.broadcast_to(block, (len(groups[0]), *block.shape))
    return lax.all_to_all(copies, axis, split_axis=0, concat_axis=0, tiled=True, axis_index_groups=groups)


def nt(left, right, precision=None):
    return lax.dot_general(
        left, right, (((1,), (1,)), ((), ())), precision=precision, preferred_element_type=jnp.float32
    )


def cross_rows(u, v):
    return [
        u[1] * v[2] - u[2] * v[1],
        u[2] * v[0] - u[0] * v[2],
        u[0] * v[1] - u[1] * v[0],
    ]


def attend_kernel(scale, cnt_ref, base_ref, dst_ref, a1_ref, a2_ref, b1_ref, b2_ref, out_ref, a_ref, g_ref, h_ref, list_ref):
    a_ref[0:SIDE] = a1_ref[...]
    a_ref[SIDE:SOURCES] = a2_ref[...]
    for q in range(QUADS):
        for c, ref in enumerate((b1_ref, b2_ref)):
            for x in range(4):
                at = (c * 4 + x) * LANES
                g_ref[q, :, at : at + LANES] = ref[x, q, ROWS:PACKED, 0:LANES]
    h_ref[...] = jnp.zeros_like(h_ref)

    def scan(f, n):
        live = cnt_ref[f] > 0

        @pl.when(live)
        def _():
            list_ref[n] = f

        return n + live.astype(jnp.int32)

    n = lax.fori_loop(0, SLOTS, scan, jnp.int32(0))
    list_ref[n] = jnp.int32(SLOTS)
    row_ids = lax.broadcasted_iota(jnp.int32, (1, LANES), 1) + base_ref[0]

    def one(f):
        at = jnp.minimum(f, SLOTS - 1)
        q = at // SOURCES
        ia = at % SOURCES
        keys = jnp.concatenate(
            [ref[x, q, 0:ROWS, :] for ref in (b1_ref, b2_ref) for x in range(4)], axis=0
        )
        scores = nt(keys, a_ref[ia, 0:ROWS, :])
        top = jnp.max(scores, axis=0, keepdims=True)
        weights = jnp.exp2((scores - top) * scale)
        high = weights.astype(jnp.bfloat16)
        low = (weights - high.astype(jnp.float32)).astype(jnp.bfloat16)
        geometry = g_ref[q]
        moment = jnp.dot(geometry, high, preferred_element_type=jnp.float32) + jnp.dot(
            geometry, low, preferred_element_type=jnp.float32
        )
        softened = moment / moment[6:7]
        m = [softened[d : d + 1] for d in range(3)]
        v = [softened[3 + d : 4 + d] for d in range(3)]
        own = a_ref[ia, ROWS:PACKED, 0:LANES].astype(jnp.float32)
        s = [own[d : d + 1] for d in range(3)]
        residual = v[0] * (s[0] - m[0]) + v[1] * (s[1] - m[1]) + v[2] * (s[2] - m[2])
        zero = jnp.zeros_like(residual)
        jacobian = jnp.concatenate(
            cross_rows(s, v) + v + [-t for t in cross_rows(m, v)] + [-t for t in v] + [residual] + [zero] * 3,
            axis=0,
        )
        seen = (row_ids < cnt_ref[f]).astype(jnp.float32)
        h_ref[f] = nt(jacobian * seen, jacobian, HIGHEST)

    def two(t, carry):
        first = list_ref[2 * t]
        second = list_ref[2 * t + 1]
        one(first)
        one(second)
        return carry

    list_ref[n + 1] = jnp.int32(SLOTS)
    lax.fori_loop(0, (n + 1) // 2, two, 0)

    col = lax.broadcasted_iota(jnp.int32, (16, LANES), 0)
    lane = lax.broadcasted_iota(jnp.int32, (16, LANES), 1)
    flat_source = jnp.zeros((SLOTS, LANES), jnp.float32)
    flat_target = jnp.zeros((SLOTS, LANES), jnp.float32)
    flat_cross = jnp.zeros((SLOTS, LANES), jnp.float32)
    for r in range(6):
        tail = (col == 12) & (lane == 36 + r)
        pick_low = (((col < 6) & (lane == 6 * r + col)) | tail).astype(jnp.float32)
        in_high = (col >= 6) & (col < 12) & (lane == 6 * r + col - 6)
        pick_high = (in_high | tail).astype(jnp.float32)
        upper = h_ref[0:SLOTS, r, :]
        lower = h_ref[0:SLOTS, 6 + r, :]
        flat_source += jnp.dot(upper, pick_low, precision=HIGHEST, preferred_element_type=jnp.float32)
        flat_cross += jnp.dot(upper, in_high.astype(jnp.float32), precision=HIGHEST, preferred_element_type=jnp.float32)
        flat_target += jnp.dot(lower, pick_high, precision=HIGHEST, preferred_element_type=jnp.float32)
    dest = lax.broadcasted_iota(jnp.int32, (SIDE * SIDE, SLOTS), 0)
    to_source = (dest == dst_ref[0:1, :]).astype(jnp.float32)
    to_target = (dest == dst_ref[1:2, :]).astype(jnp.float32)
    to_owner = (dest == dst_ref[2:3, :]).astype(jnp.float32)
    pose = jnp.dot(to_source, flat_source, precision=HIGHEST, preferred_element_type=jnp.float32)
    pose += jnp.dot(to_target, flat_target, precision=HIGHEST, preferred_element_type=jnp.float32)
    owned = []
    for q in range(QUADS):
        here = slice(q * SOURCES, (q + 1) * SOURCES)
        moved = pltpu.roll(flat_cross[here], POSE + 36 * (q % 2), 1)
        owned.append(
            jnp.dot(to_owner[:, 0:SOURCES], moved, precision=HIGHEST, preferred_element_type=jnp.float32)
        )
    out_ref[:, 0, :] = pose + owned[0] + owned[1]
    out_ref[:, 1, :] = owned[2] + owned[3]


def collect_kernel(group_ref, quad_ref, got_ref, out_ref, even_ref, odd_ref):
    even_ref[...] = jnp.zeros_like(even_ref)
    odd_ref[...] = jnp.zeros_like(odd_ref)
    for t in range(PAIRS_PER):
        q = quad_ref[t]
        row = got_ref[group_ref[t], q // 2, :].reshape(1, LANES)
        side = (q % 2).astype(jnp.float32)
        even_ref[t : t + 1, :] = row * (1.0 - side)
        odd_ref[t : t + 1, :] = row * side
    even = pltpu.roll(even_ref[...], LANES - POSE, 1)
    odd = pltpu.roll(odd_ref[...], LANES - POSE - 36, 1)
    pose = jnp.sum(got_ref[:, 0, :], axis=0, keepdims=True)
    row_id = lax.broadcasted_iota(jnp.int32, (32, LANES), 0)
    both = jnp.where(row_id == PAIRS_PER, pose, even + odd)
    for s in range(8):
        out_ref[s] = both


def finish_kernel(task_scale, pose_scale, got_ref, cross_ref, hessian_ref, gradient_ref):
    total = got_ref[0]
    for s in range(1, 8):
        total += got_ref[s]
    pose = total[PAIRS_PER : PAIRS_PER + 1, :] * pose_scale
    padded = jnp.concatenate([total, jnp.zeros((LANES - 32, LANES), jnp.float32)], axis=0) * task_scale
    turned = padded.T
    for r in range(6):
        cross_ref[r] = turned[6 * r : 6 * r + 6, 0:PAIRS_PER]
        hessian_ref[r] = pose[:, 6 * r : 6 * r + 6]
    gradient_ref[...] = pose[:, 36:42]


def looked_up(table, ids):
    at = jnp.arange(table.shape[0], dtype=jnp.int32)
    return jnp.sum(jnp.where(at[None, :] == ids[:, None], table[None, :], 0), axis=1)


def per_device(descriptors, points, normals, pair_list, intersection, pose_index):
    own = lax.axis_index("pair")
    z, y = own // SIDE, own % SIDE
    parity = z % 2
    other = z + 1 - 2 * parity

    count_high = (intersection // 16).astype(jnp.bfloat16)
    count_low = (intersection % 16).astype(jnp.bfloat16)
    left = jnp.concatenate(
        [points[0], normals[0], jnp.ones((1, ROWS), jnp.bfloat16), jnp.zeros((1, ROWS), jnp.bfloat16)], axis=0
    )
    counts = jnp.pad(jnp.stack([count_high, count_low]), ((6, 0), (0, LANES - PAIRS_PER)))
    packed = jnp.concatenate([descriptors[0], jnp.concatenate([left, counts], axis=1)], axis=0)

    targets_quad = to_each(packed, "pair", z_groups)
    sources_row = to_each(packed, "pair", y_groups)
    targets_mine = to_each(targets_quad, "split", x_groups)
    sources_next = lax.ppermute(sources_row, "pair", z_swap)
    targets_peer = lax.ppermute(targets_mine, "split", core_swap)

    all_targets = pair_list[:, 1].reshape(SIDE, SIDE, PAIRS_PER)
    task_targets = jnp.concatenate(
        [lax.dynamic_slice_in_dim(all_targets, z, 1, 0)[0], lax.dynamic_slice_in_dim(all_targets, other, 1, 0)[0]], axis=0
    )
    quads = jnp.arange(QUADS, dtype=jnp.int32)
    target_ids = (parity + 2 * quads) * SIDE + y
    is_task = task_targets[None, :, :] == target_ids[:, None, None]
    both = jnp.concatenate([sources_row[:, ROWS + 6 :, LANES:], sources_next[:, ROWS + 6 :, LANES:]], axis=0)
    both = both[:, :, :PAIRS_PER].astype(jnp.float32)
    seen_rows = (both[:, 0] * 16 + both[:, 1]).astype(jnp.int32)
    task_counts = jnp.sum(jnp.where(is_task, seen_rows[None], 0), axis=2).reshape(SLOTS)
    task_counts = jnp.pad(task_counts, (0, 64))

    slot = jnp.arange(SLOTS, dtype=jnp.int32)
    slot_source = slot % SOURCES
    source_ids = jnp.where(slot_source < SIDE, z * SIDE + slot_source, other * SIDE + slot_source - SIDE)
    slot_targets = (parity + 2 * (slot // SOURCES)) * SIDE + y
    destinations = jnp.stack(
        [looked_up(pose_index, source_ids), looked_up(pose_index, slot_targets), source_ids] + [slot] * 5
    )
    base = (lax.axis_index("split") * ROWS).reshape(1)

    smem = pl.BlockSpec(memory_space=pltpu.SMEM)
    vmem = pl.BlockSpec(memory_space=pltpu.VMEM)
    scale = WIDTH**-0.5 / math.log(2.0)
    send = pl.pallas_call(
        lambda *refs: attend_kernel(scale, *refs),
        out_shape=jax.ShapeDtypeStruct((SIDE * SIDE, 2, LANES), jnp.float32),
        in_specs=[smem, smem, vmem, vmem, vmem, vmem, vmem],
        out_specs=vmem,
        scratch_shapes=[
            pltpu.VMEM((SOURCES, PACKED, WIDTH), jnp.bfloat16),
            pltpu.VMEM((QUADS, EXTRA, 8 * LANES), jnp.bfloat16),
            pltpu.VMEM((SLOTS + 1, 16, 16), jnp.float32),
            pltpu.SMEM((SLOTS + 8,), jnp.int32),
        ],
        compiler_params=pltpu.CompilerParams(vmem_limit_bytes=48 * 1024 * 1024),
        name="attend",
    )(task_counts, base, destinations, sources_row, sources_next, targets_mine, targets_peer)
    got = lax.all_to_all(send, "pair", split_axis=0, concat_axis=0, tiled=True)

    my_targets = lax.dynamic_slice_in_dim(pair_list[:, 1], own * PAIRS_PER, PAIRS_PER, 0)
    target_z, target_y = my_targets // SIDE, my_targets % SIDE
    group = jnp.where(target_z % 2 == parity, z, other) * SIDE + target_y
    share = pl.pallas_call(
        collect_kernel,
        out_shape=jax.ShapeDtypeStruct((8, 32, LANES), jnp.float32),
        in_specs=[smem, smem, vmem],
        out_specs=vmem,
        scratch_shapes=[pltpu.VMEM((32, LANES), jnp.float32), pltpu.VMEM((32, LANES), jnp.float32)],
        name="collect",
    )(group, target_z // 2, got)
    shares = lax.all_to_all(share, "split", split_axis=0, concat_axis=0, tiled=True)

    task_scale = 1.0 / (ROWS * 8)
    cross, hessian, gradient = pl.pallas_call(
        lambda *refs: finish_kernel(task_scale, task_scale / PAIRS_PER, *refs),
        out_shape=(
            jax.ShapeDtypeStruct((6, 6, PAIRS_PER), jnp.float32),
            jax.ShapeDtypeStruct((6, 1, 6), jnp.float32),
            jax.ShapeDtypeStruct((1, 6), jnp.float32),
        ),
        in_specs=[vmem],
        out_specs=(vmem, vmem, vmem),
        name="finish",
    )(shares)
    return jnp.transpose(cross, (2, 0, 1)), jnp.transpose(hessian, (1, 0, 2)), gradient


def solution(mesh):
    in_specs = (
        P("pair", "split", None),
        P("pair", None, "split"),
        P("pair", None, "split"),
        P(),
        P("pair"),
        P(),
    )
    out_specs = (P("pair", None, None), P("pair", None, None), P("pair", None))
    return jax.shard_map(
        per_device, mesh=mesh, in_specs=in_specs, out_specs=out_specs, check_vma=False
    )
```

time: 202 us -> 144 us (0.71)
  local copies, waits for them, and re-layouts: 29.3 us -> 1.82 us
  Pallas kernels: 0 us -> 25.1 us
  blocking collectives: 71.6 us -> 49 us
  waiting for transfers between devices: 43.6 us -> 23.6 us
  starting transfers between devices: 21.5 us -> 38.2 us
  matrix products: 16.4 us -> 0 us
  between operations: 14.4 us -> 0.78 us
    all_gather x2 -> x0, blocking collectives: 71.6 us -> none  [the longest x1 46.9 us: per_device(): lax.all_gather(geometry, 'pair', axis=0, tiled=True)]
    all_to_all x0 -> x3, blocking collectives: none -> 49 us  [the longest x2 35.5 us: to_each(): lax.all_to_all(copies, axis, split_axis=0, concat_axis=0, tiled=True, axi...]
    pallas_call x0 -> x3, Pallas kernels: none -> 25.1 us  [the longest x1 21.8 us: per_device(): pl.pallas_call(lambda *refs: attend_kernel(scale, *refs), out_shape=jax.S...]
    gather x14 -> x0, local copies, waits for them, and re-layouts: 21.3 us -> none  [the longest x6 16.5 us: attend(): key_rows = target_desc[tile_ids]]
    all_gather x1 -> x0, waiting for transfers between devices: 17 us -> none  [per_device(): lax.all_gather(descriptors, 'pair', axis=0, tiled=True)]
    ppermute x0 -> x2, starting transfers between devices: none -> 16.6 us  [the longest x1 9.44 us: per_device(): sources_next = lax.ppermute(sources_row, 'pair', z_swap)]
    dot_general x16 -> x0, matrix products: 16.4 us -> none  [the longest x6 10.2 us: attend(): jnp.einsum('gij,gdj->gdi', exponent, tile_geometry, precision=highest)]
    all_to_all x3 -> x2, waiting for transfers between devices: 25.9 us -> 15.1 us  [the longest x1 10.5 us: per_device(): got = lax.all_to_all(send, 'pair', split_axis=0, concat_axis=0, tiled=True)]
  transfers between devices with their start and end apart: 4 -> 4, of which waited for: 4 -> 3; matrix products, arithmetic and copies ran while one was open for 2% -> 1% of each run, Pallas kernels for 0% -> 0%
where the time goes in v1:
time: 144 us; the launch traced here: 142 us
  blocking collectives  49 us (34%)
  starting transfers between devices  38.2 us (27%)
  Pallas kernels  25.1 us (17%)
  waiting for transfers between devices  23.6 us (16%)
  other arithmetic  3.22 us (2%)
  local copies, waits for them, and re-layouts  1.82 us (1%)
    all_to_all x2, blocking collectives, to_each(): lax.all_to_all(copies, axis, split_axis=0, concat_axis=0, tiled=True, axi...  35.5 us
    pallas_call x1, Pallas kernels, per_device(): pl.pallas_call(lambda *refs: attend_kernel(scale, *refs), out_shape=jax.S...  21.8 us
    all_to_all x1, starting transfers between devices, per_device(): got = lax.all_to_all(send, 'pair', split_axis=0, concat_axis=0, tiled=True)  14.8 us
    all_to_all x1, blocking collectives, per_device(): lax.all_to_all(share, 'split', split_axis=0, concat_axis=0, tiled=True)  13.5 us
    all_to_all x1, waiting for transfers between devices, per_device(): got = lax.all_to_all(send, 'pair', split_axis=0, concat_axis=0, tiled=True)  10.5 us
    ppermute x1, starting transfers between devices, per_device(): sources_next = lax.ppermute(sources_row, 'pair', z_swap)  9.44 us
    ppermute x1, waiting for transfers between devices, per_device(): sources_next = lax.ppermute(sources_row, 'pair', z_swap)  8.52 us
    ppermute x1, starting transfers between devices, per_device(): targets_peer = lax.ppermute(targets_mine, 'split', core_swap)  7.19 us
  transfers between devices with their start and end apart: 4, of which 3 were waited for; matrix products, arithmetic and copies ran while one was open for 1% of the time, Pallas kernels for 0%

profile of v1, /device:TPU:1, one launch (start us, length us, event | category | flops | bytes accessed | tf_op | source)
XLA Modules:
  0.0 141.8 jit_solution(15080811252051139683)
XLA Ops:
  0.6 0.7 convert_bitcast_fusion
  1.3 0.9 maximum_maximum_fusion
  2.2 19.9 %all_to_all.25 = bf16[4,136,256]{2,1,0:T(8,128)(2,1)S(1)} all-to-all(bf16[4,136,256]{2,1,0:T(8,128)(2,1)S(1)} %broadcast_in_dim.69), channel_id=1, replica_groups={{0,128,256,384},{8,136,264,392},{16,144,272,400},{24,152,280,408},{32,1..., dimensions={0} | all-to-all | bytes 557056 | tf_op jit(solution)/shard_map/all_to_all | solution.py:32
  22.1 0.1 broadcast_in_dim.70
  22.2 15.6 %all_to_all.26.refs_5_ = bf16[4,4,136,256]{3,2,1,0:T(8,128)(2,1)S(1)} all-to-all(bf16[4,4,136,256]{3,2,1,0:T(8,128)(2,1)S(1)} %broadcast_in_dim.70), channel_id=1, replica_groups={{0,2,4,6},{1,3,5,7},{8,10,12,14},{9,11,13,15},{16,18,20,22},{17,19,21,2..., dimensions={0} | all-to-all | bytes 2228224 | tf_op jit(solution)/shard_map/all_to_all | solution.py:32
  37.8 0.8 broadcast_in_dim.64
  38.6 6.8 %all-to-all-start = ((bf16[8,136,256]{2,1,0:T(8,128)(2,1)}), bf16[8,136,256]{2,1,0:T(8,128)(2,1)S(1)}, u32[]{:S(2)}, u32[]{:S(2)}) async-start(bf16[8,136,256]{2,1,0:T(8,128)(2,1)} %broadcast_in_dim.64), calls=%async_computation | async-start | bytes 1114112 | tf_op jit(solution)/shard_map/all_to_all | solution.py:32
  45.5 0.1 reshape_squeeze.3
  45.6 7.2 %collective-permute-start.1 = (bf16[4,4,136,256]{3,2,1,0:T(8,128)(2,1)S(1)}, bf16[4,4,136,256]{3,2,1,0:T(8,128)(2,1)S(1)}, u32[]{:S(2)}, u32[]{:S(2)}) collective-permute-start(bf16[4,4,136,256]{3,2,1,0:T(8,128)(2,1)S(1)} %all_to_all.26.refs_5_), channel_id=1, source_target_pairs={{0,1},{1,0},{2,3},{3,2},{4,5},{5,4},{6,7},{7,6},{8,9},{9,8},{10,11... | collective-permute-start | bytes 3342344 | tf_op jit(solution)/shard_map/ppermute | solution.py:198
  52.8 0.2 select_reduce_fusion
  53.0 4.6 %all-to-all-done.refs_3_ = bf16[8,136,256]{2,1,0:T(8,128)(2,1)S(1)} async-done(((bf16[8,136,256]{2,1,0:T(8,128)(2,1)}), bf16[8,136,256]{2,1,0:T(8,128)(2,1)S(1)}, u32[]{:S(2)}, u32[]{:S(2)}) %all-to-all-start) | async-done | bytes 557088 | tf_op jit(solution)/shard_map/all_to_all | solution.py:32
  57.6 9.4 %collective-permute-start = (bf16[8,136,256]{2,1,0:T(8,128)(2,1)S(1)}, bf16[8,136,256]{2,1,0:T(8,128)(2,1)S(1)}, u32[]{:S(2)}, u32[]{:S(2)}) collective-permute-start(bf16[8,136,256]{2,1,0:T(8,128)(2,1)S(1)} %all-to-all-done.refs_3_), channel_id=1, source_target_pairs={{0,64},{8,72},{16,80},{24,88},{32,96},{40,104},{48,112},{56,120},{... | collective-permute-start | bytes 1671176 | tf_op jit(solution)/shard_map/ppermute | solution.py:197
  67.1 0.6 and_select_fusion.5
  67.8 8.5 %collective-permute-done.refs_4_ = bf16[8,136,256]{2,1,0:T(8,128)(2,1)S(1)} collective-permute-done((bf16[8,136,256]{2,1,0:T(8,128)(2,1)S(1)}, bf16[8,136,256]{2,1,0:T(8,128)(2,1)S(1)}, u32[]{:S(2)}, u32[]{:S(2)}) %collective-permute-start) | collective-permute-done | bytes 557088 | tf_op jit(solution)/shard_map/ppermute | solution.py:197
  76.3 0.2 select_reduce_fusion.2
  76.5 0.1 reshape.105
  76.6 21.8 %attend.1 = f32[64,2,128]{2,1,0:T(2,128)} custom-call(s32[128]{0:T(128)S(1)} %pad.9.refs_0_, s32[1]{0:T(128)} %bitcast.9.refs_1_, s32[8,64]{1,0:T(8,128)S(1)} %stack.29.refs_2_, bf16[8,136,256]{2,1,0:T(8,128)(2,1)S(1)} %all-to-all-done.refs_3_, bf16[8,136,256]{2,1,0:T(8,128)(2,1)S(1)} %collective-permute-done.refs_4_, ...), custom_call_target="tpu_custom_call" | custom-call | tf_op jit(solution)/shard_map/attend/pallas_call | solution.py:225
  98.4 14.8 %all-to-all-start.3 = ((f32[64,2,128]{2,1,0:T(2,128)}), f32[64,2,128]{2,1,0:T(2,128)S(1)}, u32[]{:S(2)}, u32[]{:S(2)}) async-start(f32[64,2,128]{2,1,0:T(2,128)} %attend.1), calls=%async_computation.3 | async-start | bytes 131072 | tf_op jit(solution)/shard_map/all_to_all | solution.py:239
  113.2 0.6 fusion.8.group_ref
  113.8 10.5 %all-to-all-done.3.got_ref = f32[64,2,128]{2,1,0:T(2,128)S(1)} async-done(((f32[64,2,128]{2,1,0:T(2,128)}), f32[64,2,128]{2,1,0:T(2,128)S(1)}, u32[]{:S(2)}, u32[]{:S(2)}) %all-to-all-start.3) | async-done | bytes 65568 | tf_op jit(solution)/shard_map/all_to_all | solution.py:239
  124.3 0.6 copy-done
  124.9 1.8 %collect.1 = f32[8,32,128]{2,1,0:T(8,128)} custom-call(s32[24]{0:T(128)} %fusion.8.group_ref, s32[24]{0:T(128)} %get-tuple-element.11.quad_ref, f32[64,2,128]{2,1,0:T(2,128)} %copy-done), custom_call_target="tpu_custom_call" | custom-call | tf_op jit(solution)/shard_map/collect/pallas_call | solution.py:244
  126.7 13.5 %all_to_all.27.refs_0_ = f32[8,32,128]{2,1,0:T(8,128)} all-to-all(f32[8,32,128]{2,1,0:T(8,128)} %collect.1), channel_id=1, replica_groups=mesh['pair'=64,'split'=8] {'split'}, dimensions={0} | all-to-all | bytes 262144 | tf_op jit(solution)/shard_map/all_to_all | solution.py:252
  140.2 1.6 %finish.1 = (f32[6,6,24]{2,1,0:T(8,128)}, f32[6,1,6]{2,1,0:T(1,128)}, f32[1,6]{1,0:T(1,128)}) custom-call(f32[8,32,128]{2,1,0:T(8,128)} %all_to_all.27.refs_0_), custom_call_target="tpu_custom_call" | custom-call | tf_op jit(solution)/shard_map/finish/pallas_call | solution.py:255
  (23 shorter events, 0.2 us)
Async XLA Ops:
  37.8 7.7 %copy-start.1 = (s32[1536,2]{0,1:T(2,128)S(1)}, s32[1536,2]{0,1:T(2,128)}, u32[]{:S(2)}) copy-start(s32[1536,2]{0,1:T(2,128)} %param.9) | copy-start | bytes 36868
  37.8 15.0 %copy-start.2 = (s32[64]{0:T(128)S(1)}, s32[64]{0:T(128)}, u32[]{:S(2)}) copy-start(s32[64]{0:T(128)} %param.11) | copy-start | bytes 772
  38.6 19.0 %all-to-all-start = ((bf16[8,136,256]{2,1,0:T(8,128)(2,1)}), bf16[8,136,256]{2,1,0:T(8,128)(2,1)S(1)}, u32[]{:S(2)}, u32[]{:S(2)}) async-start(bf16[8,136,256]{2,1,0:T(8,128)(2,1)} %broadcast_in_dim.64), calls=%async_computation | async-start | bytes 1114112 | tf_op jit(solution)/shard_map/all_to_all | solution.py:32
  45.6 31.0 %collective-permute-start.1 = (bf16[4,4,136,256]{3,2,1,0:T(8,128)(2,1)S(1)}, bf16[4,4,136,256]{3,2,1,0:T(8,128)(2,1)S(1)}, u32[]{:S(2)}, u32[]{:S(2)}) collective-permute-start(bf16[4,4,136,256]{3,2,1,0:T(8,128)(2,1)S(1)} %all_to_all.26.refs_5_), channel_id=1, source_target_pairs={{0,1},{1,0},{2,3},{3,2},{4,5},{5,4},{6,7},{7,6},{8,9},{9,8},{10,11... | collective-permute-start | bytes 3342344 | tf_op jit(solution)/shard_map/ppermute | solution.py:198
  57.6 18.7 %collective-permute-start = (bf16[8,136,256]{2,1,0:T(8,128)(2,1)S(1)}, bf16[8,136,256]{2,1,0:T(8,128)(2,1)S(1)}, u32[]{:S(2)}, u32[]{:S(2)}) collective-permute-start(bf16[8,136,256]{2,1,0:T(8,128)(2,1)S(1)} %all-to-all-done.refs_3_), channel_id=1, source_target_pairs={{0,64},{8,72},{16,80},{24,88},{32,96},{40,104},{48,112},{56,120},{... | collective-permute-start | bytes 1671176 | tf_op jit(solution)/shard_map/ppermute | solution.py:197
  98.4 25.9 %all-to-all-start.3 = ((f32[64,2,128]{2,1,0:T(2,128)}), f32[64,2,128]{2,1,0:T(2,128)S(1)}, u32[]{:S(2)}, u32[]{:S(2)}) async-start(f32[64,2,128]{2,1,0:T(2,128)} %attend.1), calls=%async_computation.3 | async-start | bytes 131072 | tf_op jit(solution)/shard_map/all_to_all | solution.py:239
  124.3 0.6 copy-start

commit v2 on v1

--- a/solution.py
+++ b/solution.py
@@ -6,6 +6,7 @@
 from jax.experimental import pallas as pl
 from jax.experimental.pallas import tpu as pltpu
 from jax.sharding import PartitionSpec as P
+
 
 SIDE = 8
 PAIRS_PER = 24
@@ -21,10 +22,13 @@
 HIGHEST = lax.Precision.HIGHEST
 
 y_groups = [[z * SIDE + y for y in range(SIDE)] for z in range(SIDE)]
-z_groups = [[(par + 2 * q) * SIDE + y for q in range(QUADS)] for par in range(2) for y in range(SIDE)]
 x_groups = [[2 * x + core for x in range(4)] for core in range(2)]
 z_swap = [(z * SIDE + y, (z ^ 1) * SIDE + y) for z in range(SIDE) for y in range(SIDE)]
 core_swap = [(s, s ^ 1) for s in range(8)]
+
+
+def from_ahead(steps):
+    return [(((z + steps) % SIDE) * SIDE + y, z * SIDE + y) for z in range(SIDE) for y in range(SIDE)]
 
 
 def to_each(block, axis, groups):
@@ -191,8 +195,8 @@
     counts = jnp.pad(jnp.stack([count_high, count_low]), ((6, 0), (0, LANES - PAIRS_PER)))
     packed = jnp.concatenate([descriptors[0], jnp.concatenate([left, counts], axis=1)], axis=0)
 
-    targets_quad = to_each(packed, "pair", z_groups)
     sources_row = to_each(packed, "pair", y_groups)
+    targets_quad = jnp.stack([packed] + [lax.ppermute(packed, "pair", from_ahead(2 * q)) for q in range(1, QUADS)])
     targets_mine = to_each(targets_quad, "split", x_groups)
     sources_next = lax.ppermute(sources_row, "pair", z_swap)
     targets_peer = lax.ppermute(targets_mine, "split", core_swap)
@@ -202,9 +206,10 @@
         [lax.dynamic_slice_in_dim(all_targets, z, 1, 0)[0], lax.dynamic_slice_in_dim(all_targets, other, 1, 0)[0]], axis=0
     )
     quads = jnp.arange(QUADS, dtype=jnp.int32)
-    target_ids = (parity + 2 * quads) * SIDE + y
+    target_ids = (z + 2 * quads) % SIDE * SIDE + y
     is_task = task_targets[None, :, :] == target_ids[:, None, None]
-    both = jnp.concatenate([sources_row[:, ROWS + 6 :, LANES:], sources_next[:, ROWS + 6 :, LANES:]], axis=0)
+    next_counts = sources_next[:, ROWS + 6 :, LANES:]
+    both = jnp.concatenate([sources_row[:, ROWS + 6 :, LANES:], next_counts], axis=0)
     both = both[:, :, :PAIRS_PER].astype(jnp.float32)
     seen_rows = (both[:, 0] * 16 + both[:, 1]).astype(jnp.int32)
     task_counts = jnp.sum(jnp.where(is_task, seen_rows[None], 0), axis=2).reshape(SLOTS)
@@ -213,7 +218,7 @@
     slot = jnp.arange(SLOTS, dtype=jnp.int32)
     slot_source = slot % SOURCES
     source_ids = jnp.where(slot_source < SIDE, z * SIDE + slot_source, other * SIDE + slot_source - SIDE)
-    slot_targets = (parity + 2 * (slot // SOURCES)) * SIDE + y
+    slot_targets = (z + 2 * (slot // SOURCES)) % SIDE * SIDE + y
     destinations = jnp.stack(
         [looked_up(pose_index, source_ids), looked_up(pose_index, slot_targets), source_ids] + [slot] * 5
     )
@@ -240,7 +245,9 @@
 
     my_targets = lax.dynamic_slice_in_dim(pair_list[:, 1], own * PAIRS_PER, PAIRS_PER, 0)
     target_z, target_y = my_targets // SIDE, my_targets % SIDE
-    group = jnp.where(target_z % 2 == parity, z, other) * SIDE + target_y
+    group_z = jnp.where(target_z % 2 == parity, z, other)
+    group = group_z * SIDE + target_y
+    quad = (target_z - group_z + SIDE) % SIDE // 2
     share = pl.pallas_call(
         collect_kernel,
         out_shape=jax.ShapeDtypeStruct((8, 32, LANES), jnp.float32),
@@ -248,7 +255,7 @@
         out_specs=vmem,
         scratch_shapes=[pltpu.VMEM((32, LANES), jnp.float32), pltpu.VMEM((32, LANES), jnp.float32)],
         name="collect",
-    )(group, target_z // 2, got)
+    )(group, quad, got)
     shares = lax.all_to_all(share, "split", split_axis=0, concat_axis=0, tiled=True)
 
     task_scale = 1.0 / (ROWS * 8)

time: 144 us -> 145 us (level)
  blocking collectives: 49 us -> 31.2 us
  starting transfers between devices: 38.2 us -> 47.6 us
  waiting for transfers between devices: 23.6 us -> 31.6 us
  Pallas kernels: 25.1 us -> 26.8 us
    all_to_all x2 -> x1, blocking collectives: 35.5 us -> 17.4 us  [to_each(): lax.all_to_all(copies, axis, split_axis=0, concat_axis=0, tiled=True, axi...]
    ppermute x0 -> x3, starting transfers between devices: none -> 17.6 us  [per_device(): lax.ppermute(packed, 'pair', from_ahead(2 * q))]
    all_to_all x1, waiting for transfers between devices: 4.62 us -> 9.6 us  [to_each(): lax.all_to_all(copies, axis, split_axis=0, concat_axis=0, tiled=True, axi...]
    all_to_all x1, starting transfers between devices: 14.8 us -> 11.3 us  [per_device(): got = lax.all_to_all(send, 'pair', split_axis=0, concat_axis=0, tiled=True)]
    ppermute x1, starting transfers between devices: 9.44 us -> 6.46 us  [per_device(): sources_next = lax.ppermute(sources_row, 'pair', z_swap)]
    ppermute x0 -> x3, waiting for transfers between devices: none -> 2.1 us  [per_device(): lax.ppermute(packed, 'pair', from_ahead(2 * q))]
    ppermute x1, starting transfers between devices: 7.19 us -> 5.38 us  [per_device(): targets_peer = lax.ppermute(targets_mine, 'split', core_swap)]
    pallas_call x1, Pallas kernels: 21.8 us -> 23.5 us  [per_device(): pl.pallas_call(lambda *refs: attend_kernel(scale, *refs), out_shape=jax.S...]
  transfers between devices with their start and end apart: 4 -> 7, of which waited for: 3 -> 5; matrix products, arithmetic and copies ran while one was open for 1% -> 2% of each run, Pallas kernels for 0% -> 0%
where the time goes in v2:
time: 145 us; the launch traced here: 144 us
  starting transfers between devices  47.6 us (33%)
  waiting for transfers between devices  31.6 us (22%)
  blocking collectives  31.2 us (22%)
  Pallas kernels  26.8 us (18%)
  other arithmetic  4.1 us (3%)
  local copies, waits for them, and re-layouts  1.81 us (1%)
    pallas_call x1, Pallas kernels, per_device(): pl.pallas_call(lambda *refs: attend_kernel(scale, *refs), out_shape=jax.S...  23.5 us
    ppermute x3, starting transfers between devices, per_device(): lax.ppermute(packed, 'pair', from_ahead(2 * q))  17.6 us
    all_to_all x1, blocking collectives, to_each(): lax.all_to_all(copies, axis, split_axis=0, concat_axis=0, tiled=True, axi...  17.4 us
    all_to_all x1, blocking collectives, per_device(): lax.all_to_all(share, 'split', split_axis=0, concat_axis=0, tiled=True)  13.9 us
    all_to_all x1, starting transfers between devices, per_device(): got = lax.all_to_all(send, 'pair', split_axis=0, concat_axis=0, tiled=True)  11.3 us
    all_to_all x1, waiting for transfers between devices, per_device(): got = lax.all_to_all(send, 'pair', split_axis=0, concat_axis=0, tiled=True)  10.6 us
    all_to_all x1, waiting for transfers between devices, to_each(): lax.all_to_all(copies, axis, split_axis=0, concat_axis=0, tiled=True, axi...  9.6 us
    ppermute x1, waiting for transfers between devices, per_device(): sources_next = lax.ppermute(sources_row, 'pair', z_swap)  9.31 us
  transfers between devices with their start and end apart: 7, of which 5 were waited for; matrix products, arithmetic and copies ran while one was open for 2% of the time, Pallas kernels for 0%

profile of v2, /device:TPU:1, one launch (start us, length us, event | category | flops | bytes accessed | tf_op | source)
XLA Modules:
  0.0 143.9 jit_solution(345740673893748065)
XLA Ops:
  0.6 0.7 convert_bitcast_fusion
  1.3 0.9 maximum_maximum_fusion
  2.2 11.5 %collective-permute-start.2 = (bf16[136,256]{1,0:T(8,128)(2,1)S(1)}, bf16[136,256]{1,0:T(8,128)(2,1)S(1)}, u32[]{:S(2)}, u32[]{:S(2)}) collective-permute-start(bf16[136,256]{1,0:T(8,128)(2,1)S(1)} %maximum_maximum_fusion), channel_id=1, source_target_pairs={{256,0},{264,8},{272,16},{280,24},{288,32},{296,40},{304,48},{312,... | collective-permute-start | bytes 208904 | tf_op jit(solution)/shard_map/ppermute | solution.py:199
  13.7 1.9 %collective-permute-start.1 = (bf16[136,256]{1,0:T(8,128)(2,1)S(1)}, bf16[136,256]{1,0:T(8,128)(2,1)S(1)}, u32[]{:S(2)}, u32[]{:S(2)}) collective-permute-start(bf16[136,256]{1,0:T(8,128)(2,1)S(1)} %maximum_maximum_fusion), channel_id=1, source_target_pairs={{128,0},{136,8},{144,16},{152,24},{160,32},{168,40},{176,48},{184,... | collective-permute-start | bytes 208904 | tf_op jit(solution)/shard_map/ppermute | solution.py:199
  15.6 4.2 %collective-permute-start.3 = (bf16[136,256]{1,0:T(8,128)(2,1)S(1)}, bf16[136,256]{1,0:T(8,128)(2,1)S(1)}, u32[]{:S(2)}, u32[]{:S(2)}) collective-permute-start(bf16[136,256]{1,0:T(8,128)(2,1)S(1)} %maximum_maximum_fusion), channel_id=1, source_target_pairs={{384,0},{392,8},{400,16},{408,24},{416,32},{424,40},{432,48},{440,... | collective-permute-start | bytes 208904 | tf_op jit(solution)/shard_map/ppermute | solution.py:199
  19.9 0.9 fusion.22
  20.8 1.7 %collective-permute-done.1 = bf16[136,256]{1,0:T(8,128)(2,1)S(1)} collective-permute-done((bf16[136,256]{1,0:T(8,128)(2,1)S(1)}, bf16[136,256]{1,0:T(8,128)(2,1)S(1)}, u32[]{:S(2)}, u32[]{:S(2)}) %collective-permute-start.1) | collective-permute-done | bytes 69664 | tf_op jit(solution)/shard_map/ppermute | solution.py:199
  22.5 0.4 collective-permute-done.3
  23.0 17.4 %all_to_all.20.refs_5_ = bf16[4,4,136,256]{3,2,1,0:T(8,128)(2,1)S(1)} all-to-all(bf16[4,4,136,256]{3,2,1,0:T(8,128)(2,1)S(1)} %broadcast_in_dim.66), channel_id=1, replica_groups={{0,2,4,6},{1,3,5,7},{8,10,12,14},{9,11,13,15},{16,18,20,22},{17,19,21,2..., dimensions={0} | all-to-all | bytes 2228224 | tf_op jit(solution)/shard_map/all_to_all | solution.py:36
  40.4 0.8 broadcast_in_dim.61
  41.2 6.8 %all-to-all-start = ((bf16[8,136,256]{2,1,0:T(8,128)(2,1)}), bf16[8,136,256]{2,1,0:T(8,128)(2,1)S(1)}, u32[]{:S(2)}, u32[]{:S(2)}) async-start(bf16[8,136,256]{2,1,0:T(8,128)(2,1)} %broadcast_in_dim.61), calls=%async_computation | async-start | bytes 1114112 | tf_op jit(solution)/shard_map/all_to_all | solution.py:36
  48.4 5.4 %collective-permute-start.4 = (bf16[4,4,136,256]{3,2,1,0:T(8,128)(2,1)S(1)}, bf16[4,4,136,256]{3,2,1,0:T(8,128)(2,1)S(1)}, u32[]{:S(2)}, u32[]{:S(2)}) collective-permute-start(bf16[4,4,136,256]{3,2,1,0:T(8,128)(2,1)S(1)} %all_to_all.20.refs_5_), channel_id=1, source_target_pairs={{0,1},{1,0},{2,3},{3,2},{4,5},{5,4},{6,7},{7,6},{8,9},{9,8},{10,11... | collective-permute-start | bytes 3342344 | tf_op jit(solution)/shard_map/ppermute | solution.py:202
  53.9 9.6 %all-to-all-done.refs_3_ = bf16[8,136,256]{2,1,0:T(8,128)(2,1)S(1)} async-done(((bf16[8,136,256]{2,1,0:T(8,128)(2,1)}), bf16[8,136,256]{2,1,0:T(8,128)(2,1)S(1)}, u32[]{:S(2)}, u32[]{:S(2)}) %all-to-all-start) | async-done | bytes 557088 | tf_op jit(solution)/shard_map/all_to_all | solution.py:36
  63.5 6.5 %collective-permute-start = (bf16[8,136,256]{2,1,0:T(8,128)(2,1)S(1)}, bf16[8,136,256]{2,1,0:T(8,128)(2,1)S(1)}, u32[]{:S(2)}, u32[]{:S(2)}) collective-permute-start(bf16[8,136,256]{2,1,0:T(8,128)(2,1)S(1)} %all-to-all-done.refs_3_), channel_id=1, source_target_pairs={{0,64},{8,72},{16,80},{24,88},{32,96},{40,104},{48,112},{56,120},{... | collective-permute-start | bytes 1671176 | tf_op jit(solution)/shard_map/ppermute | solution.py:201
  70.0 0.5 and_select_fusion.7
  70.6 9.3 %collective-permute-done.refs_4_ = bf16[8,136,256]{2,1,0:T(8,128)(2,1)S(1)} collective-permute-done((bf16[8,136,256]{2,1,0:T(8,128)(2,1)S(1)}, bf16[8,136,256]{2,1,0:T(8,128)(2,1)S(1)}, u32[]{:S(2)}, u32[]{:S(2)}) %collective-permute-start) | collective-permute-done | bytes 557088 | tf_op jit(solution)/shard_map/ppermute | solution.py:201
  80.3 23.5 %attend.1 = f32[64,2,128]{2,1,0:T(2,128)} custom-call(s32[128]{0:T(128)S(1)} %pad.9.refs_0_, s32[1]{0:T(128)} %bitcast.9.refs_1_, s32[8,64]{1,0:T(8,128)S(1)} %stack.44.refs_2_, bf16[8,136,256]{2,1,0:T(8,128)(2,1)S(1)} %all-to-all-done.refs_3_, bf16[8,136,256]{2,1,0:T(8,128)(2,1)S(1)} %collective-permute-done.refs_4_, ...), custom_call_target="tpu_custom_call" | custom-call | tf_op jit(solution)/shard_map/attend/pallas_call | solution.py:230
  103.7 11.3 %all-to-all-start.2 = ((f32[64,2,128]{2,1,0:T(2,128)}), f32[64,2,128]{2,1,0:T(2,128)S(1)}, u32[]{:S(2)}, u32[]{:S(2)}) async-start(f32[64,2,128]{2,1,0:T(2,128)} %attend.1), calls=%async_computation.2 | async-start | bytes 131072 | tf_op jit(solution)/shard_map/all_to_all | solution.py:244
  115.0 0.5 fusion.8.group_ref
  115.5 10.6 %all-to-all-done.2.got_ref = f32[64,2,128]{2,1,0:T(2,128)S(1)} async-done(((f32[64,2,128]{2,1,0:T(2,128)}), f32[64,2,128]{2,1,0:T(2,128)S(1)}, u32[]{:S(2)}, u32[]{:S(2)}) %all-to-all-start.2) | async-done | bytes 65568 | tf_op jit(solution)/shard_map/all_to_all | solution.py:244
  126.1 0.6 copy-done
  126.7 1.8 %collect.1 = f32[8,32,128]{2,1,0:T(8,128)} custom-call(s32[24]{0:T(128)} %fusion.8.group_ref, s32[24]{0:T(128)} %get-tuple-element.11.quad_ref, f32[64,2,128]{2,1,0:T(2,128)} %copy-done), custom_call_target="tpu_custom_call" | custom-call | tf_op jit(solution)/shard_map/collect/pallas_call | solution.py:251
  128.4 13.9 %all_to_all.21.refs_0_ = f32[8,32,128]{2,1,0:T(8,128)} all-to-all(f32[8,32,128]{2,1,0:T(8,128)} %collect.1), channel_id=1, replica_groups=mesh['pair'=64,'split'=8] {'split'}, dimensions={0} | all-to-all | bytes 262144 | tf_op jit(solution)/shard_map/all_to_all | solution.py:259
  142.3 1.6 %finish.1 = (f32[6,6,24]{2,1,0:T(8,128)}, f32[6,1,6]{2,1,0:T(1,128)}, f32[1,6]{1,0:T(1,128)}) custom-call(f32[8,32,128]{2,1,0:T(8,128)} %all_to_all.21.refs_0_), custom_call_target="tpu_custom_call" | custom-call | tf_op jit(solution)/shard_map/finish/pallas_call | solution.py:262
  (30 shorter events, 1.0 us)
Async XLA Ops:
  2.2 18.6 %collective-permute-start.2 = (bf16[136,256]{1,0:T(8,128)(2,1)S(1)}, bf16[136,256]{1,0:T(8,128)(2,1)S(1)}, u32[]{:S(2)}, u32[]{:S(2)}) collective-permute-start(bf16[136,256]{1,0:T(8,128)(2,1)S(1)} %maximum_maximum_fusion), channel_id=1, source_target_pairs={{256,0},{264,8},{272,16},{280,24},{288,32},{296,40},{304,48},{312,... | collective-permute-start | bytes 208904 | tf_op jit(solution)/shard_map/ppermute | solution.py:199
  13.7 8.8 %collective-permute-start.1 = (bf16[136,256]{1,0:T(8,128)(2,1)S(1)}, bf16[136,256]{1,0:T(8,128)(2,1)S(1)}, u32[]{:S(2)}, u32[]{:S(2)}) collective-permute-start(bf16[136,256]{1,0:T(8,128)(2,1)S(1)} %maximum_maximum_fusion), channel_id=1, source_target_pairs={{128,0},{136,8},{144,16},{152,24},{160,32},{168,40},{176,48},{184,... | collective-permute-start | bytes 208904 | tf_op jit(solution)/shard_map/ppermute | solution.py:199
  15.6 7.2 %collective-permute-start.3 = (bf16[136,256]{1,0:T(8,128)(2,1)S(1)}, bf16[136,256]{1,0:T(8,128)(2,1)S(1)}, u32[]{:S(2)}, u32[]{:S(2)}) collective-permute-start(bf16[136,256]{1,0:T(8,128)(2,1)S(1)} %maximum_maximum_fusion), channel_id=1, source_target_pairs={{384,0},{392,8},{400,16},{408,24},{416,32},{424,40},{432,48},{440,... | collective-permute-start | bytes 208904 | tf_op jit(solution)/shard_map/ppermute | solution.py:199
  40.4 7.7 %copy-start.1 = (s32[1536,2]{0,1:T(2,128)S(1)}, s32[1536,2]{0,1:T(2,128)}, u32[]{:S(2)}) copy-start(s32[1536,2]{0,1:T(2,128)} %param.9) | copy-start | bytes 36868
  40.4 7.8 %copy-start.2 = (s32[64]{0:T(128)S(1)}, s32[64]{0:T(128)}, u32[]{:S(2)}) copy-start(s32[64]{0:T(128)} %param.11) | copy-start | bytes 772
  41.2 22.3 %all-to-all-start = ((bf16[8,136,256]{2,1,0:T(8,128)(2,1)}), bf16[8,136,256]{2,1,0:T(8,128)(2,1)S(1)}, u32[]{:S(2)}, u32[]{:S(2)}) async-start(bf16[8,136,256]{2,1,0:T(8,128)(2,1)} %broadcast_in_dim.61), calls=%async_computation | async-start | bytes 1114112 | tf_op jit(solution)/shard_map/all_to_all | solution.py:36
  48.4 31.8 %collective-permute-start.4 = (bf16[4,4,136,256]{3,2,1,0:T(8,128)(2,1)S(1)}, bf16[4,4,136,256]{3,2,1,0:T(8,128)(2,1)S(1)}, u32[]{:S(2)}, u32[]{:S(2)}) collective-permute-start(bf16[4,4,136,256]{3,2,1,0:T(8,128)(2,1)S(1)} %all_to_all.20.refs_5_), channel_id=1, source_target_pairs={{0,1},{1,0},{2,3},{3,2},{4,5},{5,4},{6,7},{7,6},{8,9},{9,8},{10,11... | collective-permute-start | bytes 3342344 | tf_op jit(solution)/shard_map/ppermute | solution.py:202
  63.5 16.4 %collective-permute-start = (bf16[8,136,256]{2,1,0:T(8,128)(2,1)S(1)}, bf16[8,136,256]{2,1,0:T(8,128)(2,1)S(1)}, u32[]{:S(2)}, u32[]{:S(2)}) collective-permute-start(bf16[8,136,256]{2,1,0:T(8,128)(2,1)S(1)} %all-to-all-done.refs_3_), channel_id=1, source_target_pairs={{0,64},{8,72},{16,80},{24,88},{32,96},{40,104},{48,112},{56,120},{... | collective-permute-start | bytes 1671176 | tf_op jit(solution)/shard_map/ppermute | solution.py:201
  103.7 22.4 %all-to-all-start.2 = ((f32[64,2,128]{2,1,0:T(2,128)}), f32[64,2,128]{2,1,0:T(2,128)S(1)}, u32[]{:S(2)}, u32[]{:S(2)}) async-start(f32[64,2,128]{2,1,0:T(2,128)} %attend.1), calls=%async_computation.2 | async-start | bytes 131072 | tf_op jit(solution)/shard_map/all_to_all | solution.py:244
  126.1 0.6 copy-start

commit v3 on v2

--- a/solution.py
+++ b/solution.py
@@ -19,6 +19,7 @@
 PACKED = ROWS + EXTRA
 LANES = 128
 POSE = 42
+CHUNKS = 1
 HIGHEST = lax.Precision.HIGHEST
 
 y_groups = [[z * SIDE + y for y in range(SIDE)] for z in range(SIDE)]
@@ -50,7 +51,7 @@
     ]
 
 
-def attend_kernel(scale, cnt_ref, base_ref, dst_ref, a1_ref, a2_ref, b1_ref, b2_ref, out_ref, a_ref, g_ref, h_ref, list_ref):
+def attend_kernel(scale, cnt_ref, base_ref, dst_ref, a1_ref, a2_ref, b1_ref, b2_ref, out_ref, a_ref, g_ref, h_ref, list_ref, even_ref, odd_ref):
     a_ref[0:SIDE] = a1_ref[...]
     a_ref[SIDE:SOURCES] = a2_ref[...]
     for q in range(QUADS):
@@ -60,36 +61,28 @@
                 g_ref[q, :, at : at + LANES] = ref[x, q, ROWS:PACKED, 0:LANES]
     h_ref[...] = jnp.zeros_like(h_ref)
 
-    def scan(f, n):
-        live = cnt_ref[f] > 0
-
-        @pl.when(live)
-        def _():
-            list_ref[n] = f
-
-        return n + live.astype(jnp.int32)
-
-    n = lax.fori_loop(0, SLOTS, scan, jnp.int32(0))
-    list_ref[n] = jnp.int32(SLOTS)
+    n = jnp.int32(0)
+    for q in range(QUADS):
+
+        def scan(ia, n, q=q):
+            f = q * SOURCES + ia
+            live = cnt_ref[f] > 0
+
+            @pl.when(live)
+            def _():
+                list_ref[n] = f
+
+            return n + live.astype(jnp.int32)
+
+        n = lax.fori_loop(0, SOURCES, scan, n, unroll=True)
+        list_ref[n] = jnp.int32(q * SOURCES + SLOTS)
+        n += n % 2
     row_ids = lax.broadcasted_iota(jnp.int32, (1, LANES), 1) + base_ref[0]
 
-    def one(f):
-        at = jnp.minimum(f, SLOTS - 1)
-        q = at // SOURCES
-        ia = at % SOURCES
-        keys = jnp.concatenate(
-            [ref[x, q, 0:ROWS, :] for ref in (b1_ref, b2_ref) for x in range(4)], axis=0
-        )
-        scores = nt(keys, a_ref[ia, 0:ROWS, :])
-        top = jnp.max(scores, axis=0, keepdims=True)
-        weights = jnp.exp2((scores - top) * scale)
-        high = weights.astype(jnp.bfloat16)
-        low = (weights - high.astype(jnp.float32)).astype(jnp.bfloat16)
-        geometry = g_ref[q]
-        moment = jnp.dot(geometry, high, preferred_element_type=jnp.float32) + jnp.dot(
-            geometry, low, preferred_element_type=jnp.float32
-        )
-        softened = moment / moment[6:7]
+    def block_of(entry, softened):
+        f = entry % SLOTS
+        ia = f % SOURCES
+        count = jnp.where(entry < SLOTS, cnt_ref[f], 0)
         m = [softened[d : d + 1] for d in range(3)]
         v = [softened[3 + d : 4 + d] for d in range(3)]
         own = a_ref[ia, ROWS:PACKED, 0:LANES].astype(jnp.float32)
@@ -100,18 +93,58 @@
             cross_rows(s, v) + v + [-t for t in cross_rows(m, v)] + [-t for t in v] + [residual] + [zero] * 3,
             axis=0,
         )
-        seen = (row_ids < cnt_ref[f]).astype(jnp.float32)
-        h_ref[f] = nt(jacobian * seen, jacobian, HIGHEST)
-
-    def two(t, carry):
-        first = list_ref[2 * t]
-        second = list_ref[2 * t + 1]
-        one(first)
-        one(second)
-        return carry
-
-    list_ref[n + 1] = jnp.int32(SLOTS)
-    lax.fori_loop(0, (n + 1) // 2, two, 0)
+        seen = (row_ids < count).astype(jnp.float32)
+        h_ref[jnp.minimum(entry, SLOTS)] = nt(jacobian * seen, jacobian, HIGHEST)
+
+    def score(pair, buffer):
+        first = list_ref[2 * pair]
+        second = list_ref[2 * pair + 1]
+        q = (first % SLOTS) // SOURCES
+        queries = jnp.concatenate(
+            [a_ref[first % SOURCES, 0:ROWS, :], a_ref[second % SOURCES, 0:ROWS, :]], axis=0
+        )
+        tops = []
+        for c, ref in enumerate((b1_ref, b2_ref)):
+            keys = jnp.concatenate([ref[x, q, 0:ROWS, :] for x in range(4)], axis=0)
+            part = nt(keys, queries)
+            buffer[c * 4 * ROWS : (c + 1) * 4 * ROWS, :] = part
+            tops.append(jnp.max(part, axis=0, keepdims=True))
+        return jnp.maximum(tops[0], tops[1])
+
+    def finish_pair(pair, buffer, top):
+        first = list_ref[2 * pair]
+        second = list_ref[2 * pair + 1]
+        q = (first % SLOTS) // SOURCES
+        moment = jnp.zeros((EXTRA, 2 * LANES), jnp.float32)
+        for c in range(CHUNKS):
+            here = slice(c * (8 * ROWS // CHUNKS), (c + 1) * (8 * ROWS // CHUNKS))
+            weights = jnp.exp2((buffer[here, :] - top) * scale)
+            high = weights.astype(jnp.bfloat16)
+            low = (weights - high.astype(jnp.float32)).astype(jnp.bfloat16)
+            geometry = g_ref[q, :, here]
+            moment += jnp.dot(geometry, high, preferred_element_type=jnp.float32)
+            moment += jnp.dot(geometry, low, preferred_element_type=jnp.float32)
+        softened = moment / moment[6:7]
+        block_of(first, softened[:, 0:LANES])
+        block_of(second, softened[:, LANES:])
+
+    pairs = n // 2
+    for extra in range(4):
+        list_ref[n + extra] = jnp.int32(SLOTS)
+
+    def two(t, top):
+        pair = 2 * t
+        next_top = score(pair + 1, odd_ref)
+        finish_pair(pair, even_ref, top)
+
+        def go_on():
+            after = score(pair + 2, even_ref)
+            finish_pair(pair + 1, odd_ref, next_top)
+            return after
+
+        return lax.cond(pair + 1 < pairs, go_on, lambda: next_top)
+
+    lax.fori_loop(0, (pairs + 1) // 2, two, score(0, even_ref))
 
     col = lax.broadcasted_iota(jnp.int32, (16, LANES), 0)
     lane = lax.broadcasted_iota(jnp.int32, (16, LANES), 1)
@@ -181,6 +214,27 @@
     return jnp.sum(jnp.where(at[None, :] == ids[:, None], table[None, :], 0), axis=1)
 
 
+def attend_call(scale, *operands):
+    smem = pl.BlockSpec(memory_space=pltpu.SMEM)
+    vmem = pl.BlockSpec(memory_space=pltpu.VMEM)
+    return pl.pallas_call(
+        lambda *refs: attend_kernel(scale, *refs),
+        out_shape=jax.ShapeDtypeStruct((SIDE * SIDE, 2, LANES), jnp.float32),
+        in_specs=[smem, smem, vmem, vmem, vmem, vmem, vmem],
+        out_specs=vmem,
+        scratch_shapes=[
+            pltpu.VMEM((SOURCES, PACKED, WIDTH), jnp.bfloat16),
+            pltpu.VMEM((QUADS, EXTRA, 8 * LANES), jnp.bfloat16),
+            pltpu.VMEM((SLOTS + 1, 16, 16), jnp.float32),
+            pltpu.SMEM((SLOTS + 16,), jnp.int32),
+            pltpu.VMEM((8 * ROWS, 2 * LANES), jnp.float32),
+            pltpu.VMEM((8 * ROWS, 2 * LANES), jnp.float32),
+        ],
+        compiler_params=pltpu.CompilerParams(vmem_limit_bytes=48 * 1024 * 1024),
+        name="attend",
+    )(*operands)
+
+
 def per_device(descriptors, points, normals, pair_list, intersection, pose_index):
     own = lax.axis_index("pair")
     z, y = own // SIDE, own % SIDE
@@ -227,20 +281,7 @@
     smem = pl.BlockSpec(memory_space=pltpu.SMEM)
     vmem = pl.BlockSpec(memory_space=pltpu.VMEM)
     scale = WIDTH**-0.5 / math.log(2.0)
-    send = pl.pallas_call(
-        lambda *refs: attend_kernel(scale, *refs),
-        out_shape=jax.ShapeDtypeStruct((SIDE * SIDE, 2, LANES), jnp.float32),
-        in_specs=[smem, smem, vmem, vmem, vmem, vmem, vmem],
-        out_specs=vmem,
-        scratch_shapes=[
-            pltpu.VMEM((SOURCES, PACKED, WIDTH), jnp.bfloat16),
-            pltpu.VMEM((QUADS, EXTRA, 8 * LANES), jnp.bfloat16),
-            pltpu.VMEM((SLOTS + 1, 16, 16), jnp.float32),
-            pltpu.SMEM((SLOTS + 8,), jnp.int32),
-        ],
-        compiler_params=pltpu.CompilerParams(vmem_limit_bytes=48 * 1024 * 1024),
-        name="attend",
-    )(task_counts, base, destinations, sources_row, sources_next, targets_mine, targets_peer)
+    send = attend_call(scale, task_counts, base, destinations, sources_row, sources_next, targets_mine, targets_peer)
     got = lax.all_to_all(send, "pair", split_axis=0, concat_axis=0, tiled=True)
 
     my_targets = lax.dynamic_slice_in_dim(pair_list[:, 1], own * PAIRS_PER, PAIRS_PER, 0)

time: 145 us -> 130 us (0.90)
  Pallas kernels: 26.8 us -> 14.9 us
  starting transfers between devices: 47.6 us -> 45.9 us
    pallas_call x1, Pallas kernels: 23.5 us -> 11.5 us  [attend_call(): pl.pallas_call(lambda *refs: attend_kernel(scale, *refs), out_shape=jax.S...]
    all_to_all x1, starting transfers between devices: 11.3 us -> 9.62 us  [per_device(): got = lax.all_to_all(send, 'pair', split_axis=0, concat_axis=0, tiled=True)]
where the time goes in v3:
time: 130 us
  starting transfers between devices  45.9 us (35%)
  waiting for transfers between devices  31.6 us (24%)
  blocking collectives  30.6 us (24%)
  Pallas kernels  14.9 us (11%)
  other arithmetic  4.1 us (3%)
  local copies, waits for them, and re-layouts  1.81 us (1%)
    ppermute x3, starting transfers between devices, per_device(): lax.ppermute(packed, 'pair', from_ahead(2 * q))  17.6 us
    all_to_all x1, blocking collectives, to_each(): lax.all_to_all(copies, axis, split_axis=0, concat_axis=0, tiled=True, axi...  17.4 us
    all_to_all x1, blocking collectives, per_device(): lax.all_to_all(share, 'split', split_axis=0, concat_axis=0, tiled=True)  13.2 us
    pallas_call x1, Pallas kernels, attend_call(): pl.pallas_call(lambda *refs: attend_kernel(scale, *refs), out_shape=jax.S...  11.5 us
    all_to_all x1, waiting for transfers between devices, per_device(): got = lax.all_to_all(send, 'pair', split_axis=0, concat_axis=0, tiled=True)  10.6 us
    all_to_all x1, starting transfers between devices, per_device(): got = lax.all_to_all(send, 'pair', split_axis=0, concat_axis=0, tiled=True)  9.62 us
    all_to_all x1, waiting for transfers between devices, to_each(): lax.all_to_all(copies, axis, split_axis=0, concat_axis=0, tiled=True, axi...  9.6 us
    ppermute x1, waiting for transfers between devices, per_device(): sources_next = lax.ppermute(sources_row, 'pair', z_swap)  9.31 us
  transfers between devices with their start and end apart: 7, of which 5 were waited for; matrix products, arithmetic and copies ran while one was open for 2% of the time, Pallas kernels for 0%

profile of v3, /device:TPU:1, one launch (start us, length us, event | category | flops | bytes accessed | tf_op | source)
XLA Modules:
  0.0 129.7 jit_solution(609419157036029167)
XLA Ops:
  0.6 0.7 convert_bitcast_fusion
  1.3 0.9 maximum_maximum_fusion
  2.2 11.5 %collective-permute-start.2 = (bf16[136,256]{1,0:T(8,128)(2,1)S(1)}, bf16[136,256]{1,0:T(8,128)(2,1)S(1)}, u32[]{:S(2)}, u32[]{:S(2)}) collective-permute-start(bf16[136,256]{1,0:T(8,128)(2,1)S(1)} %maximum_maximum_fusion), channel_id=1, source_target_pairs={{256,0},{264,8},{272,16},{280,24},{288,32},{296,40},{304,48},{312,... | collective-permute-start | bytes 208904 | tf_op jit(solution)/shard_map/ppermute | solution.py:253
  13.7 1.9 %collective-permute-start.1 = (bf16[136,256]{1,0:T(8,128)(2,1)S(1)}, bf16[136,256]{1,0:T(8,128)(2,1)S(1)}, u32[]{:S(2)}, u32[]{:S(2)}) collective-permute-start(bf16[136,256]{1,0:T(8,128)(2,1)S(1)} %maximum_maximum_fusion), channel_id=1, source_target_pairs={{128,0},{136,8},{144,16},{152,24},{160,32},{168,40},{176,48},{184,... | collective-permute-start | bytes 208904 | tf_op jit(solution)/shard_map/ppermute | solution.py:253
  15.6 4.2 %collective-permute-start.3 = (bf16[136,256]{1,0:T(8,128)(2,1)S(1)}, bf16[136,256]{1,0:T(8,128)(2,1)S(1)}, u32[]{:S(2)}, u32[]{:S(2)}) collective-permute-start(bf16[136,256]{1,0:T(8,128)(2,1)S(1)} %maximum_maximum_fusion), channel_id=1, source_target_pairs={{384,0},{392,8},{400,16},{408,24},{416,32},{424,40},{432,48},{440,... | collective-permute-start | bytes 208904 | tf_op jit(solution)/shard_map/ppermute | solution.py:253
  19.9 0.9 fusion.22
  20.8 1.7 %collective-permute-done.1 = bf16[136,256]{1,0:T(8,128)(2,1)S(1)} collective-permute-done((bf16[136,256]{1,0:T(8,128)(2,1)S(1)}, bf16[136,256]{1,0:T(8,128)(2,1)S(1)}, u32[]{:S(2)}, u32[]{:S(2)}) %collective-permute-start.1) | collective-permute-done | bytes 69664 | tf_op jit(solution)/shard_map/ppermute | solution.py:253
  22.5 0.4 collective-permute-done.3
  23.0 17.4 %all_to_all.20.refs_5_ = bf16[4,4,136,256]{3,2,1,0:T(8,128)(2,1)S(1)} all-to-all(bf16[4,4,136,256]{3,2,1,0:T(8,128)(2,1)S(1)} %broadcast_in_dim.66), channel_id=1, replica_groups={{0,2,4,6},{1,3,5,7},{8,10,12,14},{9,11,13,15},{16,18,20,22},{17,19,21,2..., dimensions={0} | all-to-all | bytes 2228224 | tf_op jit(solution)/shard_map/all_to_all | solution.py:37
  40.4 0.8 broadcast_in_dim.61
  41.2 6.8 %all-to-all-start = ((bf16[8,136,256]{2,1,0:T(8,128)(2,1)}), bf16[8,136,256]{2,1,0:T(8,128)(2,1)S(1)}, u32[]{:S(2)}, u32[]{:S(2)}) async-start(bf16[8,136,256]{2,1,0:T(8,128)(2,1)} %broadcast_in_dim.61), calls=%async_computation | async-start | bytes 1114112 | tf_op jit(solution)/shard_map/all_to_all | solution.py:37
  48.4 5.4 %collective-permute-start.4 = (bf16[4,4,136,256]{3,2,1,0:T(8,128)(2,1)S(1)}, bf16[4,4,136,256]{3,2,1,0:T(8,128)(2,1)S(1)}, u32[]{:S(2)}, u32[]{:S(2)}) collective-permute-start(bf16[4,4,136,256]{3,2,1,0:T(8,128)(2,1)S(1)} %all_to_all.20.refs_5_), channel_id=1, source_target_pairs={{0,1},{1,0},{2,3},{3,2},{4,5},{5,4},{6,7},{7,6},{8,9},{9,8},{10,11... | collective-permute-start | bytes 3342344 | tf_op jit(solution)/shard_map/ppermute | solution.py:256
  53.9 9.6 %all-to-all-done.refs_3_ = bf16[8,136,256]{2,1,0:T(8,128)(2,1)S(1)} async-done(((bf16[8,136,256]{2,1,0:T(8,128)(2,1)}), bf16[8,136,256]{2,1,0:T(8,128)(2,1)S(1)}, u32[]{:S(2)}, u32[]{:S(2)}) %all-to-all-start) | async-done | bytes 557088 | tf_op jit(solution)/shard_map/all_to_all | solution.py:37
  63.5 6.5 %collective-permute-start = (bf16[8,136,256]{2,1,0:T(8,128)(2,1)S(1)}, bf16[8,136,256]{2,1,0:T(8,128)(2,1)S(1)}, u32[]{:S(2)}, u32[]{:S(2)}) collective-permute-start(bf16[8,136,256]{2,1,0:T(8,128)(2,1)S(1)} %all-to-all-done.refs_3_), channel_id=1, source_target_pairs={{0,64},{8,72},{16,80},{24,88},{32,96},{40,104},{48,112},{56,120},{... | collective-permute-start | bytes 1671176 | tf_op jit(solution)/shard_map/ppermute | solution.py:255
  70.0 0.5 and_select_fusion.7
  70.6 9.3 %collective-permute-done.refs_4_ = bf16[8,136,256]{2,1,0:T(8,128)(2,1)S(1)} collective-permute-done((bf16[8,136,256]{2,1,0:T(8,128)(2,1)S(1)}, bf16[8,136,256]{2,1,0:T(8,128)(2,1)S(1)}, u32[]{:S(2)}, u32[]{:S(2)}) %collective-permute-start) | collective-permute-done | bytes 557088 | tf_op jit(solution)/shard_map/ppermute | solution.py:255
  80.3 11.5 %attend.1 = f32[64,2,128]{2,1,0:T(2,128)} custom-call(s32[128]{0:T(128)S(1)} %pad.9.refs_0_, s32[1]{0:T(128)} %bitcast.9.refs_1_, s32[8,64]{1,0:T(8,128)S(1)} %stack.44.refs_2_, bf16[8,136,256]{2,1,0:T(8,128)(2,1)S(1)} %all-to-all-done.refs_3_, bf16[8,136,256]{2,1,0:T(8,128)(2,1)S(1)} %collective-permute-done.refs_4_, ...), custom_call_target="tpu_custom_call" | custom-call | tf_op jit(solution)/shard_map/attend/pallas_call | solution.py:220
  91.7 9.6 %all-to-all-start.2 = ((f32[64,2,128]{2,1,0:T(2,128)}), f32[64,2,128]{2,1,0:T(2,128)S(1)}, u32[]{:S(2)}, u32[]{:S(2)}) async-start(f32[64,2,128]{2,1,0:T(2,128)} %attend.1), calls=%async_computation.2 | async-start | bytes 131072 | tf_op jit(solution)/shard_map/all_to_all | solution.py:285
  101.4 0.5 fusion.8.group_ref
  101.9 10.6 %all-to-all-done.2.got_ref = f32[64,2,128]{2,1,0:T(2,128)S(1)} async-done(((f32[64,2,128]{2,1,0:T(2,128)}), f32[64,2,128]{2,1,0:T(2,128)S(1)}, u32[]{:S(2)}, u32[]{:S(2)}) %all-to-all-start.2) | async-done | bytes 65568 | tf_op jit(solution)/shard_map/all_to_all | solution.py:285
  112.5 0.6 copy-done
  113.1 1.8 %collect.1 = f32[8,32,128]{2,1,0:T(8,128)} custom-call(s32[24]{0:T(128)} %fusion.8.group_ref, s32[24]{0:T(128)} %get-tuple-element.11.quad_ref, f32[64,2,128]{2,1,0:T(2,128)} %copy-done), custom_call_target="tpu_custom_call" | custom-call | tf_op jit(solution)/shard_map/collect/pallas_call | solution.py:292
  114.8 13.2 %all_to_all.21.refs_0_ = f32[8,32,128]{2,1,0:T(8,128)} all-to-all(f32[8,32,128]{2,1,0:T(8,128)} %collect.1), channel_id=1, replica_groups=mesh['pair'=64,'split'=8] {'split'}, dimensions={0} | all-to-all | bytes 262144 | tf_op jit(solution)/shard_map/all_to_all | solution.py:300
  128.0 1.6 %finish.1 = (f32[6,6,24]{2,1,0:T(8,128)}, f32[6,1,6]{2,1,0:T(1,128)}, f32[1,6]{1,0:T(1,128)}) custom-call(f32[8,32,128]{2,1,0:T(8,128)} %all_to_all.21.refs_0_), custom_call_target="tpu_custom_call" | custom-call | tf_op jit(solution)/shard_map/finish/pallas_call | solution.py:303
  (30 shorter events, 1.0 us)
Async XLA Ops:
  2.2 18.6 %collective-permute-start.2 = (bf16[136,256]{1,0:T(8,128)(2,1)S(1)}, bf16[136,256]{1,0:T(8,128)(2,1)S(1)}, u32[]{:S(2)}, u32[]{:S(2)}) collective-permute-start(bf16[136,256]{1,0:T(8,128)(2,1)S(1)} %maximum_maximum_fusion), channel_id=1, source_target_pairs={{256,0},{264,8},{272,16},{280,24},{288,32},{296,40},{304,48},{312,... | collective-permute-start | bytes 208904 | tf_op jit(solution)/shard_map/ppermute | solution.py:253
  13.7 8.8 %collective-permute-start.1 = (bf16[136,256]{1,0:T(8,128)(2,1)S(1)}, bf16[136,256]{1,0:T(8,128)(2,1)S(1)}, u32[]{:S(2)}, u32[]{:S(2)}) collective-permute-start(bf16[136,256]{1,0:T(8,128)(2,1)S(1)} %maximum_maximum_fusion), channel_id=1, source_target_pairs={{128,0},{136,8},{144,16},{152,24},{160,32},{168,40},{176,48},{184,... | collective-permute-start | bytes 208904 | tf_op jit(solution)/shard_map/ppermute | solution.py:253
  15.6 7.2 %collective-permute-start.3 = (bf16[136,256]{1,0:T(8,128)(2,1)S(1)}, bf16[136,256]{1,0:T(8,128)(2,1)S(1)}, u32[]{:S(2)}, u32[]{:S(2)}) collective-permute-start(bf16[136,256]{1,0:T(8,128)(2,1)S(1)} %maximum_maximum_fusion), channel_id=1, source_target_pairs={{384,0},{392,8},{400,16},{408,24},{416,32},{424,40},{432,48},{440,... | collective-permute-start | bytes 208904 | tf_op jit(solution)/shard_map/ppermute | solution.py:253
  40.4 7.7 %copy-start.1 = (s32[1536,2]{0,1:T(2,128)S(1)}, s32[1536,2]{0,1:T(2,128)}, u32[]{:S(2)}) copy-start(s32[1536,2]{0,1:T(2,128)} %param.9) | copy-start | bytes 36868
  40.4 7.8 %copy-start.2 = (s32[64]{0:T(128)S(1)}, s32[64]{0:T(128)}, u32[]{:S(2)}) copy-start(s32[64]{0:T(128)} %param.11) | copy-start | bytes 772
  41.2 22.3 %all-to-all-start = ((bf16[8,136,256]{2,1,0:T(8,128)(2,1)}), bf16[8,136,256]{2,1,0:T(8,128)(2,1)S(1)}, u32[]{:S(2)}, u32[]{:S(2)}) async-start(bf16[8,136,256]{2,1,0:T(8,128)(2,1)} %broadcast_in_dim.61), calls=%async_computation | async-start | bytes 1114112 | tf_op jit(solution)/shard_map/all_to_all | solution.py:37
  48.4 31.8 %collective-permute-start.4 = (bf16[4,4,136,256]{3,2,1,0:T(8,128)(2,1)S(1)}, bf16[4,4,136,256]{3,2,1,0:T(8,128)(2,1)S(1)}, u32[]{:S(2)}, u32[]{:S(2)}) collective-permute-start(bf16[4,4,136,256]{3,2,1,0:T(8,128)(2,1)S(1)} %all_to_all.20.refs_5_), channel_id=1, source_target_pairs={{0,1},{1,0},{2,3},{3,2},{4,5},{5,4},{6,7},{7,6},{8,9},{9,8},{10,11... | collective-permute-start | bytes 3342344 | tf_op jit(solution)/shard_map/ppermute | solution.py:256
  63.5 16.4 %collective-permute-start = (bf16[8,136,256]{2,1,0:T(8,128)(2,1)S(1)}, bf16[8,136,256]{2,1,0:T(8,128)(2,1)S(1)}, u32[]{:S(2)}, u32[]{:S(2)}) collective-permute-start(bf16[8,136,256]{2,1,0:T(8,128)(2,1)S(1)} %all-to-all-done.refs_3_), channel_id=1, source_target_pairs={{0,64},{8,72},{16,80},{24,88},{32,96},{40,104},{48,112},{56,120},{... | collective-permute-start | bytes 1671176 | tf_op jit(solution)/shard_map/ppermute | solution.py:255
  91.7 20.7 %all-to-all-start.2 = ((f32[64,2,128]{2,1,0:T(2,128)}), f32[64,2,128]{2,1,0:T(2,128)S(1)}, u32[]{:S(2)}, u32[]{:S(2)}) async-start(f32[64,2,128]{2,1,0:T(2,128)} %attend.1), calls=%async_computation.2 | async-start | bytes 131072 | tf_op jit(solution)/shard_map/all_to_all | solution.py:285
  112.5 0.6 copy-start

commit v4 on v3

--- a/solution.py
+++ b/solution.py
@@ -23,13 +23,16 @@
 HIGHEST = lax.Precision.HIGHEST
 
 y_groups = [[z * SIDE + y for y in range(SIDE)] for z in range(SIDE)]
-x_groups = [[2 * x + core for x in range(4)] for core in range(2)]
 z_swap = [(z * SIDE + y, (z ^ 1) * SIDE + y) for z in range(SIDE) for y in range(SIDE)]
 core_swap = [(s, s ^ 1) for s in range(8)]
 
 
 def from_ahead(steps):
     return [(((z + steps) % SIDE) * SIDE + y, z * SIDE + y) for z in range(SIDE) for y in range(SIDE)]
+
+
+def x_ahead(steps):
+    return [((x + steps) % 4 * 2 + core, x * 2 + core) for x in range(4) for core in range(2)]
 
 
 def to_each(block, axis, groups):
@@ -51,14 +54,13 @@
     ]
 
 
-def attend_kernel(scale, cnt_ref, base_ref, dst_ref, a1_ref, a2_ref, b1_ref, b2_ref, out_ref, a_ref, g_ref, h_ref, list_ref, even_ref, odd_ref):
+def attend_kernel(scale, cnt_ref, base_ref, dst_ref, a1_ref, a2_ref, *rest):
+    b_refs, (out_ref, a_ref, g_ref, h_ref, list_ref, even_ref, odd_ref) = rest[:8], rest[8:]
     a_ref[0:SIDE] = a1_ref[...]
     a_ref[SIDE:SOURCES] = a2_ref[...]
     for q in range(QUADS):
-        for c, ref in enumerate((b1_ref, b2_ref)):
-            for x in range(4):
-                at = (c * 4 + x) * LANES
-                g_ref[q, :, at : at + LANES] = ref[x, q, ROWS:PACKED, 0:LANES]
+        for x, ref in enumerate(b_refs):
+            g_ref[q, :, x * LANES : (x + 1) * LANES] = ref[q, ROWS:PACKED, 0:LANES]
     h_ref[...] = jnp.zeros_like(h_ref)
 
     n = jnp.int32(0)
@@ -104,8 +106,8 @@
             [a_ref[first % SOURCES, 0:ROWS, :], a_ref[second % SOURCES, 0:ROWS, :]], axis=0
         )
         tops = []
-        for c, ref in enumerate((b1_ref, b2_ref)):
-            keys = jnp.concatenate([ref[x, q, 0:ROWS, :] for x in range(4)], axis=0)
+        for c in range(2):
+            keys = jnp.concatenate([ref[q, 0:ROWS, :] for ref in b_refs[4 * c : 4 * c + 4]], axis=0)
             part = nt(keys, queries)
             buffer[c * 4 * ROWS : (c + 1) * 4 * ROWS, :] = part
             tops.append(jnp.max(part, axis=0, keepdims=True))
@@ -220,7 +222,7 @@
     return pl.pallas_call(
         lambda *refs: attend_kernel(scale, *refs),
         out_shape=jax.ShapeDtypeStruct((SIDE * SIDE, 2, LANES), jnp.float32),
-        in_specs=[smem, smem, vmem, vmem, vmem, vmem, vmem],
+        in_specs=[smem, smem] + [vmem] * 11,
         out_specs=vmem,
         scratch_shapes=[
             pltpu.VMEM((SOURCES, PACKED, WIDTH), jnp.bfloat16),
@@ -251,9 +253,12 @@
 
     sources_row = to_each(packed, "pair", y_groups)
     targets_quad = jnp.stack([packed] + [lax.ppermute(packed, "pair", from_ahead(2 * q)) for q in range(1, QUADS)])
-    targets_mine = to_each(targets_quad, "split", x_groups)
+    quarters, peers = [targets_quad], []
+    for d in (1, 2, 3):
+        quarters.append(lax.ppermute(targets_quad, "split", x_ahead(d)))
     sources_next = lax.ppermute(sources_row, "pair", z_swap)
-    targets_peer = lax.ppermute(targets_mine, "split", core_swap)
+    for d in range(4):
+        peers.append(lax.ppermute(quarters[d], "split", core_swap))
 
     all_targets = pair_list[:, 1].reshape(SIDE, SIDE, PAIRS_PER)
     task_targets = jnp.concatenate(
@@ -262,8 +267,7 @@
     quads = jnp.arange(QUADS, dtype=jnp.int32)
     target_ids = (z + 2 * quads) % SIDE * SIDE + y
     is_task = task_targets[None, :, :] == target_ids[:, None, None]
-    next_counts = sources_next[:, ROWS + 6 :, LANES:]
-    both = jnp.concatenate([sources_row[:, ROWS + 6 :, LANES:], next_counts], axis=0)
+    both = jnp.concatenate([sources_row[:, ROWS + 6 :, LANES:], sources_next[:, ROWS + 6 :, LANES:]], axis=0)
     both = both[:, :, :PAIRS_PER].astype(jnp.float32)
     seen_rows = (both[:, 0] * 16 + both[:, 1]).astype(jnp.int32)
     task_counts = jnp.sum(jnp.where(is_task, seen_rows[None], 0), axis=2).reshape(SLOTS)
@@ -281,7 +285,7 @@
     smem = pl.BlockSpec(memory_space=pltpu.SMEM)
     vmem = pl.BlockSpec(memory_space=pltpu.VMEM)
     scale = WIDTH**-0.5 / math.log(2.0)
-    send = attend_call(scale, task_counts, base, destinations, sources_row, sources_next, targets_mine, targets_peer)
+    send = attend_call(scale, task_counts, base, destinations, sources_row, sources_next, *quarters, *peers)
     got = lax.all_to_all(send, "pair", split_axis=0, concat_axis=0, tiled=True)
 
     my_targets = lax.dynamic_slice_in_dim(pair_list[:, 1], own * PAIRS_PER, PAIRS_PER, 0)

time: 130 us -> 108 us (0.83)
  waiting for transfers between devices: 31.6 us -> 11.7 us
  blocking collectives: 30.6 us -> 10.8 us
  starting transfers between devices: 45.9 us -> 61.9 us
  local copies, waits for them, and re-layouts: 1.81 us -> 3.72 us
    all_to_all x1 -> x0, blocking collectives: 17.4 us -> none  [to_each(): lax.all_to_all(copies, axis, split_axis=0, concat_axis=0, tiled=True, axi...]
    ppermute x1 -> x7, starting transfers between devices: 5.38 us -> 22.3 us  [the longest x4 11.7 us: per_device(): peers.append(lax.ppermute(quarters[d], 'split', core_swap))]
    all_to_all x1, waiting for transfers between devices: 9.6 us -> 0.01 us  [to_each(): lax.all_to_all(copies, axis, split_axis=0, concat_axis=0, tiled=True, axi...]
    ppermute x1, waiting for transfers between devices: 9.31 us -> 0.01 us  [per_device(): sources_next = lax.ppermute(sources_row, 'pair', z_swap)]
    ppermute x1, starting transfers between devices: 6.46 us -> 3.94 us  [per_device(): sources_next = lax.ppermute(sources_row, 'pair', z_swap)]
    all_to_all x1, blocking collectives: 13.2 us -> 10.8 us  [per_device(): lax.all_to_all(share, 'split', split_axis=0, concat_axis=0, tiled=True)]
    ppermute x3, waiting for transfers between devices: 2.1 us -> 0.01 us  [per_device(): lax.ppermute(packed, 'pair', from_ahead(2 * q))]
    unnamed x6 -> x12, local copies, waits for them, and re-layouts: 0.63 us -> 2.62 us
  transfers between devices with their start and end apart: 7 -> 13, of which waited for: 5 -> 2; matrix products, arithmetic and copies ran while one was open for 2% -> 2% of each run, Pallas kernels for 0% -> 0%
where the time goes in v4:
time: 108 us; the launch traced here: 107 us
  starting transfers between devices  61.9 us (57%)
  Pallas kernels  14.9 us (14%)
  waiting for transfers between devices  11.7 us (11%)
  blocking collectives  10.8 us (10%)
  local copies, waits for them, and re-layouts  3.72 us (3%)
  other arithmetic  3.18 us (3%)
    ppermute x3, starting transfers between devices, per_device(): lax.ppermute(packed, 'pair', from_ahead(2 * q))  16.8 us
    ppermute x4, starting transfers between devices, per_device(): peers.append(lax.ppermute(quarters[d], 'split', core_swap))  11.7 us
    pallas_call x1, Pallas kernels, attend_call(): pl.pallas_call(lambda *refs: attend_kernel(scale, *refs), out_shape=jax.S...  11.5 us
    all_to_all x1, starting transfers between devices, per_device(): got = lax.all_to_all(send, 'pair', split_axis=0, concat_axis=0, tiled=True)  11.2 us
    all_to_all x1, blocking collectives, per_device(): lax.all_to_all(share, 'split', split_axis=0, concat_axis=0, tiled=True)  10.8 us
    all_to_all x1, waiting for transfers between devices, per_device(): got = lax.all_to_all(send, 'pair', split_axis=0, concat_axis=0, tiled=True)  10.6 us
    ppermute x3, starting transfers between devices, per_device(): quarters.append(lax.ppermute(targets_quad, 'split', x_ahead(d)))  10.5 us
    all_to_all x1, starting transfers between devices, to_each(): lax.all_to_all(copies, axis, split_axis=0, concat_axis=0, tiled=True, axi...  7.64 us
  transfers between devices with their start and end apart: 13, of which 2 were waited for; matrix products, arithmetic and copies ran while one was open for 2% of the time, Pallas kernels for 0%

profile of v4, /device:TPU:1, one launch (start us, length us, event | category | flops | bytes accessed | tf_op | source)
XLA Modules:
  0.0 107.2 jit_solution(3961833627648152222)
XLA Ops:
  0.6 0.7 convert_bitcast_fusion
  2.0 0.8 maximum_maximum_fusion
  2.9 0.8 broadcast_in_dim.58
  3.7 7.6 %all-to-all-start = ((bf16[8,136,256]{2,1,0:T(8,128)(2,1)}), bf16[8,136,256]{2,1,0:T(8,128)(2,1)S(1)}, u32[]{:S(2)}, u32[]{:S(2)}) async-start(bf16[8,136,256]{2,1,0:T(8,128)(2,1)} %broadcast_in_dim.58), calls=%async_computation | async-start | bytes 1114112 | tf_op jit(solution)/shard_map/all_to_all | solution.py:40
  11.4 10.6 %collective-permute-start.2 = (bf16[136,256]{1,0:T(8,128)(2,1)S(1)}, bf16[136,256]{1,0:T(8,128)(2,1)S(1)}, u32[]{:S(2)}, u32[]{:S(2)}) collective-permute-start(bf16[136,256]{1,0:T(8,128)(2,1)S(1)} %maximum_maximum_fusion), channel_id=1, source_target_pairs={{256,0},{264,8},{272,16},{280,24},{288,32},{296,40},{304,48},{312,... | collective-permute-start | bytes 208904 | tf_op jit(solution)/shard_map/ppermute | solution.py:255
  22.0 1.9 %collective-permute-start.1 = (bf16[136,256]{1,0:T(8,128)(2,1)S(1)}, bf16[136,256]{1,0:T(8,128)(2,1)S(1)}, u32[]{:S(2)}, u32[]{:S(2)}) collective-permute-start(bf16[136,256]{1,0:T(8,128)(2,1)S(1)} %maximum_maximum_fusion), channel_id=1, source_target_pairs={{128,0},{136,8},{144,16},{152,24},{160,32},{168,40},{176,48},{184,... | collective-permute-start | bytes 208904 | tf_op jit(solution)/shard_map/ppermute | solution.py:255
  23.9 4.2 %collective-permute-start.3 = (bf16[136,256]{1,0:T(8,128)(2,1)S(1)}, bf16[136,256]{1,0:T(8,128)(2,1)S(1)}, u32[]{:S(2)}, u32[]{:S(2)}) collective-permute-start(bf16[136,256]{1,0:T(8,128)(2,1)S(1)} %maximum_maximum_fusion), channel_id=1, source_target_pairs={{384,0},{392,8},{400,16},{408,24},{416,32},{424,40},{432,48},{440,... | collective-permute-start | bytes 208904 | tf_op jit(solution)/shard_map/ppermute | solution.py:255
  28.2 0.7 copy-done.4
  29.2 0.6 copy-done.5
  30.1 3.9 %collective-permute-start = (bf16[8,136,256]{2,1,0:T(8,128)(2,1)S(1)}, bf16[8,136,256]{2,1,0:T(8,128)(2,1)S(1)}, u32[]{:S(2)}, u32[]{:S(2)}) collective-permute-start(bf16[8,136,256]{2,1,0:T(8,128)(2,1)S(1)} %all-to-all-done.refs_3_), channel_id=1, source_target_pairs={{0,64},{8,72},{16,80},{24,88},{32,96},{40,104},{48,112},{56,120},{... | collective-permute-start | bytes 1671176 | tf_op jit(solution)/shard_map/ppermute | solution.py:259
  34.1 3.1 %collective-permute-start.6 = (bf16[4,136,256]{2,1,0:T(8,128)(2,1)S(1)}, bf16[4,136,256]{2,1,0:T(8,128)(2,1)S(1)}, u32[]{:S(2)}, u32[]{:S(2)}) collective-permute-start(bf16[4,136,256]{2,1,0:T(8,128)(2,1)S(1)} %pad_maximum_fusion.refs_5_), channel_id=1, source_target_pairs={{6,0},{7,1},{0,2},{1,3},{2,4},{3,5},{4,6},{5,7},{14,8},{15,9},{8,1... | collective-permute-start | bytes 835592 | tf_op jit(solution)/shard_map/ppermute | solution.py:258
  37.2 4.4 %collective-permute-start.5 = (bf16[4,136,256]{2,1,0:T(8,128)(2,1)S(1)}, bf16[4,136,256]{2,1,0:T(8,128)(2,1)S(1)}, u32[]{:S(2)}, u32[]{:S(2)}) collective-permute-start(bf16[4,136,256]{2,1,0:T(8,128)(2,1)S(1)} %pad_maximum_fusion.refs_5_), channel_id=1, source_target_pairs={{4,0},{5,1},{6,2},{7,3},{0,4},{1,5},{2,6},{3,7},{12,8},{13,9},{14,... | collective-permute-start | bytes 835592 | tf_op jit(solution)/shard_map/ppermute | solution.py:258
  41.6 3.1 %collective-permute-start.4 = (bf16[4,136,256]{2,1,0:T(8,128)(2,1)S(1)}, bf16[4,136,256]{2,1,0:T(8,128)(2,1)S(1)}, u32[]{:S(2)}, u32[]{:S(2)}) collective-permute-start(bf16[4,136,256]{2,1,0:T(8,128)(2,1)S(1)} %pad_maximum_fusion.refs_5_), channel_id=1, source_target_pairs={{2,0},{3,1},{4,2},{5,3},{6,4},{7,5},{0,6},{1,7},{10,8},{11,9},{12,... | collective-permute-start | bytes 835592 | tf_op jit(solution)/shard_map/ppermute | solution.py:258
  45.3 4.0 %collective-permute-start.7 = (bf16[4,136,256]{2,1,0:T(8,128)(2,1)S(1)}, bf16[4,136,256]{2,1,0:T(8,128)(2,1)S(1)}, u32[]{:S(2)}, u32[]{:S(2)}) collective-permute-start(bf16[4,136,256]{2,1,0:T(8,128)(2,1)S(1)} %pad_maximum_fusion.refs_5_), channel_id=1, source_target_pairs={{0,1},{1,0},{2,3},{3,2},{4,5},{5,4},{6,7},{7,6},{8,9},{9,8},{10,11... | collective-permute-start | bytes 835592 | tf_op jit(solution)/shard_map/ppermute | solution.py:261
  49.3 1.9 %collective-permute-start.10 = (bf16[4,136,256]{2,1,0:T(8,128)(2,1)S(1)}, bf16[4,136,256]{2,1,0:T(8,128)(2,1)S(1)}, u32[]{:S(2)}, u32[]{:S(2)}) collective-permute-start(bf16[4,136,256]{2,1,0:T(8,128)(2,1)S(1)} %collective-permute-done.6.refs_8_), channel_id=1, source_target_pairs={{0,1},{1,0},{2,3},{3,2},{4,5},{5,4},{6,7},{7,6},{8,9},{9,8},{10,11... | collective-permute-start | bytes 835592 | tf_op jit(solution)/shard_map/ppermute | solution.py:261
  51.2 3.9 %collective-permute-start.9 = (bf16[4,136,256]{2,1,0:T(8,128)(2,1)S(1)}, bf16[4,136,256]{2,1,0:T(8,128)(2,1)S(1)}, u32[]{:S(2)}, u32[]{:S(2)}) collective-permute-start(bf16[4,136,256]{2,1,0:T(8,128)(2,1)S(1)} %collective-permute-done.5.refs_7_), channel_id=1, source_target_pairs={{0,1},{1,0},{2,3},{3,2},{4,5},{5,4},{6,7},{7,6},{8,9},{9,8},{10,11... | collective-permute-start | bytes 835592 | tf_op jit(solution)/shard_map/ppermute | solution.py:261
  55.1 1.9 %collective-permute-start.8 = (bf16[4,136,256]{2,1,0:T(8,128)(2,1)S(1)}, bf16[4,136,256]{2,1,0:T(8,128)(2,1)S(1)}, u32[]{:S(2)}, u32[]{:S(2)}) collective-permute-start(bf16[4,136,256]{2,1,0:T(8,128)(2,1)S(1)} %collective-permute-done.4.refs_6_), channel_id=1, source_target_pairs={{0,1},{1,0},{2,3},{3,2},{4,5},{5,4},{6,7},{7,6},{8,9},{9,8},{10,11... | collective-permute-start | bytes 835592 | tf_op jit(solution)/shard_map/ppermute | solution.py:261
  57.5 1.1 %collective-permute-done.8.refs_10_ = bf16[4,136,256]{2,1,0:T(8,128)(2,1)S(1)} collective-permute-done((bf16[4,136,256]{2,1,0:T(8,128)(2,1)S(1)}, bf16[4,136,256]{2,1,0:T(8,128)(2,1)S(1)}, u32[]{:S(2)}, u32[]{:S(2)}) %collective-permute-start.8) | collective-permute-done | bytes 278560 | tf_op jit(solution)/shard_map/ppermute | solution.py:261
  58.6 11.5 %attend.1 = f32[64,2,128]{2,1,0:T(2,128)} custom-call(s32[128]{0:T(128)S(1)} %pad.9.refs_0_, s32[1]{0:T(128)} %bitcast.9.refs_1_, s32[8,64]{1,0:T(8,128)S(1)} %stack.44.refs_2_, bf16[8,136,256]{2,1,0:T(8,128)(2,1)S(1)} %all-to-all-done.refs_3_, bf16[8,136,256]{2,1,0:T(8,128)(2,1)S(1)} %collective-permute-done.refs_4_, ...), custom_call_target="tpu_custom_call" | custom-call | tf_op jit(solution)/shard_map/attend/pallas_call | solution.py:222
  70.1 11.2 %all-to-all-start.1 = ((f32[64,2,128]{2,1,0:T(2,128)}), f32[64,2,128]{2,1,0:T(2,128)S(1)}, u32[]{:S(2)}, u32[]{:S(2)}) async-start(f32[64,2,128]{2,1,0:T(2,128)} %attend.1), calls=%async_computation.1 | async-start | bytes 131072 | tf_op jit(solution)/shard_map/all_to_all | solution.py:289
  81.9 10.6 %all-to-all-done.1.got_ref = f32[64,2,128]{2,1,0:T(2,128)S(1)} async-done(((f32[64,2,128]{2,1,0:T(2,128)}), f32[64,2,128]{2,1,0:T(2,128)S(1)}, u32[]{:S(2)}, u32[]{:S(2)}) %all-to-all-start.1) | async-done | bytes 65568 | tf_op jit(solution)/shard_map/all_to_all | solution.py:289
  93.0 1.8 %collect.1 = f32[8,32,128]{2,1,0:T(8,128)} custom-call(s32[24]{0:T(128)} %fusion.8.group_ref, s32[24]{0:T(128)} %get-tuple-element.11.quad_ref, f32[64,2,128]{2,1,0:T(2,128)} %copy-done), custom_call_target="tpu_custom_call" | custom-call | tf_op jit(solution)/shard_map/collect/pallas_call | solution.py:296
  94.8 10.8 %all_to_all.15.refs_0_ = f32[8,32,128]{2,1,0:T(8,128)} all-to-all(f32[8,32,128]{2,1,0:T(8,128)} %collect.1), channel_id=1, replica_groups=mesh['pair'=64,'split'=8] {'split'}, dimensions={0} | all-to-all | bytes 262144 | tf_op jit(solution)/shard_map/all_to_all | solution.py:304
  105.6 1.6 %finish.1 = (f32[6,6,24]{2,1,0:T(8,128)}, f32[6,1,6]{2,1,0:T(1,128)}, f32[1,6]{1,0:T(1,128)}) custom-call(f32[8,32,128]{2,1,0:T(8,128)} %all_to_all.15.refs_0_), custom_call_target="tpu_custom_call" | custom-call | tf_op jit(solution)/shard_map/finish/pallas_call | solution.py:307
  (46 shorter events, 3.3 us)
Async XLA Ops:
  1.3 0.7 copy-start.3
  1.3 0.7 copy-start.2
  3.7 26.3 %all-to-all-start = ((bf16[8,136,256]{2,1,0:T(8,128)(2,1)}), bf16[8,136,256]{2,1,0:T(8,128)(2,1)S(1)}, u32[]{:S(2)}, u32[]{:S(2)}) async-start(bf16[8,136,256]{2,1,0:T(8,128)(2,1)} %broadcast_in_dim.58), calls=%async_computation | async-start | bytes 1114112 | tf_op jit(solution)/shard_map/all_to_all | solution.py:40
  11.4 22.7 %collective-permute-start.2 = (bf16[136,256]{1,0:T(8,128)(2,1)S(1)}, bf16[136,256]{1,0:T(8,128)(2,1)S(1)}, u32[]{:S(2)}, u32[]{:S(2)}) collective-permute-start(bf16[136,256]{1,0:T(8,128)(2,1)S(1)} %maximum_maximum_fusion), channel_id=1, source_target_pairs={{256,0},{264,8},{272,16},{280,24},{288,32},{296,40},{304,48},{312,... | collective-permute-start | bytes 208904 | tf_op jit(solution)/shard_map/ppermute | solution.py:255
  22.0 12.1 %collective-permute-start.1 = (bf16[136,256]{1,0:T(8,128)(2,1)S(1)}, bf16[136,256]{1,0:T(8,128)(2,1)S(1)}, u32[]{:S(2)}, u32[]{:S(2)}) collective-permute-start(bf16[136,256]{1,0:T(8,128)(2,1)S(1)} %maximum_maximum_fusion), channel_id=1, source_target_pairs={{128,0},{136,8},{144,16},{152,24},{160,32},{168,40},{176,48},{184,... | collective-permute-start | bytes 208904 | tf_op jit(solution)/shard_map/ppermute | solution.py:255
  23.9 10.1 %collective-permute-start.3 = (bf16[136,256]{1,0:T(8,128)(2,1)S(1)}, bf16[136,256]{1,0:T(8,128)(2,1)S(1)}, u32[]{:S(2)}, u32[]{:S(2)}) collective-permute-start(bf16[136,256]{1,0:T(8,128)(2,1)S(1)} %maximum_maximum_fusion), channel_id=1, source_target_pairs={{384,0},{392,8},{400,16},{408,24},{416,32},{424,40},{432,48},{440,... | collective-permute-start | bytes 208904 | tf_op jit(solution)/shard_map/ppermute | solution.py:255
  28.2 0.7 copy-start.4
  28.2 1.0 copy-start.1
  29.2 0.7 copy-start.5
  30.1 27.0 %collective-permute-start = (bf16[8,136,256]{2,1,0:T(8,128)(2,1)S(1)}, bf16[8,136,256]{2,1,0:T(8,128)(2,1)S(1)}, u32[]{:S(2)}, u32[]{:S(2)}) collective-permute-start(bf16[8,136,256]{2,1,0:T(8,128)(2,1)S(1)} %all-to-all-done.refs_3_), channel_id=1, source_target_pairs={{0,64},{8,72},{16,80},{24,88},{32,96},{40,104},{48,112},{56,120},{... | collective-permute-start | bytes 1671176 | tf_op jit(solution)/shard_map/ppermute | solution.py:259
  34.1 15.1 %collective-permute-start.6 = (bf16[4,136,256]{2,1,0:T(8,128)(2,1)S(1)}, bf16[4,136,256]{2,1,0:T(8,128)(2,1)S(1)}, u32[]{:S(2)}, u32[]{:S(2)}) collective-permute-start(bf16[4,136,256]{2,1,0:T(8,128)(2,1)S(1)} %pad_maximum_fusion.refs_5_), channel_id=1, source_target_pairs={{6,0},{7,1},{0,2},{1,3},{2,4},{3,5},{4,6},{5,7},{14,8},{15,9},{8,1... | collective-permute-start | bytes 835592 | tf_op jit(solution)/shard_map/ppermute | solution.py:258
  37.2 14.0 %collective-permute-start.5 = (bf16[4,136,256]{2,1,0:T(8,128)(2,1)S(1)}, bf16[4,136,256]{2,1,0:T(8,128)(2,1)S(1)}, u32[]{:S(2)}, u32[]{:S(2)}) collective-permute-start(bf16[4,136,256]{2,1,0:T(8,128)(2,1)S(1)} %pad_maximum_fusion.refs_5_), channel_id=1, source_target_pairs={{4,0},{5,1},{6,2},{7,3},{0,4},{1,5},{2,6},{3,7},{12,8},{13,9},{14,... | collective-permute-start | bytes 835592 | tf_op jit(solution)/shard_map/ppermute | solution.py:258
  41.6 13.5 %collective-permute-start.4 = (bf16[4,136,256]{2,1,0:T(8,128)(2,1)S(1)}, bf16[4,136,256]{2,1,0:T(8,128)(2,1)S(1)}, u32[]{:S(2)}, u32[]{:S(2)}) collective-permute-start(bf16[4,136,256]{2,1,0:T(8,128)(2,1)S(1)} %pad_maximum_fusion.refs_5_), channel_id=1, source_target_pairs={{2,0},{3,1},{4,2},{5,3},{6,4},{7,5},{0,6},{1,7},{10,8},{11,9},{12,... | collective-permute-start | bytes 835592 | tf_op jit(solution)/shard_map/ppermute | solution.py:258
  45.3 12.2 %collective-permute-start.7 = (bf16[4,136,256]{2,1,0:T(8,128)(2,1)S(1)}, bf16[4,136,256]{2,1,0:T(8,128)(2,1)S(1)}, u32[]{:S(2)}, u32[]{:S(2)}) collective-permute-start(bf16[4,136,256]{2,1,0:T(8,128)(2,1)S(1)} %pad_maximum_fusion.refs_5_), channel_id=1, source_target_pairs={{0,1},{1,0},{2,3},{3,2},{4,5},{5,4},{6,7},{7,6},{8,9},{9,8},{10,11... | collective-permute-start | bytes 835592 | tf_op jit(solution)/shard_map/ppermute | solution.py:261
  49.3 8.2 %collective-permute-start.10 = (bf16[4,136,256]{2,1,0:T(8,128)(2,1)S(1)}, bf16[4,136,256]{2,1,0:T(8,128)(2,1)S(1)}, u32[]{:S(2)}, u32[]{:S(2)}) collective-permute-start(bf16[4,136,256]{2,1,0:T(8,128)(2,1)S(1)} %collective-permute-done.6.refs_8_), channel_id=1, source_target_pairs={{0,1},{1,0},{2,3},{3,2},{4,5},{5,4},{6,7},{7,6},{8,9},{9,8},{10,11... | collective-permute-start | bytes 835592 | tf_op jit(solution)/shard_map/ppermute | solution.py:261
  51.2 6.3 %collective-permute-start.9 = (bf16[4,136,256]{2,1,0:T(8,128)(2,1)S(1)}, bf16[4,136,256]{2,1,0:T(8,128)(2,1)S(1)}, u32[]{:S(2)}, u32[]{:S(2)}) collective-permute-start(bf16[4,136,256]{2,1,0:T(8,128)(2,1)S(1)} %collective-permute-done.5.refs_7_), channel_id=1, source_target_pairs={{0,1},{1,0},{2,3},{3,2},{4,5},{5,4},{6,7},{7,6},{8,9},{9,8},{10,11... | collective-permute-start | bytes 835592 | tf_op jit(solution)/shard_map/ppermute | solution.py:261
  55.1 3.5 %collective-permute-start.8 = (bf16[4,136,256]{2,1,0:T(8,128)(2,1)S(1)}, bf16[4,136,256]{2,1,0:T(8,128)(2,1)S(1)}, u32[]{:S(2)}, u32[]{:S(2)}) collective-permute-start(bf16[4,136,256]{2,1,0:T(8,128)(2,1)S(1)} %collective-permute-done.4.refs_6_), channel_id=1, source_target_pairs={{0,1},{1,0},{2,3},{3,2},{4,5},{5,4},{6,7},{7,6},{8,9},{9,8},{10,11... | collective-permute-start | bytes 835592 | tf_op jit(solution)/shard_map/ppermute | solution.py:261
  70.1 22.3 %all-to-all-start.1 = ((f32[64,2,128]{2,1,0:T(2,128)}), f32[64,2,128]{2,1,0:T(2,128)S(1)}, u32[]{:S(2)}, u32[]{:S(2)}) async-start(f32[64,2,128]{2,1,0:T(2,128)} %attend.1), calls=%async_computation.1 | async-start | bytes 131072 | tf_op jit(solution)/shard_map/all_to_all | solution.py:289
  92.4 0.6 copy-start

commit v5 on v4

--- a/solution.py
+++ b/solution.py
@@ -33,11 +33,6 @@
 
 def x_ahead(steps):
     return [((x + steps) % 4 * 2 + core, x * 2 + core) for x in range(4) for core in range(2)]
-
-
-def to_each(block, axis, groups):
-    copies = jnp.broadcast_to(block, (len(groups[0]), *block.shape))
-    return lax.all_to_all(copies, axis, split_axis=0, concat_axis=0, tiled=True, axis_index_groups=groups)
 
 
 def nt(left, right, precision=None):
@@ -216,6 +211,48 @@
     return jnp.sum(jnp.where(at[None, :] == ids[:, None], table[None, :], 0), axis=1)
 
 
+def pack_kernel(desc_ref, points_ref, normals_ref, count_ref, packed_ref, copies_ref):
+    count = count_ref[...]
+    high = (count // 16).astype(jnp.float32)
+    low = (count % 16).astype(jnp.float32)
+    blank = jnp.zeros((1, LANES - PAIRS_PER), jnp.float32)
+    right = jnp.concatenate(
+        [
+            jnp.zeros((6, LANES), jnp.float32),
+            jnp.concatenate([high, blank], axis=1),
+            jnp.concatenate([low, blank], axis=1),
+        ],
+        axis=0,
+    )
+    left = jnp.concatenate(
+        [
+            points_ref[...].astype(jnp.float32),
+            normals_ref[...].astype(jnp.float32),
+            jnp.ones((1, LANES), jnp.float32),
+            jnp.zeros((1, LANES), jnp.float32),
+        ],
+        axis=0,
+    )
+    extra = jnp.concatenate([left, right], axis=1).astype(jnp.bfloat16)
+    for ref in (packed_ref, *(copies_ref.at[i] for i in range(SIDE))):
+        ref[0:ROWS, :] = desc_ref[...]
+        ref[ROWS:PACKED, :] = extra
+
+
+def pack_call(*operands):
+    vmem = pl.BlockSpec(memory_space=pltpu.VMEM)
+    return pl.pallas_call(
+        pack_kernel,
+        out_shape=(
+            jax.ShapeDtypeStruct((PACKED, WIDTH), jnp.bfloat16),
+            jax.ShapeDtypeStruct((SIDE, PACKED, WIDTH), jnp.bfloat16),
+        ),
+        in_specs=[vmem] * 4,
+        out_specs=(vmem, vmem),
+        name="pack",
+    )(*operands)
+
+
 def attend_call(scale, *operands):
     smem = pl.BlockSpec(memory_space=pltpu.SMEM)
     vmem = pl.BlockSpec(memory_space=pltpu.VMEM)
@@ -243,15 +280,9 @@
     parity = z % 2
     other = z + 1 - 2 * parity
 
-    count_high = (intersection // 16).astype(jnp.bfloat16)
-    count_low = (intersection % 16).astype(jnp.bfloat16)
-    left = jnp.concatenate(
-        [points[0], normals[0], jnp.ones((1, ROWS), jnp.bfloat16), jnp.zeros((1, ROWS), jnp.bfloat16)], axis=0
-    )
-    counts = jnp.pad(jnp.stack([count_high, count_low]), ((6, 0), (0, LANES - PAIRS_PER)))
-    packed = jnp.concatenate([descriptors[0], jnp.concatenate([left, counts], axis=1)], axis=0)
-
-    sources_row = to_each(packed, "pair", y_groups)
+    packed, copies = pack_call(descriptors[0], points[0], normals[0], intersection.reshape(1, PAIRS_PER))
+
+    sources_row = lax.all_to_all(copies, "pair", split_axis=0, concat_axis=0, tiled=True, axis_index_groups=y_groups)
     targets_quad = jnp.stack([packed] + [lax.ppermute(packed, "pair", from_ahead(2 * q)) for q in range(1, QUADS)])
     quarters, peers = [targets_quad], []
     for d in (1, 2, 3):

time: 108 us -> 107 us (level)
  Pallas kernels: 14.9 us -> 16.6 us
  other arithmetic: 3.18 us -> 1.64 us
  local copies, waits for them, and re-layouts: 3.72 us -> 2.21 us
    pallas_call x0 -> x1, Pallas kernels: none -> 1.72 us  [pack_call(): pl.pallas_call(pack_kernel, out_shape=(jax.ShapeDtypeStruct((PACKED, WIDT...]
    ppermute x3, starting transfers between devices: 16.8 us -> 18 us  [per_device(): lax.ppermute(packed, 'pair', from_ahead(2 * q))]
    unnamed x12 -> x8, local copies, waits for them, and re-layouts: 2.62 us -> 1.96 us
where the time goes in v5:
time: 107 us; the launch traced here: 106 us
  starting transfers between devices  62 us (58%)
  Pallas kernels  16.6 us (16%)
  waiting for transfers between devices  11.7 us (11%)
  blocking collectives  10.8 us (10%)
  local copies, waits for them, and re-layouts  2.21 us (2%)
  other arithmetic  1.64 us (2%)
    ppermute x3, starting transfers between devices, per_device(): lax.ppermute(packed, 'pair', from_ahead(2 * q))  18 us
    ppermute x4, starting transfers between devices, per_device(): peers.append(lax.ppermute(quarters[d], 'split', core_swap))  11.7 us
    pallas_call x1, Pallas kernels, attend_call(): pl.pallas_call(lambda *refs: attend_kernel(scale, *refs), out_shape=jax.S...  11.5 us
    all_to_all x1, starting transfers between devices, per_device(): got = lax.all_to_all(send, 'pair', split_axis=0, concat_axis=0, tiled=True)  10.8 us
    all_to_all x1, blocking collectives, per_device(): lax.all_to_all(share, 'split', split_axis=0, concat_axis=0, tiled=True)  10.8 us
    all_to_all x1, waiting for transfers between devices, per_device(): got = lax.all_to_all(send, 'pair', split_axis=0, concat_axis=0, tiled=True)  10.6 us
    ppermute x3, starting transfers between devices, per_device(): quarters.append(lax.ppermute(targets_quad, 'split', x_ahead(d)))  10.5 us
    all_to_all x1, starting transfers between devices, per_device(): lax.all_to_all(copies, 'pair', split_axis=0, concat_axis=0, tiled=True, a...  7.77 us
  transfers between devices with their start and end apart: 13, of which 2 were waited for; matrix products, arithmetic and copies ran while one was open for 2% of the time, Pallas kernels for 0%

profile of v5, /device:TPU:1, one launch (start us, length us, event | category | flops | bytes accessed | tf_op | source)
XLA Modules:
  0.0 105.9 jit_solution(14177140683970293279)
XLA Ops:
  0.6 1.7 %pack.1 = (bf16[136,256]{1,0:T(8,128)(2,1)}, bf16[8,136,256]{2,1,0:T(8,128)(2,1)}) custom-call(bf16[128,256]{1,0:T(8,128)(2,1)} %bitcast.29, bf16[3,128]{1,0:T(4,128)(2,1)} %bitcast.33, bf16[3,128]{1,0:T(4,128)(2,1)} %bitcast.34, s32[1,24]{1,0:T(1,128)} %bitcast.35), custom_call_target="tpu_custom_call" | custom-call | tf_op jit(solution)/shard_map/pack/pallas_call | solution.py:244
  2.4 7.8 %all-to-all-start = ((bf16[8,136,256]{2,1,0:T(8,128)(2,1)}), bf16[8,136,256]{2,1,0:T(8,128)(2,1)S(1)}, u32[]{:S(2)}, u32[]{:S(2)}) async-start(bf16[8,136,256]{2,1,0:T(8,128)(2,1)} %get-tuple-element.8), calls=%async_computation | async-start | bytes 1114112 | tf_op jit(solution)/shard_map/all_to_all | solution.py:285
  10.1 5.8 %collective-permute-start.3 = (bf16[136,256]{1,0:T(8,128)(2,1)S(1)}, bf16[136,256]{1,0:T(8,128)(2,1)S(1)}, u32[]{:S(2)}, u32[]{:S(2)}) collective-permute-start(bf16[136,256]{1,0:T(8,128)(2,1)S(1)} %copy-done.1), channel_id=1, source_target_pairs={{384,0},{392,8},{400,16},{408,24},{416,32},{424,40},{432,48},{440,... | collective-permute-start | bytes 208904 | tf_op jit(solution)/shard_map/ppermute | solution.py:286
  15.9 8.8 %collective-permute-start.2 = (bf16[136,256]{1,0:T(8,128)(2,1)S(1)}, bf16[136,256]{1,0:T(8,128)(2,1)S(1)}, u32[]{:S(2)}, u32[]{:S(2)}) collective-permute-start(bf16[136,256]{1,0:T(8,128)(2,1)S(1)} %copy-done.1), channel_id=1, source_target_pairs={{256,0},{264,8},{272,16},{280,24},{288,32},{296,40},{304,48},{312,... | collective-permute-start | bytes 208904 | tf_op jit(solution)/shard_map/ppermute | solution.py:286
  24.8 3.4 %collective-permute-start.1 = (bf16[136,256]{1,0:T(8,128)(2,1)S(1)}, bf16[136,256]{1,0:T(8,128)(2,1)S(1)}, u32[]{:S(2)}, u32[]{:S(2)}) collective-permute-start(bf16[136,256]{1,0:T(8,128)(2,1)S(1)} %copy-done.1), channel_id=1, source_target_pairs={{128,0},{136,8},{144,16},{152,24},{160,32},{168,40},{176,48},{184,... | collective-permute-start | bytes 208904 | tf_op jit(solution)/shard_map/ppermute | solution.py:286
  28.2 0.7 copy-done.2
  29.2 0.6 copy-done.3
  30.0 3.1 %collective-permute-start = (bf16[8,136,256]{2,1,0:T(8,128)(2,1)S(1)}, bf16[8,136,256]{2,1,0:T(8,128)(2,1)S(1)}, u32[]{:S(2)}, u32[]{:S(2)}) collective-permute-start(bf16[8,136,256]{2,1,0:T(8,128)(2,1)S(1)} %all-to-all-done.refs_3_), channel_id=1, source_target_pairs={{0,64},{8,72},{16,80},{24,88},{32,96},{40,104},{48,112},{56,120},{... | collective-permute-start | bytes 1671176 | tf_op jit(solution)/shard_map/ppermute | solution.py:290
  33.2 3.1 %collective-permute-start.6 = (bf16[4,136,256]{2,1,0:T(8,128)(2,1)S(1)}, bf16[4,136,256]{2,1,0:T(8,128)(2,1)S(1)}, u32[]{:S(2)}, u32[]{:S(2)}) collective-permute-start(bf16[4,136,256]{2,1,0:T(8,128)(2,1)S(1)} %pad_maximum_fusion.refs_5_), channel_id=1, source_target_pairs={{6,0},{7,1},{0,2},{1,3},{2,4},{3,5},{4,6},{5,7},{14,8},{15,9},{8,1... | collective-permute-start | bytes 835592 | tf_op jit(solution)/shard_map/ppermute | solution.py:289
  36.4 4.4 %collective-permute-start.5 = (bf16[4,136,256]{2,1,0:T(8,128)(2,1)S(1)}, bf16[4,136,256]{2,1,0:T(8,128)(2,1)S(1)}, u32[]{:S(2)}, u32[]{:S(2)}) collective-permute-start(bf16[4,136,256]{2,1,0:T(8,128)(2,1)S(1)} %pad_maximum_fusion.refs_5_), channel_id=1, source_target_pairs={{4,0},{5,1},{6,2},{7,3},{0,4},{1,5},{2,6},{3,7},{12,8},{13,9},{14,... | collective-permute-start | bytes 835592 | tf_op jit(solution)/shard_map/ppermute | solution.py:289
  40.7 3.1 %collective-permute-start.4 = (bf16[4,136,256]{2,1,0:T(8,128)(2,1)S(1)}, bf16[4,136,256]{2,1,0:T(8,128)(2,1)S(1)}, u32[]{:S(2)}, u32[]{:S(2)}) collective-permute-start(bf16[4,136,256]{2,1,0:T(8,128)(2,1)S(1)} %pad_maximum_fusion.refs_5_), channel_id=1, source_target_pairs={{2,0},{3,1},{4,2},{5,3},{6,4},{7,5},{0,6},{1,7},{10,8},{11,9},{12,... | collective-permute-start | bytes 835592 | tf_op jit(solution)/shard_map/ppermute | solution.py:289
  43.9 0.5 and_select_fusion.5
  44.4 4.8 %collective-permute-start.7 = (bf16[4,136,256]{2,1,0:T(8,128)(2,1)S(1)}, bf16[4,136,256]{2,1,0:T(8,128)(2,1)S(1)}, u32[]{:S(2)}, u32[]{:S(2)}) collective-permute-start(bf16[4,136,256]{2,1,0:T(8,128)(2,1)S(1)} %pad_maximum_fusion.refs_5_), channel_id=1, source_target_pairs={{0,1},{1,0},{2,3},{3,2},{4,5},{5,4},{6,7},{7,6},{8,9},{9,8},{10,11... | collective-permute-start | bytes 835592 | tf_op jit(solution)/shard_map/ppermute | solution.py:292
  49.2 1.9 %collective-permute-start.10 = (bf16[4,136,256]{2,1,0:T(8,128)(2,1)S(1)}, bf16[4,136,256]{2,1,0:T(8,128)(2,1)S(1)}, u32[]{:S(2)}, u32[]{:S(2)}) collective-permute-start(bf16[4,136,256]{2,1,0:T(8,128)(2,1)S(1)} %collective-permute-done.6.refs_8_), channel_id=1, source_target_pairs={{0,1},{1,0},{2,3},{3,2},{4,5},{5,4},{6,7},{7,6},{8,9},{9,8},{10,11... | collective-permute-start | bytes 835592 | tf_op jit(solution)/shard_map/ppermute | solution.py:292
  51.2 3.1 %collective-permute-start.9 = (bf16[4,136,256]{2,1,0:T(8,128)(2,1)S(1)}, bf16[4,136,256]{2,1,0:T(8,128)(2,1)S(1)}, u32[]{:S(2)}, u32[]{:S(2)}) collective-permute-start(bf16[4,136,256]{2,1,0:T(8,128)(2,1)S(1)} %collective-permute-done.5.refs_7_), channel_id=1, source_target_pairs={{0,1},{1,0},{2,3},{3,2},{4,5},{5,4},{6,7},{7,6},{8,9},{9,8},{10,11... | collective-permute-start | bytes 835592 | tf_op jit(solution)/shard_map/ppermute | solution.py:292
  54.3 1.9 %collective-permute-start.8 = (bf16[4,136,256]{2,1,0:T(8,128)(2,1)S(1)}, bf16[4,136,256]{2,1,0:T(8,128)(2,1)S(1)}, u32[]{:S(2)}, u32[]{:S(2)}) collective-permute-start(bf16[4,136,256]{2,1,0:T(8,128)(2,1)S(1)} %collective-permute-done.4.refs_6_), channel_id=1, source_target_pairs={{0,1},{1,0},{2,3},{3,2},{4,5},{5,4},{6,7},{7,6},{8,9},{9,8},{10,11... | collective-permute-start | bytes 835592 | tf_op jit(solution)/shard_map/ppermute | solution.py:292
  56.6 1.1 %collective-permute-done.8.refs_10_ = bf16[4,136,256]{2,1,0:T(8,128)(2,1)S(1)} collective-permute-done((bf16[4,136,256]{2,1,0:T(8,128)(2,1)S(1)}, bf16[4,136,256]{2,1,0:T(8,128)(2,1)S(1)}, u32[]{:S(2)}, u32[]{:S(2)}) %collective-permute-start.8) | collective-permute-done | bytes 278560 | tf_op jit(solution)/shard_map/ppermute | solution.py:292
  57.7 11.5 %attend.1 = f32[64,2,128]{2,1,0:T(2,128)} custom-call(s32[128]{0:T(128)S(1)} %pad.4.refs_0_, s32[1]{0:T(128)} %bitcast.8.refs_1_, s32[8,64]{1,0:T(8,128)S(1)} %stack.32.refs_2_, bf16[8,136,256]{2,1,0:T(8,128)(2,1)S(1)} %all-to-all-done.refs_3_, bf16[8,136,256]{2,1,0:T(8,128)(2,1)S(1)} %collective-permute-done.refs_4_, ...), custom_call_target="tpu_custom_call" | custom-call | tf_op jit(solution)/shard_map/attend/pallas_call | solution.py:259
  69.2 10.8 %all-to-all-start.1 = ((f32[64,2,128]{2,1,0:T(2,128)}), f32[64,2,128]{2,1,0:T(2,128)S(1)}, u32[]{:S(2)}, u32[]{:S(2)}) async-start(f32[64,2,128]{2,1,0:T(2,128)} %attend.1), calls=%async_computation.1 | async-start | bytes 131072 | tf_op jit(solution)/shard_map/all_to_all | solution.py:320
  80.6 10.6 %all-to-all-done.1.got_ref = f32[64,2,128]{2,1,0:T(2,128)S(1)} async-done(((f32[64,2,128]{2,1,0:T(2,128)}), f32[64,2,128]{2,1,0:T(2,128)S(1)}, u32[]{:S(2)}, u32[]{:S(2)}) %all-to-all-start.1) | async-done | bytes 65568 | tf_op jit(solution)/shard_map/all_to_all | solution.py:320
  91.1 0.6 copy-done
  91.8 1.8 %collect.1 = f32[8,32,128]{2,1,0:T(8,128)} custom-call(s32[24]{0:T(128)} %fusion.2.group_ref, s32[24]{0:T(128)} %get-tuple-element.15.quad_ref, f32[64,2,128]{2,1,0:T(2,128)} %copy-done), custom_call_target="tpu_custom_call" | custom-call | tf_op jit(solution)/shard_map/collect/pallas_call | solution.py:327
  93.5 10.8 %all_to_all.15.refs_0_ = f32[8,32,128]{2,1,0:T(8,128)} all-to-all(f32[8,32,128]{2,1,0:T(8,128)} %collect.1), channel_id=1, replica_groups=mesh['pair'=64,'split'=8] {'split'}, dimensions={0} | all-to-all | bytes 262144 | tf_op jit(solution)/shard_map/all_to_all | solution.py:335
  104.3 1.6 %finish.1 = (f32[6,6,24]{2,1,0:T(8,128)}, f32[6,1,6]{2,1,0:T(1,128)}, f32[1,6]{1,0:T(1,128)}) custom-call(f32[8,32,128]{2,1,0:T(8,128)} %all_to_all.15.refs_0_), custom_call_target="tpu_custom_call" | custom-call | tf_op jit(solution)/shard_map/finish/pallas_call | solution.py:338
  (36 shorter events, 1.4 us)
Async XLA Ops:
  2.4 7.8 %copy-start.1 = (bf16[136,256]{1,0:T(8,128)(2,1)S(1)}, bf16[136,256]{1,0:T(8,128)(2,1)}, u32[]{:S(2)}) copy-start(bf16[136,256]{1,0:T(8,128)(2,1)} %get-tuple-element.9) | copy-start | bytes 208900
  2.4 27.7 %all-to-all-start = ((bf16[8,136,256]{2,1,0:T(8,128)(2,1)}), bf16[8,136,256]{2,1,0:T(8,128)(2,1)S(1)}, u32[]{:S(2)}, u32[]{:S(2)}) async-start(bf16[8,136,256]{2,1,0:T(8,128)(2,1)} %get-tuple-element.8), calls=%async_computation | async-start | bytes 1114112 | tf_op jit(solution)/shard_map/all_to_all | solution.py:285
  10.1 23.0 %collective-permute-start.3 = (bf16[136,256]{1,0:T(8,128)(2,1)S(1)}, bf16[136,256]{1,0:T(8,128)(2,1)S(1)}, u32[]{:S(2)}, u32[]{:S(2)}) collective-permute-start(bf16[136,256]{1,0:T(8,128)(2,1)S(1)} %copy-done.1), channel_id=1, source_target_pairs={{384,0},{392,8},{400,16},{408,24},{416,32},{424,40},{432,48},{440,... | collective-permute-start | bytes 208904 | tf_op jit(solution)/shard_map/ppermute | solution.py:286
  15.9 17.2 %collective-permute-start.2 = (bf16[136,256]{1,0:T(8,128)(2,1)S(1)}, bf16[136,256]{1,0:T(8,128)(2,1)S(1)}, u32[]{:S(2)}, u32[]{:S(2)}) collective-permute-start(bf16[136,256]{1,0:T(8,128)(2,1)S(1)} %copy-done.1), channel_id=1, source_target_pairs={{256,0},{264,8},{272,16},{280,24},{288,32},{296,40},{304,48},{312,... | collective-permute-start | bytes 208904 | tf_op jit(solution)/shard_map/ppermute | solution.py:286
  24.8 8.4 %collective-permute-start.1 = (bf16[136,256]{1,0:T(8,128)(2,1)S(1)}, bf16[136,256]{1,0:T(8,128)(2,1)S(1)}, u32[]{:S(2)}, u32[]{:S(2)}) collective-permute-start(bf16[136,256]{1,0:T(8,128)(2,1)S(1)} %copy-done.1), channel_id=1, source_target_pairs={{128,0},{136,8},{144,16},{152,24},{160,32},{168,40},{176,48},{184,... | collective-permute-start | bytes 208904 | tf_op jit(solution)/shard_map/ppermute | solution.py:286
  28.2 0.7 copy-start.2
  29.2 0.7 copy-start.3
  30.0 26.2 %collective-permute-start = (bf16[8,136,256]{2,1,0:T(8,128)(2,1)S(1)}, bf16[8,136,256]{2,1,0:T(8,128)(2,1)S(1)}, u32[]{:S(2)}, u32[]{:S(2)}) collective-permute-start(bf16[8,136,256]{2,1,0:T(8,128)(2,1)S(1)} %all-to-all-done.refs_3_), channel_id=1, source_target_pairs={{0,64},{8,72},{16,80},{24,88},{32,96},{40,104},{48,112},{56,120},{... | collective-permute-start | bytes 1671176 | tf_op jit(solution)/shard_map/ppermute | solution.py:290
  33.2 16.0 %collective-permute-start.6 = (bf16[4,136,256]{2,1,0:T(8,128)(2,1)S(1)}, bf16[4,136,256]{2,1,0:T(8,128)(2,1)S(1)}, u32[]{:S(2)}, u32[]{:S(2)}) collective-permute-start(bf16[4,136,256]{2,1,0:T(8,128)(2,1)S(1)} %pad_maximum_fusion.refs_5_), channel_id=1, source_target_pairs={{6,0},{7,1},{0,2},{1,3},{2,4},{3,5},{4,6},{5,7},{14,8},{15,9},{8,1... | collective-permute-start | bytes 835592 | tf_op jit(solution)/shard_map/ppermute | solution.py:289
  36.4 14.8 %collective-permute-start.5 = (bf16[4,136,256]{2,1,0:T(8,128)(2,1)S(1)}, bf16[4,136,256]{2,1,0:T(8,128)(2,1)S(1)}, u32[]{:S(2)}, u32[]{:S(2)}) collective-permute-start(bf16[4,136,256]{2,1,0:T(8,128)(2,1)S(1)} %pad_maximum_fusion.refs_5_), channel_id=1, source_target_pairs={{4,0},{5,1},{6,2},{7,3},{0,4},{1,5},{2,6},{3,7},{12,8},{13,9},{14,... | collective-permute-start | bytes 835592 | tf_op jit(solution)/shard_map/ppermute | solution.py:289
  40.7 13.5 %collective-permute-start.4 = (bf16[4,136,256]{2,1,0:T(8,128)(2,1)S(1)}, bf16[4,136,256]{2,1,0:T(8,128)(2,1)S(1)}, u32[]{:S(2)}, u32[]{:S(2)}) collective-permute-start(bf16[4,136,256]{2,1,0:T(8,128)(2,1)S(1)} %pad_maximum_fusion.refs_5_), channel_id=1, source_target_pairs={{2,0},{3,1},{4,2},{5,3},{6,4},{7,5},{0,6},{1,7},{10,8},{11,9},{12,... | collective-permute-start | bytes 835592 | tf_op jit(solution)/shard_map/ppermute | solution.py:289
  44.4 12.2 %collective-permute-start.7 = (bf16[4,136,256]{2,1,0:T(8,128)(2,1)S(1)}, bf16[4,136,256]{2,1,0:T(8,128)(2,1)S(1)}, u32[]{:S(2)}, u32[]{:S(2)}) collective-permute-start(bf16[4,136,256]{2,1,0:T(8,128)(2,1)S(1)} %pad_maximum_fusion.refs_5_), channel_id=1, source_target_pairs={{0,1},{1,0},{2,3},{3,2},{4,5},{5,4},{6,7},{7,6},{8,9},{9,8},{10,11... | collective-permute-start | bytes 835592 | tf_op jit(solution)/shard_map/ppermute | solution.py:292
  49.2 7.4 %collective-permute-start.10 = (bf16[4,136,256]{2,1,0:T(8,128)(2,1)S(1)}, bf16[4,136,256]{2,1,0:T(8,128)(2,1)S(1)}, u32[]{:S(2)}, u32[]{:S(2)}) collective-permute-start(bf16[4,136,256]{2,1,0:T(8,128)(2,1)S(1)} %collective-permute-done.6.refs_8_), channel_id=1, source_target_pairs={{0,1},{1,0},{2,3},{3,2},{4,5},{5,4},{6,7},{7,6},{8,9},{9,8},{10,11... | collective-permute-start | bytes 835592 | tf_op jit(solution)/shard_map/ppermute | solution.py:292
  51.2 5.5 %collective-permute-start.9 = (bf16[4,136,256]{2,1,0:T(8,128)(2,1)S(1)}, bf16[4,136,256]{2,1,0:T(8,128)(2,1)S(1)}, u32[]{:S(2)}, u32[]{:S(2)}) collective-permute-start(bf16[4,136,256]{2,1,0:T(8,128)(2,1)S(1)} %collective-permute-done.5.refs_7_), channel_id=1, source_target_pairs={{0,1},{1,0},{2,3},{3,2},{4,5},{5,4},{6,7},{7,6},{8,9},{9,8},{10,11... | collective-permute-start | bytes 835592 | tf_op jit(solution)/shard_map/ppermute | solution.py:292
  54.3 3.5 %collective-permute-start.8 = (bf16[4,136,256]{2,1,0:T(8,128)(2,1)S(1)}, bf16[4,136,256]{2,1,0:T(8,128)(2,1)S(1)}, u32[]{:S(2)}, u32[]{:S(2)}) collective-permute-start(bf16[4,136,256]{2,1,0:T(8,128)(2,1)S(1)} %collective-permute-done.4.refs_6_), channel_id=1, source_target_pairs={{0,1},{1,0},{2,3},{3,2},{4,5},{5,4},{6,7},{7,6},{8,9},{9,8},{10,11... | collective-permute-start | bytes 835592 | tf_op jit(solution)/shard_map/ppermute | solution.py:292
  69.2 21.9 %all-to-all-start.1 = ((f32[64,2,128]{2,1,0:T(2,128)}), f32[64,2,128]{2,1,0:T(2,128)S(1)}, u32[]{:S(2)}, u32[]{:S(2)}) async-start(f32[64,2,128]{2,1,0:T(2,128)} %attend.1), calls=%async_computation.1 | async-start | bytes 131072 | tf_op jit(solution)/shard_map/all_to_all | solution.py:320
  91.1 0.6 copy-start

commit v6 on v5

--- a/solution.py
+++ b/solution.py
@@ -50,7 +50,8 @@
 
 
 def attend_kernel(scale, cnt_ref, base_ref, dst_ref, a1_ref, a2_ref, *rest):
-    b_refs, (out_ref, a_ref, g_ref, h_ref, list_ref, even_ref, odd_ref) = rest[:8], rest[8:]
+    blocks, (out_ref, a_ref, g_ref, h_ref, list_ref, even_ref, odd_ref) = rest[:4], rest[4:]
+    b_refs = [ref.at[i] for ref in blocks for i in range(ref.shape[0])]
     a_ref[0:SIDE] = a1_ref[...]
     a_ref[SIDE:SOURCES] = a2_ref[...]
     for q in range(QUADS):
@@ -145,9 +146,8 @@
 
     col = lax.broadcasted_iota(jnp.int32, (16, LANES), 0)
     lane = lax.broadcasted_iota(jnp.int32, (16, LANES), 1)
-    flat_source = jnp.zeros((SLOTS, LANES), jnp.float32)
+    flat_both = jnp.zeros((SLOTS, 2 * LANES), jnp.float32)
     flat_target = jnp.zeros((SLOTS, LANES), jnp.float32)
-    flat_cross = jnp.zeros((SLOTS, LANES), jnp.float32)
     for r in range(6):
         tail = (col == 12) & (lane == 36 + r)
         pick_low = (((col < 6) & (lane == 6 * r + col)) | tail).astype(jnp.float32)
@@ -155,24 +155,27 @@
         pick_high = (in_high | tail).astype(jnp.float32)
         upper = h_ref[0:SLOTS, r, :]
         lower = h_ref[0:SLOTS, 6 + r, :]
-        flat_source += jnp.dot(upper, pick_low, precision=HIGHEST, preferred_element_type=jnp.float32)
-        flat_cross += jnp.dot(upper, in_high.astype(jnp.float32), precision=HIGHEST, preferred_element_type=jnp.float32)
+        picks = jnp.concatenate([pick_low, in_high.astype(jnp.float32)], axis=1)
+        flat_both += jnp.dot(upper, picks, precision=HIGHEST, preferred_element_type=jnp.float32)
         flat_target += jnp.dot(lower, pick_high, precision=HIGHEST, preferred_element_type=jnp.float32)
     dest = lax.broadcasted_iota(jnp.int32, (SIDE * SIDE, SLOTS), 0)
     to_source = (dest == dst_ref[0:1, :]).astype(jnp.float32)
     to_target = (dest == dst_ref[1:2, :]).astype(jnp.float32)
     to_owner = (dest == dst_ref[2:3, :]).astype(jnp.float32)
-    pose = jnp.dot(to_source, flat_source, precision=HIGHEST, preferred_element_type=jnp.float32)
-    pose += jnp.dot(to_target, flat_target, precision=HIGHEST, preferred_element_type=jnp.float32)
-    owned = []
-    for q in range(QUADS):
-        here = slice(q * SOURCES, (q + 1) * SOURCES)
-        moved = pltpu.roll(flat_cross[here], POSE + 36 * (q % 2), 1)
-        owned.append(
-            jnp.dot(to_owner[:, 0:SOURCES], moved, precision=HIGHEST, preferred_element_type=jnp.float32)
-        )
-    out_ref[:, 0, :] = pose + owned[0] + owned[1]
-    out_ref[:, 1, :] = owned[2] + owned[3]
+    flat_source, flat_cross = flat_both[:, 0:LANES], flat_both[:, LANES:]
+    moved = [
+        pltpu.roll(flat_cross[q * SOURCES : (q + 1) * SOURCES], POSE + 36 * (q % 2), 1) for q in range(QUADS)
+    ]
+    poses = jnp.concatenate([to_source, to_target], axis=1)
+    flats = jnp.concatenate([flat_source, flat_target], axis=0)
+    pose = jnp.dot(poses, flats, precision=HIGHEST, preferred_element_type=jnp.float32)
+    owner = to_owner[:, 0 : 2 * SOURCES]
+    owned = [
+        jnp.dot(owner, jnp.concatenate(two, axis=0), precision=HIGHEST, preferred_element_type=jnp.float32)
+        for two in (moved[:2], moved[2:])
+    ]
+    out_ref[:, 0, :] = pose + owned[0]
+    out_ref[:, 1, :] = owned[1]
 
 
 def collect_kernel(group_ref, quad_ref, got_ref, out_ref, even_ref, odd_ref):
@@ -259,7 +262,7 @@
     return pl.pallas_call(
         lambda *refs: attend_kernel(scale, *refs),
         out_shape=jax.ShapeDtypeStruct((SIDE * SIDE, 2, LANES), jnp.float32),
-        in_specs=[smem, smem] + [vmem] * 11,
+        in_specs=[smem, smem] + [vmem] * 7,
         out_specs=vmem,
         scratch_shapes=[
             pltpu.VMEM((SOURCES, PACKED, WIDTH), jnp.bfloat16),
@@ -284,12 +287,14 @@
 
     sources_row = lax.all_to_all(copies, "pair", split_axis=0, concat_axis=0, tiled=True, axis_index_groups=y_groups)
     targets_quad = jnp.stack([packed] + [lax.ppermute(packed, "pair", from_ahead(2 * q)) for q in range(1, QUADS)])
-    quarters, peers = [targets_quad], []
+    quarters, mine, peers = [targets_quad], [], []
     for d in (1, 2, 3):
         quarters.append(lax.ppermute(targets_quad, "split", x_ahead(d)))
     sources_next = lax.ppermute(sources_row, "pair", z_swap)
-    for d in range(4):
-        peers.append(lax.ppermute(quarters[d], "split", core_swap))
+    mine.append(jnp.stack([quarters[d] for d in (0,)]))
+    peers.append(lax.ppermute(mine[-1], "split", core_swap))
+    mine.append(jnp.stack([quarters[d] for d in (1, 3, 2)]))
+    peers.append(lax.ppermute(mine[-1], "split", core_swap))
 
     all_targets = pair_list[:, 1].reshape(SIDE, SIDE, PAIRS_PER)
     task_targets = jnp.concatenate(
@@ -316,7 +321,7 @@
     smem = pl.BlockSpec(memory_space=pltpu.SMEM)
     vmem = pl.BlockSpec(memory_space=pltpu.VMEM)
     scale = WIDTH**-0.5 / math.log(2.0)
-    send = attend_call(scale, task_counts, base, destinations, sources_row, sources_next, *quarters, *peers)
+    send = attend_call(scale, task_counts, base, destinations, sources_row, sources_next, *mine, *peers)
     got = lax.all_to_all(send, "pair", split_axis=0, concat_axis=0, tiled=True)
 
     my_targets = lax.dynamic_slice_in_dim(pair_list[:, 1], own * PAIRS_PER, PAIRS_PER, 0)

time: 107 us -> 109 us (1.019)
  starting transfers between devices: 62 us -> 58.8 us
  waiting for transfers between devices: 11.7 us -> 14.7 us
  blocking collectives: 10.8 us -> 13.2 us
    ppermute x4 -> x2, starting transfers between devices: 11.7 us -> 7.9 us  [per_device(): peers.append(lax.ppermute(mine[-1], 'split', core_swap))]
    all_to_all x1, blocking collectives: 10.8 us -> 13.2 us  [per_device(): lax.all_to_all(share, 'split', split_axis=0, concat_axis=0, tiled=True)]
    ppermute x3, waiting for transfers between devices: 0.01 us -> 1.68 us  [per_device(): lax.ppermute(packed, 'pair', from_ahead(2 * q))]
    ppermute x3, waiting for transfers between devices: 0.01 us -> 1.34 us  [per_device(): quarters.append(lax.ppermute(targets_quad, 'split', x_ahead(d)))]
  transfers between devices with their start and end apart: 13 -> 11, of which waited for: 2 -> 4; matrix products, arithmetic and copies ran while one was open for 2% -> 2% of each run, Pallas kernels for 0% -> 0%
where the time goes in v6:
time: 109 us; the launch traced here: 108 us
  starting transfers between devices  58.8 us (54%)
  Pallas kernels  16.4 us (15%)
  waiting for transfers between devices  14.7 us (13%)
  blocking collectives  13.2 us (12%)
  local copies, waits for them, and re-layouts  2.22 us (2%)
  other arithmetic  1.74 us (2%)
    ppermute x3, starting transfers between devices, per_device(): lax.ppermute(packed, 'pair', from_ahead(2 * q))  18 us
    all_to_all x1, blocking collectives, per_device(): lax.all_to_all(share, 'split', split_axis=0, concat_axis=0, tiled=True)  13.2 us
    all_to_all x1, starting transfers between devices, per_device(): got = lax.all_to_all(send, 'pair', split_axis=0, concat_axis=0, tiled=True)  11.3 us
    pallas_call x1, Pallas kernels, attend_call(): pl.pallas_call(lambda *refs: attend_kernel(scale, *refs), out_shape=jax.S...  11.3 us
    all_to_all x1, waiting for transfers between devices, per_device(): got = lax.all_to_all(send, 'pair', split_axis=0, concat_axis=0, tiled=True)  10.6 us
    ppermute x3, starting transfers between devices, per_device(): quarters.append(lax.ppermute(targets_quad, 'split', x_ahead(d)))  9.93 us
    ppermute x2, starting transfers between devices, per_device(): peers.append(lax.ppermute(mine[-1], 'split', core_swap))  7.9 us
    all_to_all x1, starting transfers between devices, per_device(): lax.all_to_all(copies, 'pair', split_axis=0, concat_axis=0, tiled=True, a...  7.77 us
  transfers between devices with their start and end apart: 11, of which 4 were waited for; matrix products, arithmetic and copies ran while one was open for 2% of the time, Pallas kernels for 0%

profile of v6, /device:TPU:1, one launch (start us, length us, event | category | flops | bytes accessed | tf_op | source)
XLA Modules:
  0.0 108.0 jit_solution(5899172339682808327)
XLA Ops:
  0.6 1.7 %pack.1 = (bf16[136,256]{1,0:T(8,128)(2,1)}, bf16[8,136,256]{2,1,0:T(8,128)(2,1)}) custom-call(bf16[128,256]{1,0:T(8,128)(2,1)} %bitcast.37, bf16[3,128]{1,0:T(4,128)(2,1)} %bitcast.41, bf16[3,128]{1,0:T(4,128)(2,1)} %bitcast.42, s32[1,24]{1,0:T(1,128)} %bitcast.43), custom_call_target="tpu_custom_call" | custom-call | tf_op jit(solution)/shard_map/pack/pallas_call | solution.py:247
  2.4 7.8 %all-to-all-start = ((bf16[8,136,256]{2,1,0:T(8,128)(2,1)}), bf16[8,136,256]{2,1,0:T(8,128)(2,1)S(1)}, u32[]{:S(2)}, u32[]{:S(2)}) async-start(bf16[8,136,256]{2,1,0:T(8,128)(2,1)} %get-tuple-element.8), calls=%async_computation | async-start | bytes 1114112 | tf_op jit(solution)/shard_map/all_to_all | solution.py:288
  10.1 5.8 %collective-permute-start.3 = (bf16[136,256]{1,0:T(8,128)(2,1)S(1)}, bf16[136,256]{1,0:T(8,128)(2,1)S(1)}, u32[]{:S(2)}, u32[]{:S(2)}) collective-permute-start(bf16[136,256]{1,0:T(8,128)(2,1)S(1)} %copy-done.1), channel_id=1, source_target_pairs={{384,0},{392,8},{400,16},{408,24},{416,32},{424,40},{432,48},{440,... | collective-permute-start | bytes 208904 | tf_op jit(solution)/shard_map/ppermute | solution.py:289
  16.0 8.8 %collective-permute-start.2 = (bf16[136,256]{1,0:T(8,128)(2,1)S(1)}, bf16[136,256]{1,0:T(8,128)(2,1)S(1)}, u32[]{:S(2)}, u32[]{:S(2)}) collective-permute-start(bf16[136,256]{1,0:T(8,128)(2,1)S(1)} %copy-done.1), channel_id=1, source_target_pairs={{256,0},{264,8},{272,16},{280,24},{288,32},{296,40},{304,48},{312,... | collective-permute-start | bytes 208904 | tf_op jit(solution)/shard_map/ppermute | solution.py:289
  24.8 3.4 %collective-permute-start.1 = (bf16[136,256]{1,0:T(8,128)(2,1)S(1)}, bf16[136,256]{1,0:T(8,128)(2,1)S(1)}, u32[]{:S(2)}, u32[]{:S(2)}) collective-permute-start(bf16[136,256]{1,0:T(8,128)(2,1)S(1)} %copy-done.1), channel_id=1, source_target_pairs={{128,0},{136,8},{144,16},{152,24},{160,32},{168,40},{176,48},{184,... | collective-permute-start | bytes 208904 | tf_op jit(solution)/shard_map/ppermute | solution.py:289
  28.3 0.7 copy-done.2
  29.1 1.7 %collective-permute-done.1 = bf16[136,256]{1,0:T(8,128)(2,1)S(1)} collective-permute-done((bf16[136,256]{1,0:T(8,128)(2,1)S(1)}, bf16[136,256]{1,0:T(8,128)(2,1)S(1)}, u32[]{:S(2)}, u32[]{:S(2)}) %collective-permute-start.1) | collective-permute-done | bytes 69664 | tf_op jit(solution)/shard_map/ppermute | solution.py:289
  30.8 3.1 %collective-permute-start.5 = (bf16[4,136,256]{2,1,0:T(8,128)(2,1)S(1)}, bf16[4,136,256]{2,1,0:T(8,128)(2,1)S(1)}, u32[]{:S(2)}, u32[]{:S(2)}) collective-permute-start(bf16[4,136,256]{2,1,0:T(8,128)(2,1)S(1)} %get-tuple-element.19), channel_id=1, source_target_pairs={{6,0},{7,1},{0,2},{1,3},{2,4},{3,5},{4,6},{5,7},{14,8},{15,9},{8,1... | collective-permute-start | bytes 835592 | tf_op jit(solution)/shard_map/ppermute | solution.py:292
  33.9 3.4 %collective-permute-start.4 = (bf16[4,136,256]{2,1,0:T(8,128)(2,1)S(1)}, bf16[4,136,256]{2,1,0:T(8,128)(2,1)S(1)}, u32[]{:S(2)}, u32[]{:S(2)}) collective-permute-start(bf16[4,136,256]{2,1,0:T(8,128)(2,1)S(1)} %get-tuple-element.19), channel_id=1, source_target_pairs={{2,0},{3,1},{4,2},{5,3},{6,4},{7,5},{0,6},{1,7},{10,8},{11,9},{12,... | collective-permute-start | bytes 835592 | tf_op jit(solution)/shard_map/ppermute | solution.py:292
  37.3 3.4 %collective-permute-start.6 = (bf16[4,136,256]{2,1,0:T(8,128)(2,1)S(1)}, bf16[4,136,256]{2,1,0:T(8,128)(2,1)S(1)}, u32[]{:S(2)}, u32[]{:S(2)}) collective-permute-start(bf16[4,136,256]{2,1,0:T(8,128)(2,1)S(1)} %get-tuple-element.19), channel_id=1, source_target_pairs={{4,0},{5,1},{6,2},{7,3},{0,4},{1,5},{2,6},{3,7},{12,8},{13,9},{14,... | collective-permute-start | bytes 835592 | tf_op jit(solution)/shard_map/ppermute | solution.py:292
  40.9 0.6 copy-done.3
  41.8 3.9 %collective-permute-start = (bf16[8,136,256]{2,1,0:T(8,128)(2,1)S(1)}, bf16[8,136,256]{2,1,0:T(8,128)(2,1)S(1)}, u32[]{:S(2)}, u32[]{:S(2)}) collective-permute-start(bf16[8,136,256]{2,1,0:T(8,128)(2,1)S(1)} %all-to-all-done.refs_3_), channel_id=1, source_target_pairs={{0,64},{8,72},{16,80},{24,88},{32,96},{40,104},{48,112},{56,120},{... | collective-permute-start | bytes 1671176 | tf_op jit(solution)/shard_map/ppermute | solution.py:293
  45.7 1.3 %collective-permute-done.6 = bf16[4,136,256]{2,1,0:T(8,128)(2,1)S(1)} collective-permute-done((bf16[4,136,256]{2,1,0:T(8,128)(2,1)S(1)}, bf16[4,136,256]{2,1,0:T(8,128)(2,1)S(1)}, u32[]{:S(2)}, u32[]{:S(2)}) %collective-permute-start.6) | collective-permute-done | bytes 278560 | tf_op jit(solution)/shard_map/ppermute | solution.py:292
  47.1 6.0 %collective-permute-start.8 = (bf16[3,4,136,256]{3,2,1,0:T(8,128)(2,1)S(1)}, bf16[3,4,136,256]{3,2,1,0:T(8,128)(2,1)S(1)}, u32[]{:S(2)}, u32[]{:S(2)}) collective-permute-start(bf16[3,4,136,256]{3,2,1,0:T(8,128)(2,1)S(1)} %pad_maximum_fusion.refs_6_), channel_id=1, source_target_pairs={{0,1},{1,0},{2,3},{3,2},{4,5},{5,4},{6,7},{7,6},{8,9},{9,8},{10,11... | collective-permute-start | bytes 2506760 | tf_op jit(solution)/shard_map/ppermute | solution.py:297
  53.2 0.5 and_select_fusion.5
  53.7 1.9 %collective-permute-start.7 = (bf16[1,4,136,256]{3,2,1,0:T(8,128)(2,1)S(1)}, bf16[1,4,136,256]{3,2,1,0:T(8,128)(2,1)S(1)}, u32[]{:S(2)}, u32[]{:S(2)}) collective-permute-start(bf16[1,4,136,256]{3,2,1,0:T(8,128)(2,1)S(1)} %get-tuple-element.20.refs_5_), channel_id=1, source_target_pairs={{0,1},{1,0},{2,3},{3,2},{4,5},{5,4},{6,7},{7,6},{8,9},{9,8},{10,11... | collective-permute-start | bytes 835592 | tf_op jit(solution)/shard_map/ppermute | solution.py:295
  56.0 1.1 %collective-permute-done.7.refs_7_ = bf16[1,4,136,256]{3,2,1,0:T(8,128)(2,1)S(1)} collective-permute-done((bf16[1,4,136,256]{3,2,1,0:T(8,128)(2,1)S(1)}, bf16[1,4,136,256]{3,2,1,0:T(8,128)(2,1)S(1)}, u32[]{:S(2)}, u32[]{:S(2)}) %collective-permute-start.7) | collective-permute-done | bytes 278560 | tf_op jit(solution)/shard_map/ppermute | solution.py:295
  57.2 11.3 %attend.1 = f32[64,2,128]{2,1,0:T(2,128)} custom-call(s32[128]{0:T(128)S(1)} %pad.4.refs_0_, s32[1]{0:T(128)} %bitcast.8.refs_1_, s32[8,64]{1,0:T(8,128)S(1)} %stack.47.refs_2_, bf16[8,136,256]{2,1,0:T(8,128)(2,1)S(1)} %all-to-all-done.refs_3_, bf16[8,136,256]{2,1,0:T(8,128)(2,1)S(1)} %collective-permute-done.refs_4_, ...), custom_call_target="tpu_custom_call" | custom-call | tf_op jit(solution)/shard_map/attend/pallas_call | solution.py:262
  68.4 11.3 %all-to-all-start.1 = ((f32[64,2,128]{2,1,0:T(2,128)}), f32[64,2,128]{2,1,0:T(2,128)S(1)}, u32[]{:S(2)}, u32[]{:S(2)}) async-start(f32[64,2,128]{2,1,0:T(2,128)} %attend.1), calls=%async_computation.1 | async-start | bytes 131072 | tf_op jit(solution)/shard_map/all_to_all | solution.py:325
  80.3 10.6 %all-to-all-done.1.got_ref = f32[64,2,128]{2,1,0:T(2,128)S(1)} async-done(((f32[64,2,128]{2,1,0:T(2,128)}), f32[64,2,128]{2,1,0:T(2,128)S(1)}, u32[]{:S(2)}, u32[]{:S(2)}) %all-to-all-start.1) | async-done | bytes 65568 | tf_op jit(solution)/shard_map/all_to_all | solution.py:325
  90.8 0.6 copy-done
  91.4 1.8 %collect.1 = f32[8,32,128]{2,1,0:T(8,128)} custom-call(s32[24]{0:T(128)} %fusion.2.group_ref, s32[24]{0:T(128)} %get-tuple-element.15.quad_ref, f32[64,2,128]{2,1,0:T(2,128)} %copy-done), custom_call_target="tpu_custom_call" | custom-call | tf_op jit(solution)/shard_map/collect/pallas_call | solution.py:332
  93.2 13.2 %all_to_all.15.refs_0_ = f32[8,32,128]{2,1,0:T(8,128)} all-to-all(f32[8,32,128]{2,1,0:T(8,128)} %collect.1), channel_id=1, replica_groups=mesh['pair'=64,'split'=8] {'split'}, dimensions={0} | all-to-all | bytes 262144 | tf_op jit(solution)/shard_map/all_to_all | solution.py:340
  106.4 1.6 %finish.1 = (f32[6,6,24]{2,1,0:T(8,128)}, f32[6,1,6]{2,1,0:T(1,128)}, f32[1,6]{1,0:T(1,128)}) custom-call(f32[8,32,128]{2,1,0:T(8,128)} %all_to_all.15.refs_0_), custom_call_target="tpu_custom_call" | custom-call | tf_op jit(solution)/shard_map/finish/pallas_call | solution.py:343
  (33 shorter events, 1.5 us)
Async XLA Ops:
  2.4 7.8 %copy-start.1 = (bf16[136,256]{1,0:T(8,128)(2,1)S(1)}, bf16[136,256]{1,0:T(8,128)(2,1)}, u32[]{:S(2)}) copy-start(bf16[136,256]{1,0:T(8,128)(2,1)} %get-tuple-element.9) | copy-start | bytes 208900
  2.4 39.4 %all-to-all-start = ((bf16[8,136,256]{2,1,0:T(8,128)(2,1)}), bf16[8,136,256]{2,1,0:T(8,128)(2,1)S(1)}, u32[]{:S(2)}, u32[]{:S(2)}) async-start(bf16[8,136,256]{2,1,0:T(8,128)(2,1)} %get-tuple-element.8), calls=%async_computation | async-start | bytes 1114112 | tf_op jit(solution)/shard_map/all_to_all | solution.py:288
  10.1 18.9 %collective-permute-start.3 = (bf16[136,256]{1,0:T(8,128)(2,1)S(1)}, bf16[136,256]{1,0:T(8,128)(2,1)S(1)}, u32[]{:S(2)}, u32[]{:S(2)}) collective-permute-start(bf16[136,256]{1,0:T(8,128)(2,1)S(1)} %copy-done.1), channel_id=1, source_target_pairs={{384,0},{392,8},{400,16},{408,24},{416,32},{424,40},{432,48},{440,... | collective-permute-start | bytes 208904 | tf_op jit(solution)/shard_map/ppermute | solution.py:289
  16.0 13.1 %collective-permute-start.2 = (bf16[136,256]{1,0:T(8,128)(2,1)S(1)}, bf16[136,256]{1,0:T(8,128)(2,1)S(1)}, u32[]{:S(2)}, u32[]{:S(2)}) collective-permute-start(bf16[136,256]{1,0:T(8,128)(2,1)S(1)} %copy-done.1), channel_id=1, source_target_pairs={{256,0},{264,8},{272,16},{280,24},{288,32},{296,40},{304,48},{312,... | collective-permute-start | bytes 208904 | tf_op jit(solution)/shard_map/ppermute | solution.py:289
  24.8 6.0 %collective-permute-start.1 = (bf16[136,256]{1,0:T(8,128)(2,1)S(1)}, bf16[136,256]{1,0:T(8,128)(2,1)S(1)}, u32[]{:S(2)}, u32[]{:S(2)}) collective-permute-start(bf16[136,256]{1,0:T(8,128)(2,1)S(1)} %copy-done.1), channel_id=1, source_target_pairs={{128,0},{136,8},{144,16},{152,24},{160,32},{168,40},{176,48},{184,... | collective-permute-start | bytes 208904 | tf_op jit(solution)/shard_map/ppermute | solution.py:289
  28.2 0.7 copy-start.2
  30.8 14.8 %collective-permute-start.5 = (bf16[4,136,256]{2,1,0:T(8,128)(2,1)S(1)}, bf16[4,136,256]{2,1,0:T(8,128)(2,1)S(1)}, u32[]{:S(2)}, u32[]{:S(2)}) collective-permute-start(bf16[4,136,256]{2,1,0:T(8,128)(2,1)S(1)} %get-tuple-element.19), channel_id=1, source_target_pairs={{6,0},{7,1},{0,2},{1,3},{2,4},{3,5},{4,6},{5,7},{14,8},{15,9},{8,1... | collective-permute-start | bytes 835592 | tf_op jit(solution)/shard_map/ppermute | solution.py:292
  33.9 11.7 %collective-permute-start.4 = (bf16[4,136,256]{2,1,0:T(8,128)(2,1)S(1)}, bf16[4,136,256]{2,1,0:T(8,128)(2,1)S(1)}, u32[]{:S(2)}, u32[]{:S(2)}) collective-permute-start(bf16[4,136,256]{2,1,0:T(8,128)(2,1)S(1)} %get-tuple-element.19), channel_id=1, source_target_pairs={{2,0},{3,1},{4,2},{5,3},{6,4},{7,5},{0,6},{1,7},{10,8},{11,9},{12,... | collective-permute-start | bytes 835592 | tf_op jit(solution)/shard_map/ppermute | solution.py:292
  37.3 9.7 %collective-permute-start.6 = (bf16[4,136,256]{2,1,0:T(8,128)(2,1)S(1)}, bf16[4,136,256]{2,1,0:T(8,128)(2,1)S(1)}, u32[]{:S(2)}, u32[]{:S(2)}) collective-permute-start(bf16[4,136,256]{2,1,0:T(8,128)(2,1)S(1)} %get-tuple-element.19), channel_id=1, source_target_pairs={{4,0},{5,1},{6,2},{7,3},{0,4},{1,5},{2,6},{3,7},{12,8},{13,9},{14,... | collective-permute-start | bytes 835592 | tf_op jit(solution)/shard_map/ppermute | solution.py:292
  40.9 0.7 copy-start.3
  41.8 13.9 %collective-permute-start = (bf16[8,136,256]{2,1,0:T(8,128)(2,1)S(1)}, bf16[8,136,256]{2,1,0:T(8,128)(2,1)S(1)}, u32[]{:S(2)}, u32[]{:S(2)}) collective-permute-start(bf16[8,136,256]{2,1,0:T(8,128)(2,1)S(1)} %all-to-all-done.refs_3_), channel_id=1, source_target_pairs={{0,64},{8,72},{16,80},{24,88},{32,96},{40,104},{48,112},{56,120},{... | collective-permute-start | bytes 1671176 | tf_op jit(solution)/shard_map/ppermute | solution.py:293
  47.1 10.1 %collective-permute-start.8 = (bf16[3,4,136,256]{3,2,1,0:T(8,128)(2,1)S(1)}, bf16[3,4,136,256]{3,2,1,0:T(8,128)(2,1)S(1)}, u32[]{:S(2)}, u32[]{:S(2)}) collective-permute-start(bf16[3,4,136,256]{3,2,1,0:T(8,128)(2,1)S(1)} %pad_maximum_fusion.refs_6_), channel_id=1, source_target_pairs={{0,1},{1,0},{2,3},{3,2},{4,5},{5,4},{6,7},{7,6},{8,9},{9,8},{10,11... | collective-permute-start | bytes 2506760 | tf_op jit(solution)/shard_map/ppermute | solution.py:297
  53.7 3.4 %collective-permute-start.7 = (bf16[1,4,136,256]{3,2,1,0:T(8,128)(2,1)S(1)}, bf16[1,4,136,256]{3,2,1,0:T(8,128)(2,1)S(1)}, u32[]{:S(2)}, u32[]{:S(2)}) collective-permute-start(bf16[1,4,136,256]{3,2,1,0:T(8,128)(2,1)S(1)} %get-tuple-element.20.refs_5_), channel_id=1, source_target_pairs={{0,1},{1,0},{2,3},{3,2},{4,5},{5,4},{6,7},{7,6},{8,9},{9,8},{10,11... | collective-permute-start | bytes 835592 | tf_op jit(solution)/shard_map/ppermute | solution.py:295
  68.4 22.4 %all-to-all-start.1 = ((f32[64,2,128]{2,1,0:T(2,128)}), f32[64,2,128]{2,1,0:T(2,128)S(1)}, u32[]{:S(2)}, u32[]{:S(2)}) async-start(f32[64,2,128]{2,1,0:T(2,128)} %attend.1), calls=%async_computation.1 | async-start | bytes 131072 | tf_op jit(solution)/shard_map/all_to_all | solution.py:325
  90.8 0.6 copy-start

commit v7 on v6

--- a/solution.py
+++ b/solution.py
@@ -146,8 +146,7 @@
 
     col = lax.broadcasted_iota(jnp.int32, (16, LANES), 0)
     lane = lax.broadcasted_iota(jnp.int32, (16, LANES), 1)
-    flat_both = jnp.zeros((SLOTS, 2 * LANES), jnp.float32)
-    flat_target = jnp.zeros((SLOTS, LANES), jnp.float32)
+    flat = jnp.zeros((SLOTS, 3 * LANES), jnp.float32)
     for r in range(6):
         tail = (col == 12) & (lane == 36 + r)
         pick_low = (((col < 6) & (lane == 6 * r + col)) | tail).astype(jnp.float32)
@@ -155,14 +154,21 @@
         pick_high = (in_high | tail).astype(jnp.float32)
         upper = h_ref[0:SLOTS, r, :]
         lower = h_ref[0:SLOTS, 6 + r, :]
-        picks = jnp.concatenate([pick_low, in_high.astype(jnp.float32)], axis=1)
-        flat_both += jnp.dot(upper, picks, precision=HIGHEST, preferred_element_type=jnp.float32)
-        flat_target += jnp.dot(lower, pick_high, precision=HIGHEST, preferred_element_type=jnp.float32)
+        none = jnp.zeros((16, LANES), jnp.float32)
+        picks = jnp.concatenate(
+            [
+                jnp.concatenate([pick_low, in_high.astype(jnp.float32), none], axis=1),
+                jnp.concatenate([none, none, pick_high], axis=1),
+            ],
+            axis=0,
+        )
+        both = jnp.concatenate([upper, lower], axis=1)
+        flat += jnp.dot(both, picks, precision=HIGHEST, preferred_element_type=jnp.float32)
     dest = lax.broadcasted_iota(jnp.int32, (SIDE * SIDE, SLOTS), 0)
     to_source = (dest == dst_ref[0:1, :]).astype(jnp.float32)
     to_target = (dest == dst_ref[1:2, :]).astype(jnp.float32)
     to_owner = (dest == dst_ref[2:3, :]).astype(jnp.float32)
-    flat_source, flat_cross = flat_both[:, 0:LANES], flat_both[:, LANES:]
+    flat_source, flat_cross, flat_target = (flat[:, i * LANES : (i + 1) * LANES] for i in range(3))
     moved = [
         pltpu.roll(flat_cross[q * SOURCES : (q + 1) * SOURCES], POSE + 36 * (q % 2), 1) for q in range(QUADS)
     ]

time: 109 us -> 109 us (level)
  no operation moved by 1% of the time
where the time goes in v7:
time: 109 us; the launch traced here: 108 us
  starting transfers between devices  58.8 us (54%)
  Pallas kernels  16.5 us (15%)
  waiting for transfers between devices  14.7 us (13%)
  blocking collectives  13.2 us (12%)
  local copies, waits for them, and re-layouts  2.22 us (2%)
  other arithmetic  1.74 us (2%)
    ppermute x3, starting transfers between devices, per_device(): lax.ppermute(packed, 'pair', from_ahead(2 * q))  18 us
    all_to_all x1, blocking collectives, per_device(): lax.all_to_all(share, 'split', split_axis=0, concat_axis=0, tiled=True)  13.2 us
    pallas_call x1, Pallas kernels, attend_call(): pl.pallas_call(lambda *refs: attend_kernel(scale, *refs), out_shape=jax.S...  11.3 us
    all_to_all x1, starting transfers between devices, per_device(): got = lax.all_to_all(send, 'pair', split_axis=0, concat_axis=0, tiled=True)  11.3 us
    all_to_all x1, waiting for transfers between devices, per_device(): got = lax.all_to_all(send, 'pair', split_axis=0, concat_axis=0, tiled=True)  10.6 us
    ppermute x3, starting transfers between devices, per_device(): quarters.append(lax.ppermute(targets_quad, 'split', x_ahead(d)))  9.93 us
    ppermute x2, starting transfers between devices, per_device(): peers.append(lax.ppermute(mine[-1], 'split', core_swap))  7.9 us
    all_to_all x1, starting transfers between devices, per_device(): lax.all_to_all(copies, 'pair', split_axis=0, concat_axis=0, tiled=True, a...  7.77 us
  transfers between devices with their start and end apart: 11, of which 4 were waited for; matrix products, arithmetic and copies ran while one was open for 2% of the time, Pallas kernels for 0%

profile of v7, /device:TPU:1, one launch (start us, length us, event | category | flops | bytes accessed | tf_op | source)
XLA Modules:
  0.0 108.1 jit_solution(2391126542980209751)
XLA Ops:
  0.6 1.7 %pack.1 = (bf16[136,256]{1,0:T(8,128)(2,1)}, bf16[8,136,256]{2,1,0:T(8,128)(2,1)}) custom-call(bf16[128,256]{1,0:T(8,128)(2,1)} %bitcast.37, bf16[3,128]{1,0:T(4,128)(2,1)} %bitcast.41, bf16[3,128]{1,0:T(4,128)(2,1)} %bitcast.42, s32[1,24]{1,0:T(1,128)} %bitcast.43), custom_call_target="tpu_custom_call" | custom-call | tf_op jit(solution)/shard_map/pack/pallas_call | solution.py:253
  2.4 7.8 %all-to-all-start = ((bf16[8,136,256]{2,1,0:T(8,128)(2,1)}), bf16[8,136,256]{2,1,0:T(8,128)(2,1)S(1)}, u32[]{:S(2)}, u32[]{:S(2)}) async-start(bf16[8,136,256]{2,1,0:T(8,128)(2,1)} %get-tuple-element.8), calls=%async_computation | async-start | bytes 1114112 | tf_op jit(solution)/shard_map/all_to_all | solution.py:294
  10.1 5.8 %collective-permute-start.3 = (bf16[136,256]{1,0:T(8,128)(2,1)S(1)}, bf16[136,256]{1,0:T(8,128)(2,1)S(1)}, u32[]{:S(2)}, u32[]{:S(2)}) collective-permute-start(bf16[136,256]{1,0:T(8,128)(2,1)S(1)} %copy-done.1), channel_id=1, source_target_pairs={{384,0},{392,8},{400,16},{408,24},{416,32},{424,40},{432,48},{440,... | collective-permute-start | bytes 208904 | tf_op jit(solution)/shard_map/ppermute | solution.py:295
  16.0 8.8 %collective-permute-start.2 = (bf16[136,256]{1,0:T(8,128)(2,1)S(1)}, bf16[136,256]{1,0:T(8,128)(2,1)S(1)}, u32[]{:S(2)}, u32[]{:S(2)}) collective-permute-start(bf16[136,256]{1,0:T(8,128)(2,1)S(1)} %copy-done.1), channel_id=1, source_target_pairs={{256,0},{264,8},{272,16},{280,24},{288,32},{296,40},{304,48},{312,... | collective-permute-start | bytes 208904 | tf_op jit(solution)/shard_map/ppermute | solution.py:295
  24.8 3.4 %collective-permute-start.1 = (bf16[136,256]{1,0:T(8,128)(2,1)S(1)}, bf16[136,256]{1,0:T(8,128)(2,1)S(1)}, u32[]{:S(2)}, u32[]{:S(2)}) collective-permute-start(bf16[136,256]{1,0:T(8,128)(2,1)S(1)} %copy-done.1), channel_id=1, source_target_pairs={{128,0},{136,8},{144,16},{152,24},{160,32},{168,40},{176,48},{184,... | collective-permute-start | bytes 208904 | tf_op jit(solution)/shard_map/ppermute | solution.py:295
  28.3 0.7 copy-done.2
  29.1 1.7 %collective-permute-done.1 = bf16[136,256]{1,0:T(8,128)(2,1)S(1)} collective-permute-done((bf16[136,256]{1,0:T(8,128)(2,1)S(1)}, bf16[136,256]{1,0:T(8,128)(2,1)S(1)}, u32[]{:S(2)}, u32[]{:S(2)}) %collective-permute-start.1) | collective-permute-done | bytes 69664 | tf_op jit(solution)/shard_map/ppermute | solution.py:295
  30.8 3.1 %collective-permute-start.5 = (bf16[4,136,256]{2,1,0:T(8,128)(2,1)S(1)}, bf16[4,136,256]{2,1,0:T(8,128)(2,1)S(1)}, u32[]{:S(2)}, u32[]{:S(2)}) collective-permute-start(bf16[4,136,256]{2,1,0:T(8,128)(2,1)S(1)} %get-tuple-element.19), channel_id=1, source_target_pairs={{6,0},{7,1},{0,2},{1,3},{2,4},{3,5},{4,6},{5,7},{14,8},{15,9},{8,1... | collective-permute-start | bytes 835592 | tf_op jit(solution)/shard_map/ppermute | solution.py:298
  33.9 3.4 %collective-permute-start.4 = (bf16[4,136,256]{2,1,0:T(8,128)(2,1)S(1)}, bf16[4,136,256]{2,1,0:T(8,128)(2,1)S(1)}, u32[]{:S(2)}, u32[]{:S(2)}) collective-permute-start(bf16[4,136,256]{2,1,0:T(8,128)(2,1)S(1)} %get-tuple-element.19), channel_id=1, source_target_pairs={{2,0},{3,1},{4,2},{5,3},{6,4},{7,5},{0,6},{1,7},{10,8},{11,9},{12,... | collective-permute-start | bytes 835592 | tf_op jit(solution)/shard_map/ppermute | solution.py:298
  37.3 3.4 %collective-permute-start.6 = (bf16[4,136,256]{2,1,0:T(8,128)(2,1)S(1)}, bf16[4,136,256]{2,1,0:T(8,128)(2,1)S(1)}, u32[]{:S(2)}, u32[]{:S(2)}) collective-permute-start(bf16[4,136,256]{2,1,0:T(8,128)(2,1)S(1)} %get-tuple-element.19), channel_id=1, source_target_pairs={{4,0},{5,1},{6,2},{7,3},{0,4},{1,5},{2,6},{3,7},{12,8},{13,9},{14,... | collective-permute-start | bytes 835592 | tf_op jit(solution)/shard_map/ppermute | solution.py:298
  40.9 0.6 copy-done.3
  41.8 3.9 %collective-permute-start = (bf16[8,136,256]{2,1,0:T(8,128)(2,1)S(1)}, bf16[8,136,256]{2,1,0:T(8,128)(2,1)S(1)}, u32[]{:S(2)}, u32[]{:S(2)}) collective-permute-start(bf16[8,136,256]{2,1,0:T(8,128)(2,1)S(1)} %all-to-all-done.refs_3_), channel_id=1, source_target_pairs={{0,64},{8,72},{16,80},{24,88},{32,96},{40,104},{48,112},{56,120},{... | collective-permute-start | bytes 1671176 | tf_op jit(solution)/shard_map/ppermute | solution.py:299
  45.7 1.3 %collective-permute-done.6 = bf16[4,136,256]{2,1,0:T(8,128)(2,1)S(1)} collective-permute-done((bf16[4,136,256]{2,1,0:T(8,128)(2,1)S(1)}, bf16[4,136,256]{2,1,0:T(8,128)(2,1)S(1)}, u32[]{:S(2)}, u32[]{:S(2)}) %collective-permute-start.6) | collective-permute-done | bytes 278560 | tf_op jit(solution)/shard_map/ppermute | solution.py:298
  47.1 6.0 %collective-permute-start.8 = (bf16[3,4,136,256]{3,2,1,0:T(8,128)(2,1)S(1)}, bf16[3,4,136,256]{3,2,1,0:T(8,128)(2,1)S(1)}, u32[]{:S(2)}, u32[]{:S(2)}) collective-permute-start(bf16[3,4,136,256]{3,2,1,0:T(8,128)(2,1)S(1)} %pad_maximum_fusion.refs_6_), channel_id=1, source_target_pairs={{0,1},{1,0},{2,3},{3,2},{4,5},{5,4},{6,7},{7,6},{8,9},{9,8},{10,11... | collective-permute-start | bytes 2506760 | tf_op jit(solution)/shard_map/ppermute | solution.py:303
  53.2 0.5 and_select_fusion.5
  53.7 1.9 %collective-permute-start.7 = (bf16[1,4,136,256]{3,2,1,0:T(8,128)(2,1)S(1)}, bf16[1,4,136,256]{3,2,1,0:T(8,128)(2,1)S(1)}, u32[]{:S(2)}, u32[]{:S(2)}) collective-permute-start(bf16[1,4,136,256]{3,2,1,0:T(8,128)(2,1)S(1)} %get-tuple-element.20.refs_5_), channel_id=1, source_target_pairs={{0,1},{1,0},{2,3},{3,2},{4,5},{5,4},{6,7},{7,6},{8,9},{9,8},{10,11... | collective-permute-start | bytes 835592 | tf_op jit(solution)/shard_map/ppermute | solution.py:301
  56.0 1.1 %collective-permute-done.7.refs_7_ = bf16[1,4,136,256]{3,2,1,0:T(8,128)(2,1)S(1)} collective-permute-done((bf16[1,4,136,256]{3,2,1,0:T(8,128)(2,1)S(1)}, bf16[1,4,136,256]{3,2,1,0:T(8,128)(2,1)S(1)}, u32[]{:S(2)}, u32[]{:S(2)}) %collective-permute-start.7) | collective-permute-done | bytes 278560 | tf_op jit(solution)/shard_map/ppermute | solution.py:301
  57.2 11.3 %attend.1 = f32[64,2,128]{2,1,0:T(2,128)} custom-call(s32[128]{0:T(128)S(1)} %pad.4.refs_0_, s32[1]{0:T(128)} %bitcast.8.refs_1_, s32[8,64]{1,0:T(8,128)S(1)} %stack.47.refs_2_, bf16[8,136,256]{2,1,0:T(8,128)(2,1)S(1)} %all-to-all-done.refs_3_, bf16[8,136,256]{2,1,0:T(8,128)(2,1)S(1)} %collective-permute-done.refs_4_, ...), custom_call_target="tpu_custom_call" | custom-call | tf_op jit(solution)/shard_map/attend/pallas_call | solution.py:268
  68.5 11.3 %all-to-all-start.1 = ((f32[64,2,128]{2,1,0:T(2,128)}), f32[64,2,128]{2,1,0:T(2,128)S(1)}, u32[]{:S(2)}, u32[]{:S(2)}) async-start(f32[64,2,128]{2,1,0:T(2,128)} %attend.1), calls=%async_computation.1 | async-start | bytes 131072 | tf_op jit(solution)/shard_map/all_to_all | solution.py:331
  80.4 10.6 %all-to-all-done.1.got_ref = f32[64,2,128]{2,1,0:T(2,128)S(1)} async-done(((f32[64,2,128]{2,1,0:T(2,128)}), f32[64,2,128]{2,1,0:T(2,128)S(1)}, u32[]{:S(2)}, u32[]{:S(2)}) %all-to-all-start.1) | async-done | bytes 65568 | tf_op jit(solution)/shard_map/all_to_all | solution.py:331
  90.9 0.6 copy-done
  91.5 1.8 %collect.1 = f32[8,32,128]{2,1,0:T(8,128)} custom-call(s32[24]{0:T(128)} %fusion.2.group_ref, s32[24]{0:T(128)} %get-tuple-element.15.quad_ref, f32[64,2,128]{2,1,0:T(2,128)} %copy-done), custom_call_target="tpu_custom_call" | custom-call | tf_op jit(solution)/shard_map/collect/pallas_call | solution.py:338
  93.3 13.2 %all_to_all.15.refs_0_ = f32[8,32,128]{2,1,0:T(8,128)} all-to-all(f32[8,32,128]{2,1,0:T(8,128)} %collect.1), channel_id=1, replica_groups=mesh['pair'=64,'split'=8] {'split'}, dimensions={0} | all-to-all | bytes 262144 | tf_op jit(solution)/shard_map/all_to_all | solution.py:346
  106.5 1.6 %finish.1 = (f32[6,6,24]{2,1,0:T(8,128)}, f32[6,1,6]{2,1,0:T(1,128)}, f32[1,6]{1,0:T(1,128)}) custom-call(f32[8,32,128]{2,1,0:T(8,128)} %all_to_all.15.refs_0_), custom_call_target="tpu_custom_call" | custom-call | tf_op jit(solution)/shard_map/finish/pallas_call | solution.py:349
  (33 shorter events, 1.5 us)
Async XLA Ops:
  2.4 7.8 %copy-start.1 = (bf16[136,256]{1,0:T(8,128)(2,1)S(1)}, bf16[136,256]{1,0:T(8,128)(2,1)}, u32[]{:S(2)}) copy-start(bf16[136,256]{1,0:T(8,128)(2,1)} %get-tuple-element.9) | copy-start | bytes 208900
  2.4 39.4 %all-to-all-start = ((bf16[8,136,256]{2,1,0:T(8,128)(2,1)}), bf16[8,136,256]{2,1,0:T(8,128)(2,1)S(1)}, u32[]{:S(2)}, u32[]{:S(2)}) async-start(bf16[8,136,256]{2,1,0:T(8,128)(2,1)} %get-tuple-element.8), calls=%async_computation | async-start | bytes 1114112 | tf_op jit(solution)/shard_map/all_to_all | solution.py:294
  10.1 18.9 %collective-permute-start.3 = (bf16[136,256]{1,0:T(8,128)(2,1)S(1)}, bf16[136,256]{1,0:T(8,128)(2,1)S(1)}, u32[]{:S(2)}, u32[]{:S(2)}) collective-permute-start(bf16[136,256]{1,0:T(8,128)(2,1)S(1)} %copy-done.1), channel_id=1, source_target_pairs={{384,0},{392,8},{400,16},{408,24},{416,32},{424,40},{432,48},{440,... | collective-permute-start | bytes 208904 | tf_op jit(solution)/shard_map/ppermute | solution.py:295
  16.0 13.1 %collective-permute-start.2 = (bf16[136,256]{1,0:T(8,128)(2,1)S(1)}, bf16[136,256]{1,0:T(8,128)(2,1)S(1)}, u32[]{:S(2)}, u32[]{:S(2)}) collective-permute-start(bf16[136,256]{1,0:T(8,128)(2,1)S(1)} %copy-done.1), channel_id=1, source_target_pairs={{256,0},{264,8},{272,16},{280,24},{288,32},{296,40},{304,48},{312,... | collective-permute-start | bytes 208904 | tf_op jit(solution)/shard_map/ppermute | solution.py:295
  24.8 6.0 %collective-permute-start.1 = (bf16[136,256]{1,0:T(8,128)(2,1)S(1)}, bf16[136,256]{1,0:T(8,128)(2,1)S(1)}, u32[]{:S(2)}, u32[]{:S(2)}) collective-permute-start(bf16[136,256]{1,0:T(8,128)(2,1)S(1)} %copy-done.1), channel_id=1, source_target_pairs={{128,0},{136,8},{144,16},{152,24},{160,32},{168,40},{176,48},{184,... | collective-permute-start | bytes 208904 | tf_op jit(solution)/shard_map/ppermute | solution.py:295
  28.2 0.7 copy-start.2
  30.8 14.8 %collective-permute-start.5 = (bf16[4,136,256]{2,1,0:T(8,128)(2,1)S(1)}, bf16[4,136,256]{2,1,0:T(8,128)(2,1)S(1)}, u32[]{:S(2)}, u32[]{:S(2)}) collective-permute-start(bf16[4,136,256]{2,1,0:T(8,128)(2,1)S(1)} %get-tuple-element.19), channel_id=1, source_target_pairs={{6,0},{7,1},{0,2},{1,3},{2,4},{3,5},{4,6},{5,7},{14,8},{15,9},{8,1... | collective-permute-start | bytes 835592 | tf_op jit(solution)/shard_map/ppermute | solution.py:298
  33.9 11.7 %collective-permute-start.4 = (bf16[4,136,256]{2,1,0:T(8,128)(2,1)S(1)}, bf16[4,136,256]{2,1,0:T(8,128)(2,1)S(1)}, u32[]{:S(2)}, u32[]{:S(2)}) collective-permute-start(bf16[4,136,256]{2,1,0:T(8,128)(2,1)S(1)} %get-tuple-element.19), channel_id=1, source_target_pairs={{2,0},{3,1},{4,2},{5,3},{6,4},{7,5},{0,6},{1,7},{10,8},{11,9},{12,... | collective-permute-start | bytes 835592 | tf_op jit(solution)/shard_map/ppermute | solution.py:298
  37.3 9.7 %collective-permute-start.6 = (bf16[4,136,256]{2,1,0:T(8,128)(2,1)S(1)}, bf16[4,136,256]{2,1,0:T(8,128)(2,1)S(1)}, u32[]{:S(2)}, u32[]{:S(2)}) collective-permute-start(bf16[4,136,256]{2,1,0:T(8,128)(2,1)S(1)} %get-tuple-element.19), channel_id=1, source_target_pairs={{4,0},{5,1},{6,2},{7,3},{0,4},{1,5},{2,6},{3,7},{12,8},{13,9},{14,... | collective-permute-start | bytes 835592 | tf_op jit(solution)/shard_map/ppermute | solution.py:298
  40.9 0.7 copy-start.3
  41.8 13.9 %collective-permute-start = (bf16[8,136,256]{2,1,0:T(8,128)(2,1)S(1)}, bf16[8,136,256]{2,1,0:T(8,128)(2,1)S(1)}, u32[]{:S(2)}, u32[]{:S(2)}) collective-permute-start(bf16[8,136,256]{2,1,0:T(8,128)(2,1)S(1)} %all-to-all-done.refs_3_), channel_id=1, source_target_pairs={{0,64},{8,72},{16,80},{24,88},{32,96},{40,104},{48,112},{56,120},{... | collective-permute-start | bytes 1671176 | tf_op jit(solution)/shard_map/ppermute | solution.py:299
  47.1 10.1 %collective-permute-start.8 = (bf16[3,4,136,256]{3,2,1,0:T(8,128)(2,1)S(1)}, bf16[3,4,136,256]{3,2,1,0:T(8,128)(2,1)S(1)}, u32[]{:S(2)}, u32[]{:S(2)}) collective-permute-start(bf16[3,4,136,256]{3,2,1,0:T(8,128)(2,1)S(1)} %pad_maximum_fusion.refs_6_), channel_id=1, source_target_pairs={{0,1},{1,0},{2,3},{3,2},{4,5},{5,4},{6,7},{7,6},{8,9},{9,8},{10,11... | collective-permute-start | bytes 2506760 | tf_op jit(solution)/shard_map/ppermute | solution.py:303
  53.7 3.4 %collective-permute-start.7 = (bf16[1,4,136,256]{3,2,1,0:T(8,128)(2,1)S(1)}, bf16[1,4,136,256]{3,2,1,0:T(8,128)(2,1)S(1)}, u32[]{:S(2)}, u32[]{:S(2)}) collective-permute-start(bf16[1,4,136,256]{3,2,1,0:T(8,128)(2,1)S(1)} %get-tuple-element.20.refs_5_), channel_id=1, source_target_pairs={{0,1},{1,0},{2,3},{3,2},{4,5},{5,4},{6,7},{7,6},{8,9},{9,8},{10,11... | collective-permute-start | bytes 835592 | tf_op jit(solution)/shard_map/ppermute | solution.py:301
  68.5 22.4 %all-to-all-start.1 = ((f32[64,2,128]{2,1,0:T(2,128)}), f32[64,2,128]{2,1,0:T(2,128)S(1)}, u32[]{:S(2)}, u32[]{:S(2)}) async-start(f32[64,2,128]{2,1,0:T(2,128)} %attend.1), calls=%async_computation.1 | async-start | bytes 131072 | tf_op jit(solution)/shard_map/all_to_all | solution.py:331
  90.9 0.6 copy-start
